TPU v7x, 8 devices: a whole 2x2x1 slice. The times are simulated.
8 devices in a mesh: dp: 2 (over z, y), sp: 4 (over x, core).
Axes of the slice: x: 2, y: 2, z: 1, core: 2. Of those that a mesh axis runs over, the one named last changes fastest.
Arguments:
- hidden: bfloat16 [2, 4096, 1024], P('dp', 'sp')
- positions: int32 [2, 4096], P('dp', 'sp')
- grad_out: bfloat16 [2, 4096, 1024], P('dp', 'sp')
- gain_attn: bfloat16 [1024], P(('dp', 'sp'))
- gain_mlp: bfloat16 [1024], P(('dp', 'sp'))
- w_query: bfloat16 [1024, 2048], P(('dp', 'sp'))
- w_key: bfloat16 [1024, 1024], P(('dp', 'sp'))
- w_value: bfloat16 [1024, 1024], P(('dp', 'sp'))
- w_out: bfloat16 [2048, 1024], P(('dp', 'sp'))
- w_gate: bfloat16 [1024, 3072], P(('dp', 'sp'))
- w_up: bfloat16 [1024, 3072], P(('dp', 'sp'))
- w_down: bfloat16 [3072, 1024], P(('dp', 'sp'))
Outputs:
- output 1: bfloat16 [2, 4096, 1024], P('dp', 'sp')
- output 2: bfloat16 [2, 4096, 1024], P('dp', 'sp')
- output 3: float32 [1024], P(('dp', 'sp'))
- output 4: float32 [1024], P(('dp', 'sp'))
- output 5: float32 [1024, 2048], P(('dp', 'sp'))
- output 6: float32 [1024, 1024], P(('dp', 'sp'))
- output 7: float32 [1024, 1024], P(('dp', 'sp'))
- output 8: float32 [2048, 1024], P(('dp', 'sp'))
- output 9: float32 [1024, 3072], P(('dp', 'sp'))
- output 10: float32 [1024, 3072], P(('dp', 'sp'))
- output 11: float32 [3072, 1024], P(('dp', 'sp'))
All inputs are finite; a program needn't handle non-finite values.
Results may differ from a plain program's by a relative error of at most 0.0154287.
Values are sent between devices in bfloat16 or wider.
A program may use at most 1 GiB of HBM per device.

v0:
```python
import math

import jax
import jax.numpy as jnp
from jax import lax
from jax.experimental import pallas as pl
from jax.experimental.pallas import tpu as pltpu
from jax.sharding import PartitionSpec as P


HEAD_DIM = 128
ROPE_BASE = 10000.0
NORM_EPS = 1e-5
ATTN_SCALE = HEAD_DIM ** -0.5
LOG2E = math.log2(math.e)
SCALE2 = ATTN_SCALE * LOG2E
ALL_AXES = ('dp', 'sp')
BLK = 512
QSUB = 256
SEQ = 4096
TOK = 1024
DIM = 1024
HALF = 1536
SEND = 144
CORE_GROUPS = [[0, 2, 4, 6], [1, 3, 5, 7]]
PAIR = 256
TINY = 10 ** 8
SP = 4
PAIRS = 2
GRP = 512
OWN = 384
NEG = -1e30
VMEM_LIMIT = 60 * 1024 * 1024


def dot_nt(left, right):
    return lax.dot_general(left, right, (((1,), (1,)), ((), ())), preferred_element_type=jnp.float32)


def dot_nn(left, right):
    return lax.dot_general(left, right, (((1,), (0,)), ((), ())), preferred_element_type=jnp.float32)


def dot_tn(left, right):
    return lax.dot_general(left, right, (((0,), (0,)), ((), ())), preferred_element_type=jnp.float32)


def params(**kw):
    return pltpu.CompilerParams(vmem_limit_bytes=VMEM_LIMIT, dimension_semantics=('arbitrary',), **kw)


def cost(flops, mib):
    return pl.CostEstimate(flops=flops, bytes_accessed=mib << 20, transcendentals=0)


def pack_kernel(core_ref, wq_ref, wk_ref, wv_ref, w1_ref, w3_ref, g1_ref, g2_ref, all_ref, send_ref, a1_ref, b1_ref, a3_ref, b3_ref):
    for g in range(PAIRS):
        for n in range(SP):
            m = g * 4 + n
            piece = jnp.concatenate([wq_ref[:, m * PAIR:(m + 1) * PAIR], wk_ref[:, m * HEAD_DIM:(m + 1) * HEAD_DIM], wv_ref[:, m * HEAD_DIM:(m + 1) * HEAD_DIM]], axis=1)
            all_ref[:, m * GRP:(m + 1) * GRP] = piece
            send_ref[n * SEND:n * SEND + HEAD_DIM, g * GRP:(g + 1) * GRP] = piece
    tail = jnp.concatenate([g1_ref[...], g2_ref[...], jnp.zeros((1, DIM - PAIR), jnp.bfloat16)], axis=1)
    for n in range(SP):
        send_ref[n * SEND + HEAD_DIM:(n + 1) * SEND, :] = jnp.broadcast_to(tail, (SEND - HEAD_DIM, DIM))
    core = core_ref[0]
    for ref, own_ref, other_ref in ((w1_ref, a1_ref, b1_ref), (w3_ref, a3_ref, b3_ref)):
        for n in range(SP):
            cols = slice(n * OWN, (n + 1) * OWN)
            own_ref[:, cols] = ref[:, pl.ds(pl.multiple_of((n * 2 + core) * OWN, HEAD_DIM), OWN)]
            other_ref[:, cols] = ref[:, pl.ds(pl.multiple_of((n * 2 + 1 - core) * OWN, HEAD_DIM), OWN)]


def pack_call(core_arr, *weights):
    out = lambda *shape: jax.ShapeDtypeStruct(shape, jnp.bfloat16)
    return pl.pallas_call(
        pack_kernel,
        in_specs=[pl.BlockSpec(memory_space=pltpu.SMEM)] + [pl.BlockSpec(memory_space=pltpu.VMEM)] * 7,
        out_shape=[out(HEAD_DIM, SEQ), out(4 * SEND, DIM)] + [out(HEAD_DIM, HALF)] * 4,
        cost_estimate=cost(TINY, 6),
        name='pack',
    )(core_arr, *weights)


def join_kernel(pos_ref, *refs):
    count = len(refs) // 3
    for n in range(count):
        own_ref, got_ref, out_ref = refs[2 * n], refs[2 * n + 1], refs[2 * count + n]
        rows = own_ref.shape[0]
        out_ref[pl.ds(pl.multiple_of(pos_ref[0] * rows, HEAD_DIM), rows), :] = own_ref[...]
        out_ref[pl.ds(pl.multiple_of((1 - pos_ref[0]) * rows, HEAD_DIM), rows), :] = got_ref[...]


def join_call(pos_arr, *pairs):
    flat = [t for pair in pairs for t in pair]
    return pl.pallas_call(
        join_kernel,
        in_specs=[pl.BlockSpec(memory_space=pltpu.SMEM)] + [pl.BlockSpec(memory_space=pltpu.VMEM)] * len(flat),
        out_shape=[jax.ShapeDtypeStruct((2 * a.shape[0], a.shape[1]), a.dtype) for a, _ in pairs],
        cost_estimate=cost(TINY, 4),
        name='join',
    )(pos_arr, *flat)


def join_qkv_kernel(dp_ref, own_ref, got_ref, w_ref, g1_ref, g2_ref):
    for ref, part in ((own_ref, dp_ref[0]), (got_ref, 1 - dp_ref[0])):
        for n in range(SP):
            rows = pl.ds(pl.multiple_of((part * 4 + n) * HEAD_DIM, HEAD_DIM), HEAD_DIM)
            w_ref[rows, :] = ref[n * SEND:n * SEND + HEAD_DIM, :]
            tail = ref[n * SEND + HEAD_DIM:(n + 1) * SEND, 0:PAIR]
            g1_ref[:, rows] = tail[:, 0:HEAD_DIM]
            g2_ref[:, rows] = tail[:, HEAD_DIM:PAIR]


def join_qkv_call(dp_arr, own, got):
    out = lambda rows: jax.ShapeDtypeStruct((rows, DIM), jnp.bfloat16)
    return pl.pallas_call(
        join_qkv_kernel,
        in_specs=[pl.BlockSpec(memory_space=pltpu.SMEM)] + [pl.BlockSpec(memory_space=pltpu.VMEM)] * 2,
        out_shape=[out(DIM), out(SEND - HEAD_DIM), out(SEND - HEAD_DIM)],
        cost_estimate=cost(TINY, 4),
        name='join_qkv',
    )(dp_arr, own, got)


def unpack_qkv_kernel(p0_ref, p1_ref, wq_ref, wk_ref, wv_ref):
    for g, ref in enumerate((p0_ref, p1_ref)):
        for n in range(SP):
            m = g * 4 + n
            total = ref[n] + ref[4 + n]
            wq_ref[:, m * PAIR:(m + 1) * PAIR] = total[:, 0:PAIR]
            wk_ref[:, m * HEAD_DIM:(m + 1) * HEAD_DIM] = total[:, PAIR:OWN]
            wv_ref[:, m * HEAD_DIM:(m + 1) * HEAD_DIM] = total[:, OWN:GRP]


def unpack_qkv_call(p0, p1):
    out = lambda cols: jax.ShapeDtypeStruct((HEAD_DIM, cols), jnp.float32)
    return pl.pallas_call(unpack_qkv_kernel, out_shape=[out(2048), out(DIM), out(DIM)], cost_estimate=cost(TINY, 6), name='unpack_qkv')(p0, p1)


def unpack_cols_kernel(core_ref, own_ref, got_ref, gate_ref, up_ref):
    core = core_ref[0]
    mine = own_ref[pl.ds(pl.multiple_of(core * HEAD_DIM, HEAD_DIM), HEAD_DIM), :]
    for w, ref in enumerate((gate_ref, up_ref)):
        for n in range(SP):
            cols = slice(w * HALF + n * OWN, w * HALF + (n + 1) * OWN)
            ref[:, pl.ds(pl.multiple_of((n * 2 + core) * OWN, HEAD_DIM), OWN)] = mine[:, cols]
            ref[:, pl.ds(pl.multiple_of((n * 2 + 1 - core) * OWN, HEAD_DIM), OWN)] = got_ref[:, cols]


def unpack_cols_call(core_arr, own, got):
    return pl.pallas_call(
        unpack_cols_kernel,
        in_specs=[pl.BlockSpec(memory_space=pltpu.SMEM)] + [pl.BlockSpec(memory_space=pltpu.VMEM)] * 2,
        out_shape=[jax.ShapeDtypeStruct((HEAD_DIM, 2 * HALF), jnp.float32)] * 2,
        cost_estimate=cost(TINY, 4),
        name='unpack_cols',
    )(core_arr, own, got)


def qkv_kernel(sp_ref, xa_ref, xb_ref, g_ref, w_ref, cos_ref, sin_ref, *rest):
    u_ref, q0_ref, k0_ref, v0_ref, q1_ref, k1_ref, v1_ref, x_scr = rest[-8:]
    i = pl.program_id(0)

    @pl.when(i < 2)
    def _():
        x_scr[...] = xa_ref[...]

    @pl.when(i >= 2)
    def _():
        x_scr[...] = xb_ref[...]

    x32 = x_scr[...].astype(jnp.float32)
    inv_rms = lax.rsqrt(jnp.mean(x32 * x32, axis=-1, keepdims=True) + NORM_EPS)
    u = (x32 * inv_rms * g_ref[...].astype(jnp.float32)).astype(jnp.bfloat16)
    u_ref[...] = u
    cos, sin = cos_ref[...], sin_ref[...]

    def rope(t):
        return (t * cos + pltpu.roll(t, 64, 1) * sin).astype(jnp.bfloat16)

    for g, (q_ref, k_ref, v_ref) in enumerate(((q0_ref, k0_ref, v0_ref), (q1_ref, k1_ref, v1_ref))):
        y = dot_nn(u, w_ref[:, g * GRP:(g + 1) * GRP])
        q_ref[:, 0:HEAD_DIM] = rope(y[:, 0:HEAD_DIM])
        q_ref[:, HEAD_DIM:PAIR] = rope(y[:, HEAD_DIM:PAIR])
        k_ref[...] = rope(y[:, PAIR:OWN])
        v_ref[...] = y[:, OWN:GRP].astype(jnp.bfloat16)


def qkv_call(sp_arr, xa, xb, first, gain, w_own, cos, sin, prev):
    place = lambda width: pl.BlockSpec((BLK, width), lambda i, s: ((s[0] ^ (first + i // 2)) * 2 + i % 2, 0))
    local = lambda width: pl.BlockSpec((BLK, width), lambda i, s: (first * 2 + i, 0))
    fixed = lambda shape: pl.BlockSpec(shape, lambda i, s: (0, 0))
    out = lambda width: jax.ShapeDtypeStruct((SEQ, width), jnp.bfloat16)
    xa_spec = pl.BlockSpec((BLK, DIM), lambda i, s: (jnp.minimum(i, 1), 0))
    xb_spec = pl.BlockSpec((BLK, DIM), lambda i, s: (jnp.maximum(i - 2, 0), 0))
    widths = (DIM, PAIR, HEAD_DIM, HEAD_DIM, PAIR, HEAD_DIM, HEAD_DIM)
    return pl.pallas_call(
        qkv_kernel,
        grid_spec=pltpu.PrefetchScalarGridSpec(
            num_scalar_prefetch=1,
            grid=(4,),
            in_specs=[xa_spec, xb_spec, fixed((1, DIM)), fixed((DIM, DIM)), local(HEAD_DIM), local(HEAD_DIM)]
            + [pl.BlockSpec(memory_space=pl.ANY)] * len(prev),
            out_specs=[local(DIM)] + [place(w) for w in widths[1:]],
            scratch_shapes=[pltpu.VMEM((BLK, DIM), jnp.bfloat16)],
        ),
        out_shape=[out(w) for w in widths],
        input_output_aliases={7 + n: n for n in range(len(prev))},
        compiler_params=params(),
        cost_estimate=cost(2 * 2048 * DIM * DIM, 20),
        name='qkv',
    )(sp_arr, xa, xb, gain, w_own, cos, sin, *prev)


def fwd_kernel(q_ref, k_ref, v_ref, o_ref, lse_ref, acc_ref, q_scr):
    i = pl.program_id(0)
    for h in range(PAIRS):
        q_scr[h * BLK:(h + 1) * BLK, :] = q_ref[:, h * HEAD_DIM:(h + 1) * HEAD_DIM]

    chunks = [(h, n) for h in range(PAIRS) for n in range(BLK // QSUB)]

    def step(j, carry, masked):
        start = pl.multiple_of(j * BLK, BLK)
        k = k_ref[pl.ds(start, BLK), :]
        v = v_ref[pl.ds(start, BLK), :]

        def scores(c):
            h, n = chunks[c]
            s = dot_nt(k, q_scr[h * BLK + n * QSUB:h * BLK + (n + 1) * QSUB, :])
            if masked:
                kv_idx = lax.broadcasted_iota(jnp.int32, (BLK, QSUB), 0)
                q_idx = lax.broadcasted_iota(jnp.int32, (BLK, QSUB), 1) + n * QSUB
                s = jnp.where(q_idx >= kv_idx, s, NEG)
            return s

        out = []
        s_next = scores(0)
        for c in range(len(chunks)):
            s = s_next
            if c + 1 < len(chunks):
                s_next = scores(c + 1)
            m, l = carry[c]
            m_new = jnp.maximum(m, jnp.max(s, axis=0, keepdims=True))
            p = jnp.exp2(s * SCALE2 - m_new * SCALE2)
            alpha = jnp.exp2((m - m_new) * SCALE2)
            l_new = alpha * l + jnp.sum(p, axis=0, keepdims=True)
            acc_ref[c] = acc_ref[c] * alpha + dot_tn(v, p.astype(jnp.bfloat16))
            out.append((m_new, l_new))
        return tuple(out)

    acc_ref[...] = jnp.zeros_like(acc_ref)
    init = tuple((jnp.full((1, QSUB), NEG, jnp.float32), jnp.zeros((1, QSUB), jnp.float32)) for _ in chunks)
    carry = lax.fori_loop(0, i, lambda j, c: step(j, c, False), init)
    carry = step(i, carry, True)
    for c, (h, n) in enumerate(chunks):
        m, l = carry[c]
        rows = slice(n * QSUB, (n + 1) * QSUB)
        o_ref[0, rows, h * HEAD_DIM:(h + 1) * HEAD_DIM] = (acc_ref[c] / l).T.astype(jnp.bfloat16)
        lse_ref[h, :, rows] = jnp.broadcast_to(m * SCALE2 + jnp.log2(l), (8, QSUB))


def fwd_call(q, k, v):
    fixed = pl.BlockSpec((SEQ, HEAD_DIM), lambda i: (0, 0))
    per = TOK // BLK
    return pl.pallas_call(
        fwd_kernel,
        grid=(SEQ // BLK,),
        in_specs=[pl.BlockSpec((BLK, PAIR), lambda i: (i, 0)), fixed, fixed],
        out_specs=[pl.BlockSpec((1, BLK, PAIR), lambda i: (i // per, i % per, 0)), pl.BlockSpec((2, 8, BLK), lambda i: (0, 0, i))],
        out_shape=[jax.ShapeDtypeStruct((SEQ // TOK, TOK, PAIR), jnp.bfloat16), jax.ShapeDtypeStruct((2, 8, SEQ), jnp.float32)],
        scratch_shapes=[pltpu.VMEM((2 * BLK // QSUB, HEAD_DIM, QSUB), jnp.float32), pltpu.VMEM((2 * BLK, HEAD_DIM), jnp.bfloat16)],
        compiler_params=params(),
        cost_estimate=cost(24 * 10 ** 9, 8),
        name='attn_fwd',
    )(q, k, v)


def bwd_kernel(sp_ref, q_ref, k_ref, v_ref, o_ref, do_ref, lse_ref, cos_ref, sin_ref, out0_ref, out1_ref, out2_ref, out3_ref, dq_acc, dk_acc, dv_acc, delta):
    j = pl.program_id(0)
    n_blk = SEQ // BLK

    @pl.when(j == 0)
    def _():
        dq_acc[...] = jnp.zeros_like(dq_acc)

        def rows(i, _):
            start = pl.multiple_of(i * BLK, BLK)
            prod = o_ref[pl.ds(start, BLK), :].astype(jnp.float32) * do_ref[pl.ds(start, BLK), :].astype(jnp.float32)
            for h in range(PAIRS):
                tot = jnp.sum(prod[:, h * HEAD_DIM:(h + 1) * HEAD_DIM], axis=1, keepdims=True)
                delta[h, :, pl.ds(start, BLK)] = jnp.broadcast_to(tot, (BLK, HEAD_DIM)).T[0:8, :]
            return 0

        lax.fori_loop(0, n_blk, rows, 0)

    k = k_ref[...]
    v = v_ref[...]
    dk_acc[...] = jnp.zeros_like(dk_acc)
    dv_acc[...] = jnp.zeros_like(dv_acc)

    def step(i, masked):
        start = pl.multiple_of(i * BLK, BLK)
        rows = pl.ds(start, BLK)
        for h in range(PAIRS):
            cols = slice(h * HEAD_DIM, (h + 1) * HEAD_DIM)
            q = q_ref[rows, cols]
            do = do_ref[rows, cols]
            s = dot_nt(k, q)
            p = jnp.exp2(s * SCALE2 - lse_ref[h, 0:1, rows])
            if masked:
                kv_idx = lax.broadcasted_iota(jnp.int32, (BLK, BLK), 0)
                q_idx = lax.broadcasted_iota(jnp.int32, (BLK, BLK), 1)
                p = jnp.where(q_idx >= kv_idx, p, 0.0)
            dp = dot_nt(v, do)
            dv_acc[...] += dot_nn(p.astype(jnp.bfloat16), do)
            ds = (p * (dp - delta[h, 0:1, rows]) * ATTN_SCALE).astype(jnp.bfloat16)
            dk_acc[...] += dot_nn(ds, q)
            dq_acc[rows, cols] += dot_tn(ds, k)

    step(j, True)

    def body(i, _):
        step(i, False)
        return 0

    lax.fori_loop(j + 1, n_blk, body, 0)

    cos, sin = cos_ref[...], sin_ref[...]

    def rope_back(t):
        t = t.astype(jnp.bfloat16).astype(jnp.float32)
        return (t * cos - pltpu.roll(t, 64, 1) * sin).astype(jnp.bfloat16)

    mine = pl.ds(pl.multiple_of(j * BLK, BLK), BLK)
    result = jnp.concatenate(
        [rope_back(dq_acc[mine, h * HEAD_DIM:(h + 1) * HEAD_DIM]) for h in range(PAIRS)] + [rope_back(dk_acc[...]), dv_acc[...].astype(jnp.bfloat16)], axis=1)
    for n, ref in enumerate((out0_ref, out1_ref, out2_ref, out3_ref)):
        @pl.when((j * BLK // TOK) ^ sp_ref[0] == n)
        def _(ref=ref):
            ref[...] = result


def bwd_call(sp_arr, q, k, v, o, do, lse, cos, sin):
    whole = lambda width: pl.BlockSpec((SEQ, width), lambda j, s: (0, 0))
    block = pl.BlockSpec((BLK, HEAD_DIM), lambda j, s: (j, 0))
    per = TOK // BLK
    table = pl.BlockSpec((BLK, HEAD_DIM), lambda j, s: (((j // per) ^ s[0]) * per + j % per, 0))
    piece = lambda n: pl.BlockSpec((BLK, GRP), lambda j, s: (jnp.clip(j - per * (s[0] ^ n), 0, per - 1), 0))
    return pl.pallas_call(
        bwd_kernel,
        grid_spec=pltpu.PrefetchScalarGridSpec(
            num_scalar_prefetch=1,
            grid=(SEQ // BLK,),
            in_specs=[whole(PAIR), block, block, whole(PAIR), whole(PAIR), pl.BlockSpec((2, 8, SEQ), lambda j, s: (0, 0, 0)), table, table],
            out_specs=[piece(n) for n in range(SP)],
            scratch_shapes=[
                pltpu.VMEM((SEQ, PAIR), jnp.float32),
                pltpu.VMEM((BLK, HEAD_DIM), jnp.float32),
                pltpu.VMEM((BLK, HEAD_DIM), jnp.float32),
                pltpu.VMEM((2, 8, SEQ), jnp.float32),
            ],
        ),
        out_shape=[jax.ShapeDtypeStruct((TOK, GRP), jnp.bfloat16)] * 4,
        compiler_params=params(),
        cost_estimate=cost(60 * 10 ** 9, 16),
        name='attn_bwd',
    )(sp_arr, q, k, v, o, do, lse, cos, sin)


def oproj_kernel(a0_ref, a1_ref, w_ref, x_ref, g_ref, h_ref, u_ref):
    total = x_ref[...].astype(jnp.float32)
    for g, a_ref in enumerate((a0_ref, a1_ref)):
        a = jnp.concatenate([a_ref[s] for s in range(SP)], axis=1)
        total += dot_nn(a, w_ref[g * DIM:(g + 1) * DIM, :])
    h = total.astype(jnp.bfloat16)
    h_ref[...] = h
    h32 = h.astype(jnp.float32)
    inv_rms = lax.rsqrt(jnp.mean(h32 * h32, axis=-1, keepdims=True) + NORM_EPS)
    u_ref[...] = (h32 * inv_rms * g_ref[...].astype(jnp.float32)).astype(jnp.bfloat16)


def oproj_call(a0, a1, wo, x, gain):
    blk = PAIR
    row = pl.BlockSpec((blk, DIM), lambda i: (i, 0))
    part = pl.BlockSpec((4, blk, PAIR), lambda i: (0, i, 0))
    return pl.pallas_call(
        oproj_kernel,
        grid=(TOK // blk,),
        in_specs=[part, part, pl.BlockSpec((2048, DIM), lambda i: (0, 0)), row, pl.BlockSpec((1, DIM), lambda i: (0, 0))],
        out_specs=[row, row],
        out_shape=[jax.ShapeDtypeStruct((TOK, DIM), jnp.bfloat16)] * 2,
        compiler_params=params(),
        cost_estimate=cost(2 * TOK * DIM * 2048, 14),
        name='oproj',
    )(a0, a1, wo, x, gain)


def mlp_kernel(u_ref, dy_ref, w1_ref, w3_ref, w2_ref, z_ref, da_ref, dc_ref, y_ref, d_ref):
    u, dy = u_ref[...], dy_ref[...]
    for n in range(HALF // GRP):
        cols = slice(n * GRP, (n + 1) * GRP)
        gate = dot_nn(u, w1_ref[:, cols])
        up = dot_nn(u, w3_ref[:, cols])
        e = dot_nt(dy, w2_ref[cols, :])
        sig = 1.0 / (1.0 + jnp.exp(-gate))
        silu = gate * sig
        z_ref[:, cols] = (silu * up).astype(jnp.bfloat16)
        da_ref[:, cols] = (e * up * sig * (1.0 + gate * (1.0 - sig))).astype(jnp.bfloat16)
        dc_ref[:, cols] = (e * silu).astype(jnp.bfloat16)
    d_ref[...] = dot_nt(da_ref[...], w1_ref[...]) + dot_nt(dc_ref[...], w3_ref[...])
    y_ref[...] = dot_nn(z_ref[...], w2_ref[...])


def mlp_call(u, dy, w1, w3, w2):
    blk = PAIR
    row = lambda width: pl.BlockSpec((blk, width), lambda i: (i, 0))
    fixed = lambda shape: pl.BlockSpec(shape, lambda i: (0, 0))
    return pl.pallas_call(
        mlp_kernel,
        grid=(TOK // blk,),
        in_specs=[row(DIM), row(DIM), fixed((DIM, HALF)), fixed((DIM, HALF)), fixed((HALF, DIM))],
        out_specs=[row(HALF), row(HALF), row(HALF), row(DIM), row(DIM)],
        out_shape=[jax.ShapeDtypeStruct((TOK, HALF), jnp.bfloat16)] * 3 + [jax.ShapeDtypeStruct((TOK, DIM), jnp.float32)] * 2,
        compiler_params=params(),
        cost_estimate=cost(12 * TOK * DIM * HALF, 30),
        name='mlp',
    )(u, dy, w1, w3, w2)


def dw_kernel(la_ref, lb_ref, *refs):
    rights, out_ref = refs[:-1], refs[-1]
    for n in range(len(rights) // 2):
        ra_ref, rb_ref = rights[2 * n], rights[2 * n + 1]
        cols = ra_ref.shape[1]
        out_ref[:, n * cols:(n + 1) * cols] = dot_tn(la_ref[...], ra_ref[...]) + dot_tn(lb_ref[...], rb_ref[...])


def dw_call(la, lb, *rights):
    rows, cols = la.shape[1] // 4, rights[0].shape[1]
    total = cols * len(rights) // 2
    left = pl.BlockSpec((TOK, rows), lambda b: (0, b))
    right = pl.BlockSpec((TOK, cols), lambda b: (0, 0))
    return pl.pallas_call(
        dw_kernel,
        grid=(4,),
        in_specs=[left, left] + [right] * len(rights),
        out_specs=pl.BlockSpec((rows, total), lambda b: (b, 0)),
        out_shape=jax.ShapeDtypeStruct((4 * rows, total), jnp.float32),
        compiler_params=params(),
        cost_estimate=cost(4 * TOK * rows * 4 * total, 20),
        name='dw',
    )(la, lb, *rights)


def dw_qkv_kernel(u_ref, *refs):
    out_ref = refs[-1]
    total = dot_tn(u_ref[0:TOK, :], refs[0][...])
    for n in range(1, 4):
        total += dot_tn(u_ref[n * TOK:(n + 1) * TOK, :], refs[n][...])
    out_ref[...] = total


def dw_qkv_call(u, pieces):
    return pl.pallas_call(
        dw_qkv_kernel,
        grid=(4,),
        in_specs=[pl.BlockSpec((SEQ, PAIR), lambda b: (0, b))] + [pl.BlockSpec((TOK, GRP), lambda b: (0, 0))] * 4,
        out_specs=pl.BlockSpec((PAIR, GRP), lambda b: (b, 0)),
        out_shape=jax.ShapeDtypeStruct((DIM, GRP), jnp.float32),
        compiler_params=params(),
        cost_estimate=cost(2 * SEQ * DIM * GRP, 14),
        name='dw_qkv',
    )(u, *pieces)


def dout_kernel(sp_ref, h0_ref, h1_ref, h2_ref, h3_ref, o0_ref, o1_ref, wa_ref, wb_ref, d0_ref, d1_ref, dwo_ref, scr):
    i = pl.program_id(0)
    for n, ref in enumerate((h0_ref, h1_ref, h2_ref, h3_ref)):
        @pl.when(i // 2 == n)
        def _(ref=ref):
            scr[...] = ref[...]
    dh = scr[...]
    d0_ref[...] = dot_nt(dh, wa_ref[...]).astype(jnp.bfloat16)
    d1_ref[...] = dot_nt(dh, wb_ref[...]).astype(jnp.bfloat16)

    @pl.when(i == 0)
    def _():
        dwo_ref[...] = jnp.zeros_like(dwo_ref)

    dwo_ref[0] += dot_tn(o0_ref[0], dh)
    dwo_ref[1] += dot_tn(o1_ref[0], dh)


def dout_call(sp_arr, dhs, o0, o1, wo):
    src = lambda n: pl.BlockSpec((BLK, DIM), lambda i, s: (jnp.clip(i - 2 * n, 0, 1), 0))
    o_spec = pl.BlockSpec((1, BLK, PAIR), lambda i, s: (s[0] ^ (i // 2), i % 2, 0))
    d_spec = pl.BlockSpec((BLK, PAIR), lambda i, s: ((s[0] ^ (i // 2)) * 2 + i % 2, 0))
    out = jax.ShapeDtypeStruct((SEQ, PAIR), jnp.bfloat16)
    return pl.pallas_call(
        dout_kernel,
        grid_spec=pltpu.PrefetchScalarGridSpec(
            num_scalar_prefetch=1,
            grid=(SEQ // BLK,),
            in_specs=[src(0), src(1), src(2), src(3), o_spec, o_spec,
                      pl.BlockSpec((PAIR, DIM), lambda i, s: (s[0], 0)), pl.BlockSpec((PAIR, DIM), lambda i, s: (4 + s[0], 0))],
            out_specs=[d_spec, d_spec, pl.BlockSpec((2, PAIR, DIM), lambda i, s: (0, 0, 0))],
            scratch_shapes=[pltpu.VMEM((BLK, DIM), jnp.bfloat16)],
        ),
        out_shape=[out, out, jax.ShapeDtypeStruct((2, PAIR, DIM), jnp.float32)],
        compiler_params=params(),
        cost_estimate=cost(4 * SEQ * DIM * GRP, 20),
        name='dout',
    )(sp_arr, *dhs, o0, o1, wo, wo)


def dx_kernel(sp_ref, *refs):
    pieces, (w_ref, x_ref, dr_ref, g_ref, dx_ref, dg_ref) = refs[:8], refs[8:]
    i = pl.program_id(0)
    d_u = jnp.zeros(dr_ref.shape, jnp.float32)
    for n in range(8):
        cols = pl.ds(pl.multiple_of(((n // 4) * 4 + (sp_ref[0] ^ (n % 4))) * GRP, GRP), GRP)
        piece = pieces[n][...]
        d_u += dot_nt(piece, w_ref[:, cols])
    x32 = x_ref[...].astype(jnp.float32)
    inv_rms = lax.rsqrt(jnp.mean(x32 * x32, axis=-1, keepdims=True) + NORM_EPS)
    normed = x32 * inv_rms
    d_normed = d_u * g_ref[...].astype(jnp.float32)
    grad_in = inv_rms * (d_normed - normed * jnp.mean(d_normed * normed, axis=-1, keepdims=True))
    dx_ref[...] = (dr_ref[...] + grad_in).astype(jnp.bfloat16)

    @pl.when(i == 0)
    def _():
        dg_ref[...] = jnp.zeros_like(dg_ref)

    dg_ref[...] += jnp.sum(d_u * normed, axis=0, keepdims=True)


def dx_call(sp_arr, pieces, w_all, x, d_resid, gain):
    blk = PAIR
    row = lambda width: pl.BlockSpec((blk, width), lambda i, s: (i, 0))
    one = pl.BlockSpec((1, DIM), lambda i, s: (0, 0))
    return pl.pallas_call(
        dx_kernel,
        grid_spec=pltpu.PrefetchScalarGridSpec(
            num_scalar_prefetch=1,
            grid=(TOK // blk,),
            in_specs=[row(GRP)] * 8 + [pl.BlockSpec((DIM, SEQ), lambda i, s: (0, 0)), row(DIM), row(DIM), one],
            out_specs=[row(DIM), one],
        ),
        out_shape=[jax.ShapeDtypeStruct((TOK, DIM), jnp.bfloat16), jax.ShapeDtypeStruct((1, DIM), jnp.float32)],
        compiler_params=params(),
        cost_estimate=cost(2 * TOK * DIM * SEQ, 24),
        name='dx',
    )(sp_arr, *pieces, w_all, x, d_resid, gain)


def gather_full(shard):
    return lax.all_gather(shard, ALL_AXES, axis=0, tiled=True)


def gather_core(shard):
    return lax.all_gather(shard, ALL_AXES, axis=0, tiled=True, axis_index_groups=CORE_GROUPS)


def swap_seq(parts):
    return lax.all_to_all(parts, 'sp', 0, 0, tiled=True)


def swap_all(parts):
    return lax.all_to_all(parts, ALL_AXES, 0, 0, tiled=True)


def from_sp(value, bits):
    return lax.ppermute(value, 'sp', [(s, s ^ bits) for s in range(SP)])


def from_dp(value):
    return lax.ppermute(value, 'dp', [(0, 1), (1, 0)])


def gather_chip_then_core(value):
    far = from_sp(value, 2)
    return value, from_sp(value, 1), far, from_sp(far, 1)


def reduce_chips(part):
    return lax.psum_scatter(part, ALL_AXES, scatter_dimension=0, tiled=True, axis_index_groups=CORE_GROUPS)


def layer_step(hidden, positions, grad_out, gain_attn, gain_mlp, w_query, w_key, w_value, w_out, w_gate, w_up, w_down):
    tokens = hidden[0]
    d_layer = grad_out[0]
    dp = lax.axis_index('dp')
    sp = lax.axis_index('sp')
    core = sp % 2
    f32, bf16 = jnp.float32, jnp.bfloat16
    sp_arr, dp_arr, core_arr = (t.astype(jnp.int32)[None] for t in (sp, dp, core))

    xs = gather_chip_then_core(tokens)
    w_cols, w_send, a1, b1, a3, b3 = pack_call(core_arr, w_query, w_key, w_value, w_gate, w_up, gain_attn[None], gain_mlp[None])
    w_mine = swap_seq(w_send)
    w_own, gain1, gain2 = join_qkv_call(dp_arr, w_mine, from_dp(w_mine))
    gain1, gain2 = gain1[0:1], gain2[0:1]
    pos = gather_chip_then_core(positions[0].reshape(8, HEAD_DIM))
    pos_all = jnp.concatenate(pos).reshape(SEQ)
    w1_rows, w3_rows = join_call(core_arr, (a1, from_sp(b1, 1)), (a3, from_sp(b3, 1)))
    wo_full = gather_full(w_out)
    w2 = gather_core(w_down)
    w1, w3 = gather_core(w1_rows), gather_core(w3_rows)
    w_all = gather_full(w_cols)
    dy_pair = from_sp(d_layer, 1)

    lane = jnp.arange(HEAD_DIM)
    half = HEAD_DIM // 2
    inv_freq = ROPE_BASE ** (-((lane % half).astype(f32) * (2.0 / HEAD_DIM)))
    angles = pos_all.astype(f32)[:, None] * inv_freq
    cos = jnp.cos(angles)
    sin = jnp.sin(angles) * jnp.where(lane < half, -1.0, 1.0)

    near = qkv_call(sp_arr, xs[0], xs[1], 0, gain1, w_own, cos, sin, ())
    u_all, q0, k0, v0, q1, k1, v1 = qkv_call(sp_arr, xs[2], xs[3], 2, gain1, w_own, cos, sin, near)
    o0, lse0 = fwd_call(q0, k0, v0)
    got0 = swap_seq(o0)
    o1, lse1 = fwd_call(q1, k1, v1)
    got1 = swap_seq(o1)
    residual, u_mlp = oproj_call(got0, got1, wo_full, tokens, gain2)

    u_pair = from_sp(u_mlp, 1)
    z_a, da_a, dc_a, y_a, d_a = mlp_call(u_mlp, d_layer, w1, w3, w2)
    z_b, da_b, dc_b, y_b, d_b = mlp_call(u_pair, dy_pair, w1, w3, w2)
    d_umlp = d_a + from_sp(d_b, 1)
    h32 = residual.astype(f32)
    layer_out = (h32 + (y_a + from_sp(y_b, 1))).astype(bf16)
    inv_rms2 = lax.rsqrt(jnp.mean(h32 * h32, axis=-1, keepdims=True) + NORM_EPS)
    normed2 = h32 * inv_rms2
    d_normed2 = d_umlp * gain2.astype(f32)
    d_gain2 = jnp.sum(d_umlp * normed2, axis=0)
    d_resid = d_layer.astype(f32) + inv_rms2 * (d_normed2 - normed2 * jnp.mean(d_normed2 * normed2, axis=-1, keepdims=True))
    dhs = gather_chip_then_core(d_resid.astype(bf16))
    grad_w_down = reduce_chips(dw_call(z_a, z_b, d_layer, dy_pair))

    part = reduce_chips(dw_call(u_mlp, u_pair, da_a, da_b, dc_a, dc_b))

    do0, do1, dwo = dout_call(sp_arr, dhs, o0, o1, wo_full)
    o_seq = (o0.reshape(SEQ, PAIR), o1.reshape(SEQ, PAIR))
    d0 = bwd_call(sp_arr, q0, k0, v0, o_seq[0], do0, lse0, cos, sin)
    back0 = [d0[0]] + [from_sp(d0[n], n) for n in (2, 3, 1)]
    part0 = dw_qkv_call(u_all, d0).reshape(8, HEAD_DIM, GRP)
    dw0 = swap_all(part0)
    d1 = bwd_call(sp_arr, q1, k1, v1, o_seq[1], do1, lse1, cos, sin)
    back1 = [d1[0]] + [from_sp(d1[n], n) for n in (2, 3, 1)]
    part1 = dw_qkv_call(u_all, d1).reshape(8, HEAD_DIM, GRP)
    part1, _ = lax.optimization_barrier((part1, dw0))
    dw1 = swap_all(part1)
    pieces = [t[n] for t in (back0, back1) for n in (0, 3, 1, 2)]

    grad_w_out = lax.dynamic_index_in_dim(dwo, dp, 0, keepdims=False) + from_dp(lax.dynamic_index_in_dim(dwo, 1 - dp, 0, keepdims=False))
    grad_w_query, grad_w_key, grad_w_value = unpack_qkv_call(dw0, dw1)

    grad_hidden, d_gain1 = dx_call(sp_arr, pieces, w_all, tokens, d_resid, gain1)
    part, _ = lax.optimization_barrier((part, d_gain1))
    send = lax.dynamic_slice(part, ((1 - core) * HEAD_DIM, 0), (HEAD_DIM, 2 * HALF))
    grad_w_gate, grad_w_up = unpack_cols_call(core_arr, part, from_sp(send, 1))
    gain_parts = jnp.stack([d_gain1.reshape(8, HEAD_DIM), d_gain2.reshape(8, HEAD_DIM)], axis=1)
    gain_parts, _ = lax.optimization_barrier((gain_parts, dw1))
    gain_sums = jnp.sum(swap_all(gain_parts), axis=0)
    return (layer_out[None], grad_hidden[None], gain_sums[0], gain_sums[1], grad_w_query, grad_w_key, grad_w_value,
            grad_w_out, grad_w_gate, grad_w_up, grad_w_down)


def solution(mesh):
    act_spec = P('dp', 'sp', None)
    pos_spec = P('dp', 'sp')
    vec_spec = P(ALL_AXES)
    mat_spec = P(ALL_AXES, None)
    in_specs = (act_spec, pos_spec, act_spec, vec_spec, vec_spec) + (mat_spec,) * 7
    out_specs = (act_spec, act_spec, vec_spec, vec_spec) + (mat_spec,) * 7

    return jax.shard_map(layer_step, mesh=mesh, in_specs=in_specs, out_specs=out_specs, check_vma=False)
```

profile of v0, /device:TPU:0, one launch (start us, length us, event | category | flops | bytes accessed | tf_op | source)
XLA Modules:
  0.0 822.3 jit_solution(10086961576378433820)
XLA Ops:
  26.6 66.9 %collective-permute-done.xa_ref = bf16[1024,1024]{1,0:T(8,128)(2,1)S(1)} collective-permute-done((bf16[1024,1024]{1,0:T(8,128)(2,1)}, bf16[1024,1024]{1,0:T(8,128)(2,1)S(1)}, u32[]{:S(2)}, u32[]{:S(2)}) %collective-permute-start) | collective-permute-done | bytes 2097184 | tf_op jit(solution)/shard_map/ppermute | solution.py:575
  94.5 24.3 %collective-permute-done.4 = s32[8,128]{1,0:T(8,128)S(1)} collective-permute-done((s32[8,128]{1,0:T(8,128)S(1)}, s32[8,128]{1,0:T(8,128)S(1)}, u32[]{:S(2)}, u32[]{:S(2)}) %collective-permute-start.4) | collective-permute-done | bytes 4128 | tf_op jit(solution)/shard_map/ppermute | solution.py:575
  120.4 9.4 %fusion.10 = (f32[4096,128]{1,0:T(8,128)}, f32[4096,128]{1,0:T(8,128)}) fusion(f32[128]{0:T(128)S(1)} %get-tuple-element.146, f32[128]{0:T(128)S(1)} %get-tuple-element.147, f32[4096]{0:T(1024)S(1)} %fusion.12), kind=kLoop, calls=%fused_computation.15 | loop fusion | flops 1048576 | bytes 4211712 | tf_op jit(solution)/shard_map/mul | solution.py:619
  129.8 30.6 %collective-permute-done.2.got_ref = bf16[576,1024]{1,0:T(8,128)(2,1)} collective-permute-done((bf16[576,1024]{1,0:T(8,128)(2,1)S(1)}, bf16[576,1024]{1,0:T(8,128)(2,1)}, u32[]{:S(2)}, u32[]{:S(2)}) %collective-permute-start.2) | collective-permute-done | bytes 1179680 | tf_op jit(solution)/shard_map/ppermute | solution.py:579
  164.8 10.3 %qkv.2 = (bf16[4096,1024]{1,0:T(8,128)(2,1)}, bf16[4096,256]{1,0:T(8,128)(2,1)}, bf16[4096,128]{1,0:T(8,128)(2,1)}, bf16[4096,128]{1,0:T(8,128)(2,1)}, bf16[4096...) custom-call(s32[1]{0:T(128)} %bitcast.sp_ref, bf16[1024,1024]{1,0:T(8,128)(2,1)} %bitcast.55, ...), custom_call_target="tpu_custom_call" | custom-call | flops 4294967296 | bytes 20971520 | tf_op jit(solution)/shard_map/qkv/pallas_call | solution.py:198
  175.1 10.3 %qkv.3 = (bf16[4096,1024]{1,0:T(8,128)(2,1)}, bf16[4096,256]{1,0:T(8,128)(2,1)}, bf16[4096,128]{1,0:T(8,128)(2,1)}, bf16[4096,128]{1,0:T(8,128)(2,1)}, bf16[4096...) custom-call(s32[1]{0:T(128)} %bitcast.sp_ref, ...), custom_call_target="tpu_custom_call", output_to_operand_aliasing={{0}: (7, {}), {1}: (8, {}), {2}: (9, {}), {3}: (10, {}), {4... | custom-call | flops 4294967296 | bytes 20971520 | tf_op jit(solution)/shard_map/qkv/pallas_call | solution.py:198
  185.4 46.4 %attn_fwd.3 = (bf16[4,1024,256]{2,1,0:T(8,128)(2,1)}, f32[2,8,4096]{2,1,0:T(8,128)}) custom-call(bf16[4096,256]{1,0:T(8,128)(2,1)} %get-tuple-element.87.q_ref, bf16[4096,128]{1,0:T(8,128)(2,1)} %get-tuple-element.88.k_ref, bf16[4096,128]{1,0:T(8,128)(2,1)} %get-tuple-element.89.v_ref), custom_call_target="tpu_custom_call" | custom-call | flops 24000000000 | bytes 8388608 | tf_op jit(solution)/shard_map/attn_fwd/pallas_call | solution.py:266
  235.4 46.4 %attn_fwd.2 = (bf16[4,1024,256]{2,1,0:T(8,128)(2,1)}, f32[2,8,4096]{2,1,0:T(8,128)}) custom-call(bf16[4096,256]{1,0:T(8,128)(2,1)} %get-tuple-element.83.q_ref, bf16[4096,128]{1,0:T(8,128)(2,1)} %get-tuple-element.84.k_ref, bf16[4096,128]{1,0:T(8,128)(2,1)} %get-tuple-element.85.v_ref), custom_call_target="tpu_custom_call" | custom-call | flops 24000000000 | bytes 8388608 | tf_op jit(solution)/shard_map/attn_fwd/pallas_call | solution.py:266
  290.9 23.7 %all-to-all-done.1.a0_ref = bf16[4,1024,256]{2,1,0:T(8,128)(2,1)} async-done(((bf16[4,1024,256]{2,1,0:T(8,128)(2,1)}), bf16[4,1024,256]{2,1,0:T(8,128)(2,1)}, u32[]{:S(2)}, u32[]{:S(2)}) %all-to-all-start.1) | async-done | bytes 2097184 | tf_op jit(solution)/shard_map/all_to_all | solution.py:567
  314.7 9.5 %oproj.1 = (bf16[1024,1024]{1,0:T(8,128)(2,1)}, bf16[1024,1024]{1,0:T(8,128)(2,1)}) custom-call(bf16[4,1024,256]{2,1,0:T(8,128)(2,1)} %all-to-all-done.1.a0_ref, bf16[4,1024,256]{2,1,0:T(8,128)(2,1)} %copy-done.9, bf16[2048,1024]{1,0:T(8,128)(2,1)} %all-gather.6.cloned.1.call-done.w_ref.wa_ref.wb_ref, bf16[1024,1024]{1,0:T(8,128)(2,1)} %bitcast.56, ...), custom_call_target="tpu_custom_call" | custom-call | flops 4294967296 | bytes 14680064 | tf_op jit(solution)/shard_map/oproj/pallas_call | solution.py:387
  324.2 26.7 %mlp.2 = (bf16[1024,1536]{1,0:T(8,128)(2,1)}, bf16[1024,1536]{1,0:T(8,128)(2,1)}, bf16[1024,1536]{1,0:T(8,128)(2,1)}, f32[1024,1024]{1,0:T(8,128)}, f32[1024,1024]{1,0:T(8,128)}) custom-call(bf16[1024,1024]{1,0:T(8,128)(2,1)} %get-tuple-element.93.u_ref.la_ref, bf16[1024,1024]{1,0:T(8,128)(2,1)} %bitcast.36, ...), custom_call_target="tpu_custom_call" | custom-call | flops 19327352832 | bytes 31457280 | tf_op jit(solution)/shard_map/mlp/pallas_call | solution.py:419
  351.0 26.7 %mlp.3 = (bf16[1024,1536]{1,0:T(8,128)(2,1)}, bf16[1024,1536]{1,0:T(8,128)(2,1)}, bf16[1024,1536]{1,0:T(8,128)(2,1)}, f32[1024,1024]{1,0:T(8,128)}, f32[1024,1024]{1,0:T(8,128)}) custom-call(bf16[1024,1024]{1,0:T(8,128)(2,1)} %collective-permute-done.9.u_ref.lb_ref, bf16[1024,1024]{1,0:T(8,128)(2,1)} %collective-permute-done.10.dy_ref.refs_1_, ...), custom_call_target="tpu_custom_call" | custom-call | flops 19327352832 | bytes 31457280 | tf_op jit(solution)/shard_map/mlp/pallas_call | solution.py:419
  377.6 20.6 %dw.2 = f32[1024,3072]{1,0:T(8,128)} custom-call(bf16[1024,1024]{1,0:T(8,128)(2,1)} %get-tuple-element.93.u_ref.la_ref, bf16[1024,1024]{1,0:T(8,128)(2,1)} %collective-permute-done.9.u_ref.lb_ref, bf16[1024,1536]{1,0:T(8,128)(2,1)} %get-tuple-element.126.refs_0_, bf16[1024,1536]{1,0:T(8,128)(2,1)} %get-tuple-element.127.refs_1_, ...), custom_call_target="tpu_custom_call" | custom-call | flops 12884901888 | bytes 20971520 | tf_op jit(solution)/shard_map/dw/pallas_call | solution.py:444
  416.7 93.0 %collective-permute-done.14.h2_ref = bf16[1024,1024]{1,0:T(8,128)(2,1)S(1)} collective-permute-done((bf16[1024,1024]{1,0:T(8,128)(2,1)}, bf16[1024,1024]{1,0:T(8,128)(2,1)S(1)}, u32[]{:S(2)}, u32[]{:S(2)}) %collective-permute-start.14) | collective-permute-done | bytes 2097184 | tf_op jit(solution)/shard_map/ppermute | solution.py:575
  509.7 12.2 %dw.3 = f32[1536,1024]{1,0:T(8,128)} custom-call(bf16[1024,1536]{1,0:T(8,128)(2,1)} %get-tuple-element.133.la_ref, bf16[1024,1536]{1,0:T(8,128)(2,1)} %get-tuple-element.134.lb_ref, bf16[1024,1024]{1,0:T(8,128)(2,1)} %bitcast.37, bf16[1024,1024]{1,0:T(8,128)(2,1)} %collective-permute-done.10.dy_ref.refs_1_), custom_call_target="tpu_custom_call" | custom-call | flops 6442450944 | bytes 20971520 | tf_op jit(solution)/shard_map/dw/pallas_call | solution.py:444
  522.0 18.4 %dout.1 = (bf16[4096,256]{1,0:T(8,128)(2,1)}, bf16[4096,256]{1,0:T(8,128)(2,1)}, f32[2,256,1024]{2,1,0:T(8,128)}) custom-call(s32[1]{0:T(128)} %bitcast.sp_ref, bf16[1024,1024]{1,0:T(8,128)(2,1)} %get-tuple-element.137.h0_ref, bf16[1024,1024]{1,0:T(8,128)(2,1)} %collective-permute-done.13.h1_ref, bf16[1024,1024]{1,0:T(8,128)(2,1)} %copy-done.15, ...), custom_call_target="tpu_custom_call" | custom-call | flops 8589934592 | bytes 20971520 | tf_op jit(solution)/shard_map/dout/pallas_call | solution.py:500
  540.4 66.9 %attn_bwd.3 = (bf16[1024,512]{1,0:T(8,128)(2,1)}, bf16[1024,512]{1,0:T(8,128)(2,1)}, bf16[1024,512]{1,0:T(8,128)(2,1)}, bf16[1024,512]{1,0:T(8,128)(2,1)}) custom-call(s32[1]{0:T(128)} %bitcast.sp_ref, bf16[4096,256]{1,0:T(8,128)(2,1)} %get-tuple-element.87.q_ref, bf16[4096,128]{1,0:T(8,128)(2,1)} %get-tuple-element.88.k_ref, ...), custom_call_target="tpu_custom_call" | custom-call | flops 60000002048 | bytes 16777216 | tf_op jit(solution)/shard_map/attn_bwd/pallas_call | solution.py:350
  609.1 66.6 %attn_bwd.2 = (bf16[1024,512]{1,0:T(8,128)(2,1)}, bf16[1024,512]{1,0:T(8,128)(2,1)}, bf16[1024,512]{1,0:T(8,128)(2,1)}, bf16[1024,512]{1,0:T(8,128)(2,1)}) custom-call(s32[1]{0:T(128)} %bitcast.sp_ref, bf16[4096,256]{1,0:T(8,128)(2,1)} %get-tuple-element.83.q_ref, bf16[4096,128]{1,0:T(8,128)(2,1)} %get-tuple-element.84.k_ref, ...), custom_call_target="tpu_custom_call" | custom-call | flops 60000002048 | bytes 16777216 | tf_op jit(solution)/shard_map/attn_bwd/pallas_call | solution.py:350
  677.8 9.6 %dw_qkv.3 = f32[1024,512]{1,0:T(8,128)} custom-call(bf16[4096,1024]{1,0:T(8,128)(2,1)} %get-tuple-element.119.u_ref, bf16[1024,512]{1,0:T(8,128)(2,1)} %get-tuple-element.106.refs_0_, bf16[1024,512]{1,0:T(8,128)(2,1)} %get-tuple-element.107.refs_1_, bf16[1024,512]{1,0:T(8,128)(2,1)} %get-tuple-element.108.refs_2_, bf16[1024,512]{1,0:T(8,128)(2,1)} %get-tuple-element.109.refs_3_), custom_call_target="tpu_custom_call" | custom-call | flops 4294967296 | bytes 14680064 | tf_op jit(solution)/shard_map/dw_qkv/pallas_call | solution.py:465
  690.6 9.4 %dw_qkv.2 = f32[1024,512]{1,0:T(8,128)} custom-call(bf16[4096,1024]{1,0:T(8,128)(2,1)} %get-tuple-element.119.u_ref, bf16[1024,512]{1,0:T(8,128)(2,1)} %get-tuple-element.112.refs_4_.refs_0_, bf16[1024,512]{1,0:T(8,128)(2,1)} %get-tuple-element.113.refs_1_, bf16[1024,512]{1,0:T(8,128)(2,1)} %get-tuple-element.114.refs_2_, ...), custom_call_target="tpu_custom_call" | custom-call | flops 4294967296 | bytes 14680064 | tf_op jit(solution)/shard_map/dw_qkv/pallas_call | solution.py:465
  702.8 20.6 %collective-permute-done.18.refs_3_ = bf16[1024,512]{1,0:T(8,128)(2,1)} collective-permute-done((bf16[1024,512]{1,0:T(8,128)(2,1)}, bf16[1024,512]{1,0:T(8,128)(2,1)}, u32[]{:S(2)}, u32[]{:S(2)}) %collective-permute-start.18) | collective-permute-done | bytes 1048608 | tf_op jit(solution)/shard_map/ppermute | solution.py:575
  723.4 16.7 %dx.1 = (bf16[1024,1024]{1,0:T(8,128)(2,1)}, f32[1,1024]{1,0:T(1,128)}) custom-call(s32[1]{0:T(128)} %bitcast.sp_ref, bf16[1024,512]{1,0:T(8,128)(2,1)} %get-tuple-element.106.refs_0_, bf16[1024,512]{1,0:T(8,128)(2,1)} %collective-permute-done.16.refs_1_, bf16[1024,512]{1,0:T(8,128)(2,1)} %collective-permute-done.17.refs_2_, ...), custom_call_target="tpu_custom_call" | custom-call | flops 8589934592 | bytes 25165824 | tf_op jit(solution)/shard_map/dx/pallas_call | solution.py:543
  740.1 8.6 %all-to-all-done.3.p0_ref = f32[8,128,512]{2,1,0:T(8,128)S(1)} async-done(((f32[8,128,512]{2,1,0:T(8,128)}), f32[8,128,512]{2,1,0:T(8,128)S(1)}, u32[]{:S(2)}, u32[]{:S(2)}) %all-to-all-start.3) | async-done | bytes 2097184 | tf_op jit(solution)/shard_map/all_to_all | solution.py:571
  758.7 42.5 %collective-permute-done.22 = f32[256,1024]{1,0:T(8,128)} collective-permute-done((f32[256,1024]{1,0:T(8,128)S(1)}, f32[256,1024]{1,0:T(8,128)}, u32[]{:S(2)}, u32[]{:S(2)}) %collective-permute-start.22) | collective-permute-done | bytes 1048608 | tf_op jit(solution)/shard_map/ppermute | solution.py:579
  (127 shorter events, 91.1 us)
Async XLA Ops:
  7.2 307.5 %all-gather.6.cloned.1.call-start = ((), (), s32[]{:S(2)}) async-start(), calls=%async_computation.8 | async-start | bytes 4718592 | tf_op jit(solution)/shard_map/all_gather | solution.py:559
  7.9 316.3 %all-gather.12.cloned.1.call-start = ((), (), s32[]{:S(2)}) async-start(), calls=%async_computation.11 | async-start | bytes 3932160 | tf_op jit(solution)/shard_map/all_gather | solution.py:563
  8.7 315.6 %all-gather.10.cloned.1.call-start = ((), (), s32[]{:S(2)}) async-start(), calls=%async_computation.10 | async-start | bytes 3932160 | tf_op jit(solution)/shard_map/all_gather | solution.py:563
  19.1 305.1 %all-gather.8.cloned.1.call-start = ((), (), s32[]{:S(2)}) async-start(), calls=%async_computation.9 | async-start | bytes 3932160 | tf_op jit(solution)/shard_map/all_gather | solution.py:563
  19.7 680.3 %all-gather.14.cloned.1.call-start = ((), (), s32[]{:S(2)}) async-start(), calls=%async_computation.12 | async-start | bytes 9437184 | tf_op jit(solution)/shard_map/all_gather | solution.py:559
  19.7 73.7 %collective-permute-start = (bf16[1024,1024]{1,0:T(8,128)(2,1)}, bf16[1024,1024]{1,0:T(8,128)(2,1)S(1)}, u32[]{:S(2)}, u32[]{:S(2)}) collective-permute-start(bf16[1024,1024]{1,0:T(8,128)(2,1)} %bitcast.53), channel_id=1, source_target_pairs={{0,2},{1,3},{2,0},{3,1},{4,6},{5,7},{6,4},{7,5}} | collective-permute-start | bytes 6291464 | tf_op jit(solution)/shard_map/ppermute | solution.py:575
  22.6 96.2 %all-to-all-start = ((bf16[4,144,1024]{2,1,0:T(8,128)(2,1)}), bf16[4,144,1024]{2,1,0:T(8,128)(2,1)S(1)}, u32[]{:S(2)}, u32[]{:S(2)}) async-start(bf16[4,144,1024]{2,1,0:T(8,128)(2,1)} %bitcast.43), calls=%async_computation | async-start | bytes 2359296 | tf_op jit(solution)/shard_map/all_to_all | solution.py:567
  26.1 138.7 %collective-permute-start.6 = (bf16[1024,1024]{1,0:T(8,128)(2,1)}, bf16[1024,1024]{1,0:T(8,128)(2,1)}, u32[]{:S(2)}, u32[]{:S(2)}) collective-permute-start(bf16[1024,1024]{1,0:T(8,128)(2,1)} %bitcast.54), channel_id=1, source_target_pairs={{0,1},{1,0},{2,3},{3,2},{4,5},{5,4},{6,7},{7,6}} | collective-permute-start | bytes 6291464 | tf_op jit(solution)/shard_map/ppermute | solution.py:575
  93.5 81.6 %collective-permute-start.1 = (bf16[1024,1024]{1,0:T(8,128)(2,1)S(1)}, bf16[1024,1024]{1,0:T(8,128)(2,1)}, u32[]{:S(2)}, u32[]{:S(2)}) collective-permute-start(bf16[1024,1024]{1,0:T(8,128)(2,1)S(1)} %collective-permute-done.xa_ref), channel_id=1, source_target_pairs={{0,1},{1,0},{2,3},{3,2},{4,5},{5,4},{6,7},{7,6}} | collective-permute-start | bytes 6291464 | tf_op jit(solution)/shard_map/ppermute | solution.py:575
  118.8 41.6 %collective-permute-start.2 = (bf16[576,1024]{1,0:T(8,128)(2,1)S(1)}, bf16[576,1024]{1,0:T(8,128)(2,1)}, u32[]{:S(2)}, u32[]{:S(2)}) collective-permute-start(bf16[576,1024]{1,0:T(8,128)(2,1)S(1)} %bitcast.34), channel_id=1, source_target_pairs={{0,4},{4,0},{1,5},{5,1},{2,6},{6,2},{3,7},{7,3}} | collective-permute-start | bytes 3538952 | tf_op jit(solution)/shard_map/ppermute | solution.py:579
  231.8 51.2 %all-to-all-start.2 = ((bf16[4,1024,256]{2,1,0:T(8,128)(2,1)}), bf16[4,1024,256]{2,1,0:T(8,128)(2,1)S(1)}, u32[]{:S(2)}, u32[]{:S(2)}) async-start(bf16[4,1024,256]{2,1,0:T(8,128)(2,1)} %get-tuple-element.90.o1_ref), calls=%async_computation.2 | async-start | bytes 4194304 | tf_op jit(solution)/shard_map/all_to_all | solution.py:567
  288.9 464.2 %reduce-scatter.3.cloned.1.call-start = ((), (), s32[]{:S(2)}) async-start(), calls=%async_computation.13 | async-start | bytes 15728640 | tf_op jit(solution)/shard_map/reduce_scatter | solution.py:588
  289.2 61.8 %collective-permute-start.10 = (bf16[1024,1024]{1,0:T(8,128)(2,1)S(1)}, bf16[1024,1024]{1,0:T(8,128)(2,1)}, u32[]{:S(2)}, u32[]{:S(2)}) collective-permute-start(bf16[1024,1024]{1,0:T(8,128)(2,1)S(1)} %bitcast.38), channel_id=1, source_target_pairs={{0,1},{1,0},{2,3},{3,2},{4,5},{5,4},{6,7},{7,6}} | collective-permute-start | bytes 6291464 | tf_op jit(solution)/shard_map/ppermute | solution.py:575
  398.3 416.8 %reduce-scatter.5.cloned.1.call-start = ((), (), s32[]{:S(2)}) async-start(), calls=%async_computation.14 | async-start | bytes 7864320 | tf_op jit(solution)/shard_map/reduce_scatter | solution.py:588
  416.2 93.5 %collective-permute-start.14 = (bf16[1024,1024]{1,0:T(8,128)(2,1)}, bf16[1024,1024]{1,0:T(8,128)(2,1)S(1)}, u32[]{:S(2)}, u32[]{:S(2)}) collective-permute-start(bf16[1024,1024]{1,0:T(8,128)(2,1)} %get-tuple-element.137.h0_ref), channel_id=1, source_target_pairs={{0,2},{1,3},{2,0},{3,1},{4,6},{5,7},{6,4},{7,5}} | collective-permute-start | bytes 6291464 | tf_op jit(solution)/shard_map/ppermute | solution.py:575
  416.6 105.3 %collective-permute-start.13 = (bf16[1024,1024]{1,0:T(8,128)(2,1)}, bf16[1024,1024]{1,0:T(8,128)(2,1)}, u32[]{:S(2)}, u32[]{:S(2)}) collective-permute-start(bf16[1024,1024]{1,0:T(8,128)(2,1)} %get-tuple-element.137.h0_ref), channel_id=1, source_target_pairs={{0,1},{1,0},{2,3},{3,2},{4,5},{5,4},{6,7},{7,6}} | collective-permute-start | bytes 6291464 | tf_op jit(solution)/shard_map/ppermute | solution.py:575
  607.3 69.2 %collective-permute-start.19 = (bf16[1024,512]{1,0:T(8,128)(2,1)}, bf16[1024,512]{1,0:T(8,128)(2,1)S(1)}, u32[]{:S(2)}, u32[]{:S(2)}) collective-permute-start(bf16[1024,512]{1,0:T(8,128)(2,1)} %get-tuple-element.113.refs_1_), channel_id=1, source_target_pairs={{0,1},{1,0},{2,3},{3,2},{4,5},{5,4},{6,7},{7,6}} | collective-permute-start | bytes 3145736 | tf_op jit(solution)/shard_map/ppermute | solution.py:575
  607.7 92.3 %collective-permute-start.20 = (bf16[1024,512]{1,0:T(8,128)(2,1)}, bf16[1024,512]{1,0:T(8,128)(2,1)}, u32[]{:S(2)}, u32[]{:S(2)}) collective-permute-start(bf16[1024,512]{1,0:T(8,128)(2,1)} %get-tuple-element.114.refs_2_), channel_id=1, source_target_pairs={{0,2},{1,3},{2,0},{3,1},{4,6},{5,7},{6,4},{7,5}} | collective-permute-start | bytes 3145736 | tf_op jit(solution)/shard_map/ppermute | solution.py:575
  607.7 92.3 %collective-permute-start.21 = (bf16[1024,512]{1,0:T(8,128)(2,1)}, bf16[1024,512]{1,0:T(8,128)(2,1)}, u32[]{:S(2)}, u32[]{:S(2)}) collective-permute-start(bf16[1024,512]{1,0:T(8,128)(2,1)} %get-tuple-element.115.refs_3_), channel_id=1, source_target_pairs={{0,3},{1,2},{2,1},{3,0},{4,7},{5,6},{6,5},{7,4}} | collective-permute-start | bytes 3145736 | tf_op jit(solution)/shard_map/ppermute | solution.py:575
  676.5 46.9 %collective-permute-start.18 = (bf16[1024,512]{1,0:T(8,128)(2,1)}, bf16[1024,512]{1,0:T(8,128)(2,1)}, u32[]{:S(2)}, u32[]{:S(2)}) collective-permute-start(bf16[1024,512]{1,0:T(8,128)(2,1)} %get-tuple-element.109.refs_3_), channel_id=1, source_target_pairs={{0,3},{1,2},{2,1},{3,0},{4,7},{5,6},{6,5},{7,4}} | collective-permute-start | bytes 3145736 | tf_op jit(solution)/shard_map/ppermute | solution.py:575
  687.5 61.2 %all-to-all-start.3 = ((f32[8,128,512]{2,1,0:T(8,128)}), f32[8,128,512]{2,1,0:T(8,128)S(1)}, u32[]{:S(2)}, u32[]{:S(2)}) async-start(f32[8,128,512]{2,1,0:T(8,128)} %bitcast.42), calls=%async_computation.3 | async-start | bytes 4194304 | tf_op jit(solution)/shard_map/all_to_all | solution.py:571
  750.0 53.6 %all-to-all-start.4 = ((f32[8,128,512]{2,1,0:T(8,128)}), f32[8,128,512]{2,1,0:T(8,128)}, u32[]{:S(2)}, u32[]{:S(2)}) async-start(f32[8,128,512]{2,1,0:T(8,128)} %bitcast.41), calls=%async_computation.4 | async-start | bytes 4194304 | tf_op jit(solution)/shard_map/all_to_all | solution.py:571
  756.0 54.8 %collective-permute-start.23 = (f32[128,3072]{1,0:T(8,128)}, f32[128,3072]{1,0:T(8,128)}, u32[]{:S(2)}, u32[]{:S(2)}) collective-permute-start(f32[128,3072]{1,0:T(8,128)} %constant_dynamic-slice_fusion), channel_id=1, source_target_pairs={{0,1},{1,0},{2,3},{3,2},{4,5},{5,4},{6,7},{7,6}} | collective-permute-start | bytes 4718600 | tf_op jit(solution)/shard_map/ppermute | solution.py:575
  756.4 44.8 %collective-permute-start.22 = (f32[256,1024]{1,0:T(8,128)S(1)}, f32[256,1024]{1,0:T(8,128)}, u32[]{:S(2)}, u32[]{:S(2)}) collective-permute-start(f32[256,1024]{1,0:T(8,128)S(1)} %dynamic-slice_bitcast_fusion), channel_id=1, source_target_pairs={{0,4},{4,0},{1,5},{5,1},{2,6},{6,2},{3,7},{7,3}} | collective-permute-start | bytes 3145736 | tf_op jit(solution)/shard_map/ppermute | solution.py:579
  (30 other events, 391.3 us)
Sparse Core Ops, SparseCore 0:
  9.8 46.3 all-gather.5
  57.9 62.1 all-gather.11
  121.9 50.8 all-gather.9
  174.4 38.5 all-gather.7
  215.2 69.9 all-gather.13
  398.4 161.6 reduce-scatter.2
  563.5 80.1 reduce-scatter.4
where the time goes:
time: 831 us; the launch traced here: 822 us
  Pallas kernels  414 us (50%)
  waiting for transfers between devices  327 us (39%)
  starting transfers between devices  34.5 us (4%)
  other arithmetic  22.8 us (3%)
  between operations  14.9 us (2%)
  local copies, waits for them, and re-layouts  9.24 us (1%)
    ppermute x22, waiting for transfers between devices, from_sp(): return lax.ppermute(value, 'sp', [(s, s ^ bits) for s in range(SP)])  217 us
    pallas_call x2, Pallas kernels, bwd_call(): pl.pallas_call(bwd_kernel, grid_spec=pltpu.PrefetchScalarGridSpec(num_sca...  134 us
    pallas_call x2, Pallas kernels, fwd_call(): pl.pallas_call(fwd_kernel, grid=(SEQ // BLK,), in_specs=[pl.BlockSpec((BL...  92.8 us
    ppermute x2, waiting for transfers between devices, from_dp(): return lax.ppermute(value, 'dp', [(0, 1), (1, 0)])  73.1 us
    pallas_call x2, Pallas kernels, mlp_call(): pl.pallas_call(mlp_kernel, grid=(TOK // blk,), in_specs=[row(DIM), row(DI...  53.3 us
    pallas_call x2, Pallas kernels, dw_call(): pl.pallas_call(dw_kernel, grid=(4,), in_specs=[left, left] + [right] * le...  32.8 us
    all_to_all x3, waiting for transfers between devices, swap_seq(): return lax.all_to_all(parts, 'sp', 0, 0, tiled=True)  24.9 us
    pallas_call x2, Pallas kernels, qkv_call(): pl.pallas_call(qkv_kernel, grid_spec=pltpu.PrefetchScalarGridSpec(num_sca...  20.6 us
  transfers between devices with their start and end apart: 37, of which 15 were waited for; matrix products, arithmetic and copies ran while one was open for 3% of the time, Pallas kernels for 50%

commit v1 on v0

--- a/solution.py
+++ b/solution.py
@@ -45,6 +45,10 @@
     return lax.dot_general(left, right, (((0,), (0,)), ((), ())), preferred_element_type=jnp.float32)
 
 
+def fixed(shape):
+    return pl.BlockSpec(shape, lambda *_: tuple(0 for _ in shape))
+
+
 def params(**kw):
     return pltpu.CompilerParams(vmem_limit_bytes=VMEM_LIMIT, dimension_semantics=('arbitrary',), **kw)
 
@@ -190,7 +194,6 @@
 def qkv_call(sp_arr, xa, xb, first, gain, w_own, cos, sin, prev):
     place = lambda width: pl.BlockSpec((BLK, width), lambda i, s: ((s[0] ^ (first + i // 2)) * 2 + i % 2, 0))
     local = lambda width: pl.BlockSpec((BLK, width), lambda i, s: (first * 2 + i, 0))
-    fixed = lambda shape: pl.BlockSpec(shape, lambda i, s: (0, 0))
     out = lambda width: jax.ShapeDtypeStruct((SEQ, width), jnp.bfloat16)
     xa_spec = pl.BlockSpec((BLK, DIM), lambda i, s: (jnp.minimum(i, 1), 0))
     xb_spec = pl.BlockSpec((BLK, DIM), lambda i, s: (jnp.maximum(i - 2, 0), 0))
@@ -261,12 +264,12 @@
 
 
 def fwd_call(q, k, v):
-    fixed = pl.BlockSpec((SEQ, HEAD_DIM), lambda i: (0, 0))
+    whole = fixed((SEQ, HEAD_DIM))
     per = TOK // BLK
     return pl.pallas_call(
         fwd_kernel,
         grid=(SEQ // BLK,),
-        in_specs=[pl.BlockSpec((BLK, PAIR), lambda i: (i, 0)), fixed, fixed],
+        in_specs=[pl.BlockSpec((BLK, PAIR), lambda i: (i, 0)), whole, whole],
         out_specs=[pl.BlockSpec((1, BLK, PAIR), lambda i: (i // per, i % per, 0)), pl.BlockSpec((2, 8, BLK), lambda i: (0, 0, i))],
         out_shape=[jax.ShapeDtypeStruct((SEQ // TOK, TOK, PAIR), jnp.bfloat16), jax.ShapeDtypeStruct((2, 8, SEQ), jnp.float32)],
         scratch_shapes=[pltpu.VMEM((2 * BLK // QSUB, HEAD_DIM, QSUB), jnp.float32), pltpu.VMEM((2 * BLK, HEAD_DIM), jnp.bfloat16)],
@@ -342,7 +345,7 @@
 
 
 def bwd_call(sp_arr, q, k, v, o, do, lse, cos, sin):
-    whole = lambda width: pl.BlockSpec((SEQ, width), lambda j, s: (0, 0))
+    whole = lambda width: fixed((SEQ, width))
     block = pl.BlockSpec((BLK, HEAD_DIM), lambda j, s: (j, 0))
     per = TOK // BLK
     table = pl.BlockSpec((BLK, HEAD_DIM), lambda j, s: (((j // per) ^ s[0]) * per + j % per, 0))
@@ -352,7 +355,7 @@
         grid_spec=pltpu.PrefetchScalarGridSpec(
             num_scalar_prefetch=1,
             grid=(SEQ // BLK,),
-            in_specs=[whole(PAIR), block, block, whole(PAIR), whole(PAIR), pl.BlockSpec((2, 8, SEQ), lambda j, s: (0, 0, 0)), table, table],
+            in_specs=[whole(PAIR), block, block, whole(PAIR), whole(PAIR), fixed((2, 8, SEQ)), table, table],
             out_specs=[piece(n) for n in range(SP)],
             scratch_shapes=[
                 pltpu.VMEM((SEQ, PAIR), jnp.float32),
@@ -387,7 +390,7 @@
     return pl.pallas_call(
         oproj_kernel,
         grid=(TOK // blk,),
-        in_specs=[part, part, pl.BlockSpec((2048, DIM), lambda i: (0, 0)), row, pl.BlockSpec((1, DIM), lambda i: (0, 0))],
+        in_specs=[part, part, fixed((2048, DIM)), row, fixed((1, DIM))],
         out_specs=[row, row],
         out_shape=[jax.ShapeDtypeStruct((TOK, DIM), jnp.bfloat16)] * 2,
         compiler_params=params(),
@@ -415,7 +418,6 @@
 def mlp_call(u, dy, w1, w3, w2):
     blk = PAIR
     row = lambda width: pl.BlockSpec((blk, width), lambda i: (i, 0))
-    fixed = lambda shape: pl.BlockSpec(shape, lambda i: (0, 0))
     return pl.pallas_call(
         mlp_kernel,
         grid=(TOK // blk,),
@@ -440,7 +442,7 @@
     rows, cols = la.shape[1] // 4, rights[0].shape[1]
     total = cols * len(rights) // 2
     left = pl.BlockSpec((TOK, rows), lambda b: (0, b))
-    right = pl.BlockSpec((TOK, cols), lambda b: (0, 0))
+    right = fixed((TOK, cols))
     return pl.pallas_call(
         dw_kernel,
         grid=(4,),
@@ -451,6 +453,31 @@
         cost_estimate=cost(4 * TOK * rows * 4 * total, 20),
         name='dw',
     )(la, lb, *rights)
+
+
+def dw_split_kernel(idx_ref, la_ref, lb_ref, ra_ref, rb_ref, send_ref, keep_ref):
+    b = pl.program_id(0)
+    total = dot_tn(la_ref[...], ra_ref[...]) + dot_tn(lb_ref[...], rb_ref[...])
+    for n, ref in enumerate((send_ref, keep_ref)):
+        @pl.when(b // PAIRS == n)
+        def _(ref=ref):
+            ref[0] = total
+
+
+def dw_split_call(idx, la, lb, ra, rb):
+    rows, cols = la.shape[1] // SP, ra.shape[1]
+    left = pl.BlockSpec((TOK, rows), lambda b, s: (0, s[b]))
+    right = fixed((TOK, cols))
+    out = lambda n: pl.BlockSpec((1, rows, cols), lambda b, s: (jnp.clip(b - PAIRS * n, 0, 1), 0, 0))
+    return pl.pallas_call(
+        dw_split_kernel,
+        grid_spec=pltpu.PrefetchScalarGridSpec(
+            num_scalar_prefetch=1, grid=(SP,), in_specs=[left, left, right, right], out_specs=[out(0), out(1)]),
+        out_shape=[jax.ShapeDtypeStruct((PAIRS, rows, cols), jnp.float32)] * PAIRS,
+        compiler_params=params(),
+        cost_estimate=cost(SP * TOK * rows * SP * cols, 20),
+        name='dw_split',
+    )(idx, la, lb, ra, rb)
 
 
 def dw_qkv_kernel(u_ref, *refs):
@@ -465,7 +492,7 @@
     return pl.pallas_call(
         dw_qkv_kernel,
         grid=(4,),
-        in_specs=[pl.BlockSpec((SEQ, PAIR), lambda b: (0, b))] + [pl.BlockSpec((TOK, GRP), lambda b: (0, 0))] * 4,
+        in_specs=[pl.BlockSpec((SEQ, PAIR), lambda b: (0, b))] + [fixed((TOK, GRP))] * 4,
         out_specs=pl.BlockSpec((PAIR, GRP), lambda b: (b, 0)),
         out_shape=jax.ShapeDtypeStruct((DIM, GRP), jnp.float32),
         compiler_params=params(),
@@ -504,7 +531,7 @@
             grid=(SEQ // BLK,),
             in_specs=[src(0), src(1), src(2), src(3), o_spec, o_spec,
                       pl.BlockSpec((PAIR, DIM), lambda i, s: (s[0], 0)), pl.BlockSpec((PAIR, DIM), lambda i, s: (4 + s[0], 0))],
-            out_specs=[d_spec, d_spec, pl.BlockSpec((2, PAIR, DIM), lambda i, s: (0, 0, 0))],
+            out_specs=[d_spec, d_spec, fixed((2, PAIR, DIM))],
             scratch_shapes=[pltpu.VMEM((BLK, DIM), jnp.bfloat16)],
         ),
         out_shape=[out, out, jax.ShapeDtypeStruct((2, PAIR, DIM), jnp.float32)],
@@ -514,14 +541,21 @@
     )(sp_arr, *dhs, o0, o1, wo, wo)
 
 
+def du_sum(sp_ref, pieces, w_ref):
+    total = 0.0
+    for n, piece in enumerate(pieces):
+        cols = pl.ds(pl.multiple_of((sp_ref[0] ^ n) * GRP, GRP), GRP)
+        total += dot_nt(piece[...], w_ref[:, cols])
+    return total
+
+
+def du_kernel(sp_ref, *refs):
+    refs[-1][...] = du_sum(sp_ref, refs[:SP], refs[SP])
+
+
 def dx_kernel(sp_ref, *refs):
-    pieces, (w_ref, x_ref, dr_ref, g_ref, dx_ref, dg_ref) = refs[:8], refs[8:]
-    i = pl.program_id(0)
-    d_u = jnp.zeros(dr_ref.shape, jnp.float32)
-    for n in range(8):
-        cols = pl.ds(pl.multiple_of(((n // 4) * 4 + (sp_ref[0] ^ (n % 4))) * GRP, GRP), GRP)
-        piece = pieces[n][...]
-        d_u += dot_nt(piece, w_ref[:, cols])
+    w_ref, du_ref, x_ref, dr_ref, g_ref, dx_ref, dg_ref = refs[SP:]
+    d_u = du_ref[...] + du_sum(sp_ref, refs[:SP], w_ref)
     x32 = x_ref[...].astype(jnp.float32)
     inv_rms = lax.rsqrt(jnp.mean(x32 * x32, axis=-1, keepdims=True) + NORM_EPS)
     normed = x32 * inv_rms
@@ -529,30 +563,31 @@
     grad_in = inv_rms * (d_normed - normed * jnp.mean(d_normed * normed, axis=-1, keepdims=True))
     dx_ref[...] = (dr_ref[...] + grad_in).astype(jnp.bfloat16)
 
-    @pl.when(i == 0)
+    @pl.when(pl.program_id(0) == 0)
     def _():
         dg_ref[...] = jnp.zeros_like(dg_ref)
 
     dg_ref[...] += jnp.sum(d_u * normed, axis=0, keepdims=True)
 
 
-def dx_call(sp_arr, pieces, w_all, x, d_resid, gain):
-    blk = PAIR
-    row = lambda width: pl.BlockSpec((blk, width), lambda i, s: (i, 0))
-    one = pl.BlockSpec((1, DIM), lambda i, s: (0, 0))
-    return pl.pallas_call(
-        dx_kernel,
+def dx_call(sp_arr, group, pieces, w_all, *rest):
+    row = lambda width: pl.BlockSpec((PAIR, width), lambda i, s: (i, 0))
+    one = fixed((1, DIM))
+    du_shape = jax.ShapeDtypeStruct((TOK, DIM), jnp.float32)
+    last = len(rest) > 0
+    return pl.pallas_call(
+        dx_kernel if last else du_kernel,
         grid_spec=pltpu.PrefetchScalarGridSpec(
             num_scalar_prefetch=1,
-            grid=(TOK // blk,),
-            in_specs=[row(GRP)] * 8 + [pl.BlockSpec((DIM, SEQ), lambda i, s: (0, 0)), row(DIM), row(DIM), one],
-            out_specs=[row(DIM), one],
+            grid=(TOK // PAIR,),
+            in_specs=[row(GRP)] * SP + [pl.BlockSpec((DIM, SP * GRP), lambda i, s: (0, group))] + ([row(DIM)] * 3 + [one] if last else []),
+            out_specs=[row(DIM), one] if last else row(DIM),
         ),
-        out_shape=[jax.ShapeDtypeStruct((TOK, DIM), jnp.bfloat16), jax.ShapeDtypeStruct((1, DIM), jnp.float32)],
-        compiler_params=params(),
-        cost_estimate=cost(2 * TOK * DIM * SEQ, 24),
-        name='dx',
-    )(sp_arr, *pieces, w_all, x, d_resid, gain)
+        out_shape=[jax.ShapeDtypeStruct((TOK, DIM), jnp.bfloat16), jax.ShapeDtypeStruct((1, DIM), jnp.float32)] if last else du_shape,
+        compiler_params=params(),
+        cost_estimate=cost(SP * TOK * DIM * DIM, 16),
+        name='dx' if last else 'du',
+    )(sp_arr, *pieces, w_all, *rest)
 
 
 def gather_full(shard):
@@ -638,30 +673,34 @@
     d_gain2 = jnp.sum(d_umlp * normed2, axis=0)
     d_resid = d_layer.astype(f32) + inv_rms2 * (d_normed2 - normed2 * jnp.mean(d_normed2 * normed2, axis=-1, keepdims=True))
     dhs = gather_chip_then_core(d_resid.astype(bf16))
-    grad_w_down = reduce_chips(dw_call(z_a, z_b, d_layer, dy_pair))
+    chip = dp * PAIRS + sp // PAIRS
+    order = jnp.stack([chip ^ 3, chip ^ 2, chip ^ 1, chip]).astype(jnp.int32)
+    down_send, down_keep = dw_split_call(order, z_a, z_b, d_layer, dy_pair)
+    down_got = from_dp(down_send)
 
     part = reduce_chips(dw_call(u_mlp, u_pair, da_a, da_b, dc_a, dc_b))
 
     do0, do1, dwo = dout_call(sp_arr, dhs, o0, o1, wo_full)
+    down_far, down_near = down_keep[0] + down_got[0], down_keep[1] + down_got[1]
+    down_last = from_sp(down_far, 2)
     o_seq = (o0.reshape(SEQ, PAIR), o1.reshape(SEQ, PAIR))
     d0 = bwd_call(sp_arr, q0, k0, v0, o_seq[0], do0, lse0, cos, sin)
-    back0 = [d0[0]] + [from_sp(d0[n], n) for n in (2, 3, 1)]
+    back0 = [d0[0]] + [from_sp(d0[n], n) for n in (1, 2, 3)]
     part0 = dw_qkv_call(u_all, d0).reshape(8, HEAD_DIM, GRP)
     dw0 = swap_all(part0)
     d1 = bwd_call(sp_arr, q1, k1, v1, o_seq[1], do1, lse1, cos, sin)
-    back1 = [d1[0]] + [from_sp(d1[n], n) for n in (2, 3, 1)]
+    back1 = [d1[0]] + [from_sp(d1[n], n) for n in (1, 2, 3)]
     part1 = dw_qkv_call(u_all, d1).reshape(8, HEAD_DIM, GRP)
     part1, _ = lax.optimization_barrier((part1, dw0))
     dw1 = swap_all(part1)
-    pieces = [t[n] for t in (back0, back1) for n in (0, 3, 1, 2)]
-
     grad_w_out = lax.dynamic_index_in_dim(dwo, dp, 0, keepdims=False) + from_dp(lax.dynamic_index_in_dim(dwo, 1 - dp, 0, keepdims=False))
-    grad_w_query, grad_w_key, grad_w_value = unpack_qkv_call(dw0, dw1)
-
-    grad_hidden, d_gain1 = dx_call(sp_arr, pieces, w_all, tokens, d_resid, gain1)
-    part, _ = lax.optimization_barrier((part, d_gain1))
+    part, _ = lax.optimization_barrier((part, part1))
     send = lax.dynamic_slice(part, ((1 - core) * HEAD_DIM, 0), (HEAD_DIM, 2 * HALF))
     grad_w_gate, grad_w_up = unpack_cols_call(core_arr, part, from_sp(send, 1))
+    grad_w_down = down_near + down_last
+    du0 = dx_call(sp_arr, 0, back0, w_all)
+    grad_hidden, d_gain1 = dx_call(sp_arr, 1, back1, w_all, du0, tokens, d_resid, gain1)
+    grad_w_query, grad_w_key, grad_w_value = unpack_qkv_call(dw0, dw1)
     gain_parts = jnp.stack([d_gain1.reshape(8, HEAD_DIM), d_gain2.reshape(8, HEAD_DIM)], axis=1)
     gain_parts, _ = lax.optimization_barrier((gain_parts, dw1))
     gain_sums = jnp.sum(swap_all(gain_parts), axis=0)

time: 831 us -> 855 us (1.029)
  other arithmetic: 22.8 us -> 35 us
    pallas_call x2 -> x4, Pallas kernels: 26.2 us -> 43.3 us  [the longest x2 20.8 us: dx_call(): pl.pallas_call(dx_kernel if last else du_kernel, grid_spec=pltpu.Prefetch...]
    pallas_call x2 -> x1, Pallas kernels: 32.8 us -> 20.9 us  [dw_call(): pl.pallas_call(dw_kernel, grid=(4,), in_specs=[left, left] + [right] * le...]
    ppermute x22 -> x23, waiting for transfers between devices: 217 us -> 227 us  [from_sp(): return lax.ppermute(value, 'sp', [(s, s ^ bits) for s in range(SP)])]
    all_to_all x3, waiting for transfers between devices: 9.57 us -> 0.94 us  [swap_all(): return lax.all_to_all(parts, ALL_AXES, 0, 0, tiled=True)]
    ppermute x2 -> x3, waiting for transfers between devices: 73.1 us -> 73.2 us  [from_dp(): return lax.ppermute(value, 'dp', [(0, 1), (1, 0)])]
  transfers between devices with their start and end apart: 37 -> 38, of which waited for: 15 -> 13; matrix products, arithmetic and copies ran while one was open for 3% -> 5% of each run, Pallas kernels for 50% -> 43%
where the time goes in v1:
time: 855 us; the launch traced here: 846 us
  Pallas kernels  419 us (49%)
  waiting for transfers between devices  326 us (38%)
  starting transfers between devices  38.6 us (5%)
  other arithmetic  35 us (4%)
  between operations  14.6 us (2%)
  local copies, waits for them, and re-layouts  12.1 us (1%)
    ppermute x23, waiting for transfers between devices, from_sp(): return lax.ppermute(value, 'sp', [(s, s ^ bits) for s in range(SP)])  227 us
    pallas_call x2, Pallas kernels, bwd_call(): pl.pallas_call(bwd_kernel, grid_spec=pltpu.PrefetchScalarGridSpec(num_sca...  134 us
    pallas_call x2, Pallas kernels, fwd_call(): pl.pallas_call(fwd_kernel, grid=(SEQ // BLK,), in_specs=[pl.BlockSpec((BL...  92.8 us
    ppermute x3, waiting for transfers between devices, from_dp(): return lax.ppermute(value, 'dp', [(0, 1), (1, 0)])  73.2 us
    pallas_call x2, Pallas kernels, mlp_call(): pl.pallas_call(mlp_kernel, grid=(TOK // blk,), in_specs=[row(DIM), row(DI...  53.4 us
    all_to_all x3, waiting for transfers between devices, swap_seq(): return lax.all_to_all(parts, 'sp', 0, 0, tiled=True)  23.4 us
    pallas_call x1, Pallas kernels, dw_call(): pl.pallas_call(dw_kernel, grid=(4,), in_specs=[left, left] + [right] * le...  20.9 us
    pallas_call x2, Pallas kernels, dx_call(): pl.pallas_call(dx_kernel if last else du_kernel, grid_spec=pltpu.Prefetch...  20.8 us
  transfers between devices with their start and end apart: 38, of which 13 were waited for; matrix products, arithmetic and copies ran while one was open for 5% of the time, Pallas kernels for 43%

profile of v1, /device:TPU:0, one launch (start us, length us, event | category | flops | bytes accessed | tf_op | source)
XLA Modules:
  0.0 845.9 jit_solution(17394456789043921615)
XLA Ops:
  25.9 66.9 %collective-permute-done.xa_ref = bf16[1024,1024]{1,0:T(8,128)(2,1)S(1)} collective-permute-done((bf16[1024,1024]{1,0:T(8,128)(2,1)}, bf16[1024,1024]{1,0:T(8,128)(2,1)S(1)}, u32[]{:S(2)}, u32[]{:S(2)}) %collective-permute-start) | collective-permute-done | bytes 2097184 | tf_op jit(solution)/shard_map/ppermute | solution.py:610
  93.6 24.5 %collective-permute-done.4 = s32[8,128]{1,0:T(8,128)S(1)} collective-permute-done((s32[8,128]{1,0:T(8,128)S(1)}, s32[8,128]{1,0:T(8,128)S(1)}, u32[]{:S(2)}, u32[]{:S(2)}) %collective-permute-start.4) | collective-permute-done | bytes 4128 | tf_op jit(solution)/shard_map/ppermute | solution.py:610
  119.8 9.4 %fusion.10 = (f32[4096,128]{1,0:T(8,128)}, f32[4096,128]{1,0:T(8,128)}) fusion(f32[128]{0:T(128)S(1)} %get-tuple-element.150, f32[128]{0:T(128)S(1)} %get-tuple-element.151, f32[4096]{0:T(1024)S(1)} %fusion.15), kind=kLoop, calls=%fused_computation.15 | loop fusion | flops 1048576 | bytes 4211712 | tf_op jit(solution)/shard_map/mul | solution.py:654
  129.2 29.9 %collective-permute-done.2.got_ref = bf16[576,1024]{1,0:T(8,128)(2,1)} collective-permute-done((bf16[576,1024]{1,0:T(8,128)(2,1)S(1)}, bf16[576,1024]{1,0:T(8,128)(2,1)}, u32[]{:S(2)}, u32[]{:S(2)}) %collective-permute-start.2) | collective-permute-done | bytes 1179680 | tf_op jit(solution)/shard_map/ppermute | solution.py:614
  163.5 10.3 %qkv.2 = (bf16[4096,1024]{1,0:T(8,128)(2,1)}, bf16[4096,256]{1,0:T(8,128)(2,1)}, bf16[4096,128]{1,0:T(8,128)(2,1)}, bf16[4096,128]{1,0:T(8,128)(2,1)}, bf16[4096...) custom-call(s32[1]{0:T(128)} %bitcast.sp_ref, bf16[1024,1024]{1,0:T(8,128)(2,1)} %bitcast.55, ...), custom_call_target="tpu_custom_call" | custom-call | flops 4294967296 | bytes 20971520 | tf_op jit(solution)/shard_map/qkv/pallas_call | solution.py:201
  173.8 10.3 %qkv.3 = (bf16[4096,1024]{1,0:T(8,128)(2,1)}, bf16[4096,256]{1,0:T(8,128)(2,1)}, bf16[4096,128]{1,0:T(8,128)(2,1)}, bf16[4096,128]{1,0:T(8,128)(2,1)}, bf16[4096...) custom-call(s32[1]{0:T(128)} %bitcast.sp_ref, ...), custom_call_target="tpu_custom_call", output_to_operand_aliasing={{0}: (7, {}), {1}: (8, {}), {2}: (9, {}), {3}: (10, {}), {4... | custom-call | flops 4294967296 | bytes 20971520 | tf_op jit(solution)/shard_map/qkv/pallas_call | solution.py:201
  184.1 46.4 %attn_fwd.3 = (bf16[4,1024,256]{2,1,0:T(8,128)(2,1)}, f32[2,8,4096]{2,1,0:T(8,128)}) custom-call(bf16[4096,256]{1,0:T(8,128)(2,1)} %get-tuple-element.89.q_ref, bf16[4096,128]{1,0:T(8,128)(2,1)} %get-tuple-element.90.k_ref, bf16[4096,128]{1,0:T(8,128)(2,1)} %get-tuple-element.91.v_ref), custom_call_target="tpu_custom_call" | custom-call | flops 24000000000 | bytes 8388608 | tf_op jit(solution)/shard_map/attn_fwd/pallas_call | solution.py:269
  234.1 46.4 %attn_fwd.2 = (bf16[4,1024,256]{2,1,0:T(8,128)(2,1)}, f32[2,8,4096]{2,1,0:T(8,128)}) custom-call(bf16[4096,256]{1,0:T(8,128)(2,1)} %get-tuple-element.85.q_ref, bf16[4096,128]{1,0:T(8,128)(2,1)} %get-tuple-element.86.k_ref, bf16[4096,128]{1,0:T(8,128)(2,1)} %get-tuple-element.87.v_ref), custom_call_target="tpu_custom_call" | custom-call | flops 24000000000 | bytes 8388608 | tf_op jit(solution)/shard_map/attn_fwd/pallas_call | solution.py:269
  288.7 23.4 %all-to-all-done.1.a0_ref = bf16[4,1024,256]{2,1,0:T(8,128)(2,1)} async-done(((bf16[4,1024,256]{2,1,0:T(8,128)(2,1)}), bf16[4,1024,256]{2,1,0:T(8,128)(2,1)}, u32[]{:S(2)}, u32[]{:S(2)}) %all-to-all-start.1) | async-done | bytes 2097184 | tf_op jit(solution)/shard_map/all_to_all | solution.py:602
  312.1 9.5 %oproj.1 = (bf16[1024,1024]{1,0:T(8,128)(2,1)}, bf16[1024,1024]{1,0:T(8,128)(2,1)}) custom-call(bf16[4,1024,256]{2,1,0:T(8,128)(2,1)} %all-to-all-done.1.a0_ref, bf16[4,1024,256]{2,1,0:T(8,128)(2,1)} %copy-done.11, bf16[2048,1024]{1,0:T(8,128)(2,1)} %all-gather.6.cloned.1.call-done.w_ref.wa_ref.wb_ref, bf16[1024,1024]{1,0:T(8,128)(2,1)} %bitcast.56, ...), custom_call_target="tpu_custom_call" | custom-call | flops 4294967296 | bytes 14680064 | tf_op jit(solution)/shard_map/oproj/pallas_call | solution.py:390
  321.8 26.6 %mlp.2 = (bf16[1024,1536]{1,0:T(8,128)(2,1)}, bf16[1024,1536]{1,0:T(8,128)(2,1)}, bf16[1024,1536]{1,0:T(8,128)(2,1)}, f32[1024,1024]{1,0:T(8,128)}, f32[1024,1024]{1,0:T(8,128)}) custom-call(bf16[1024,1024]{1,0:T(8,128)(2,1)} %get-tuple-element.95.u_ref.la_ref, bf16[1024,1024]{1,0:T(8,128)(2,1)} %bitcast.46, ...), custom_call_target="tpu_custom_call" | custom-call | flops 19327352832 | bytes 31457280 | tf_op jit(solution)/shard_map/mlp/pallas_call | solution.py:421
  348.4 26.7 %mlp.3 = (bf16[1024,1536]{1,0:T(8,128)(2,1)}, bf16[1024,1536]{1,0:T(8,128)(2,1)}, bf16[1024,1536]{1,0:T(8,128)(2,1)}, f32[1024,1024]{1,0:T(8,128)}, f32[1024,1024]{1,0:T(8,128)}) custom-call(bf16[1024,1024]{1,0:T(8,128)(2,1)} %collective-permute-done.9.u_ref.lb_ref, bf16[1024,1024]{1,0:T(8,128)(2,1)} %collective-permute-done.10.dy_ref.rb_ref, ...), custom_call_target="tpu_custom_call" | custom-call | flops 19327352832 | bytes 31457280 | tf_op jit(solution)/shard_map/mlp/pallas_call | solution.py:421
  375.1 20.9 %dw.1 = f32[1024,3072]{1,0:T(8,128)} custom-call(bf16[1024,1024]{1,0:T(8,128)(2,1)} %get-tuple-element.95.u_ref.la_ref, bf16[1024,1024]{1,0:T(8,128)(2,1)} %collective-permute-done.9.u_ref.lb_ref, bf16[1024,1536]{1,0:T(8,128)(2,1)} %get-tuple-element.128.refs_0_, bf16[1024,1536]{1,0:T(8,128)(2,1)} %get-tuple-element.129.refs_1_, ...), custom_call_target="tpu_custom_call" | custom-call | flops 12884901888 | bytes 20971520 | tf_op jit(solution)/shard_map/dw/pallas_call | solution.py:446
  417.8 13.0 %dw_split.1 = (f32[2,384,1024]{2,1,0:T(8,128)}, f32[2,384,1024]{2,1,0:T(8,128)}) custom-call(s32[4]{0:T(128)} %pad_add_fusion.idx_ref, bf16[1024,1536]{1,0:T(8,128)(2,1)} %get-tuple-element.135.la_ref, bf16[1024,1536]{1,0:T(8,128)(2,1)} %get-tuple-element.136.lb_ref, bf16[1024,1024]{1,0:T(8,128)(2,1)} %bitcast.47, ...), custom_call_target="tpu_custom_call" | custom-call | flops 6442450944 | bytes 20971520 | tf_op jit(solution)/shard_map/dw_split/pallas_call | solution.py:472
  434.2 76.6 %collective-permute-done.14.h2_ref = bf16[1024,1024]{1,0:T(8,128)(2,1)} collective-permute-done((bf16[1024,1024]{1,0:T(8,128)(2,1)}, bf16[1024,1024]{1,0:T(8,128)(2,1)}, u32[]{:S(2)}, u32[]{:S(2)}) %collective-permute-start.14) | collective-permute-done | bytes 2097184 | tf_op jit(solution)/shard_map/ppermute | solution.py:610
  510.9 43.3 %collective-permute-done.24 = f32[2,384,1024]{2,1,0:T(8,128)S(1)} collective-permute-done((f32[2,384,1024]{2,1,0:T(8,128)}, f32[2,384,1024]{2,1,0:T(8,128)S(1)}, u32[]{:S(2)}, u32[]{:S(2)}) %collective-permute-start.24) | collective-permute-done | bytes 3145760 | tf_op jit(solution)/shard_map/ppermute | solution.py:614
  559.7 17.9 %dout.1 = (bf16[4096,256]{1,0:T(8,128)(2,1)}, bf16[4096,256]{1,0:T(8,128)(2,1)}, f32[2,256,1024]{2,1,0:T(8,128)}) custom-call(s32[1]{0:T(128)} %bitcast.sp_ref, bf16[1024,1024]{1,0:T(8,128)(2,1)} %get-tuple-element.141.h0_ref, bf16[1024,1024]{1,0:T(8,128)(2,1)} %collective-permute-done.13.h1_ref, bf16[1024,1024]{1,0:T(8,128)(2,1)} %collective-permute-done.14.h2_ref, ...), custom_call_target="tpu_custom_call" | custom-call | flops 8589934592 | bytes 20971520 | tf_op jit(solution)/shard_map/dout/pallas_call | solution.py:527
  577.6 67.3 %attn_bwd.3 = (bf16[1024,512]{1,0:T(8,128)(2,1)}, bf16[1024,512]{1,0:T(8,128)(2,1)}, bf16[1024,512]{1,0:T(8,128)(2,1)}, bf16[1024,512]{1,0:T(8,128)(2,1)}) custom-call(s32[1]{0:T(128)} %bitcast.sp_ref, bf16[4096,256]{1,0:T(8,128)(2,1)} %get-tuple-element.85.q_ref, bf16[4096,128]{1,0:T(8,128)(2,1)} %get-tuple-element.86.k_ref, ...), custom_call_target="tpu_custom_call" | custom-call | flops 60000002048 | bytes 16777216 | tf_op jit(solution)/shard_map/attn_bwd/pallas_call | solution.py:353
  646.7 9.4 %dw_qkv.3 = f32[1024,512]{1,0:T(8,128)} custom-call(bf16[4096,1024]{1,0:T(8,128)(2,1)} %get-tuple-element.121.u_ref, bf16[1024,512]{1,0:T(8,128)(2,1)} %get-tuple-element.115.refs_0_, bf16[1024,512]{1,0:T(8,128)(2,1)} %get-tuple-element.116.refs_1_, bf16[1024,512]{1,0:T(8,128)(2,1)} %get-tuple-element.117.refs_2_, bf16[1024,512]{1,0:T(8,128)(2,1)} %get-tuple-element.118.refs_3_), custom_call_target="tpu_custom_call" | custom-call | flops 4294967296 | bytes 14680064 | tf_op jit(solution)/shard_map/dw_qkv/pallas_call | solution.py:492
  658.7 66.8 %attn_bwd.2 = (bf16[1024,512]{1,0:T(8,128)(2,1)}, bf16[1024,512]{1,0:T(8,128)(2,1)}, bf16[1024,512]{1,0:T(8,128)(2,1)}, bf16[1024,512]{1,0:T(8,128)(2,1)}) custom-call(s32[1]{0:T(128)} %bitcast.sp_ref, bf16[4096,256]{1,0:T(8,128)(2,1)} %get-tuple-element.89.q_ref, bf16[4096,128]{1,0:T(8,128)(2,1)} %get-tuple-element.90.k_ref, ...), custom_call_target="tpu_custom_call" | custom-call | flops 60000002048 | bytes 16777216 | tf_op jit(solution)/shard_map/attn_bwd/pallas_call | solution.py:353
  728.1 9.4 %dw_qkv.2 = f32[1024,512]{1,0:T(8,128)} custom-call(bf16[4096,1024]{1,0:T(8,128)(2,1)} %get-tuple-element.121.u_ref, bf16[1024,512]{1,0:T(8,128)(2,1)} %get-tuple-element.108.refs_0_, bf16[1024,512]{1,0:T(8,128)(2,1)} %get-tuple-element.109.refs_1_, bf16[1024,512]{1,0:T(8,128)(2,1)} %get-tuple-element.110.refs_2_, bf16[1024,512]{1,0:T(8,128)(2,1)} %get-tuple-element.111.refs_3_), custom_call_target="tpu_custom_call" | custom-call | flops 4294967296 | bytes 14680064 | tf_op jit(solution)/shard_map/dw_qkv/pallas_call | solution.py:492
  761.0 29.6 %collective-permute-done.17.refs_2_ = bf16[1024,512]{1,0:T(8,128)(2,1)} collective-permute-done((bf16[1024,512]{1,0:T(8,128)(2,1)}, bf16[1024,512]{1,0:T(8,128)(2,1)}, u32[]{:S(2)}, u32[]{:S(2)}) %collective-permute-start.17) | collective-permute-done | bytes 1048608 | tf_op jit(solution)/shard_map/ppermute | solution.py:610
  790.7 21.3 %collective-permute-done.18.refs_3_ = bf16[1024,512]{1,0:T(8,128)(2,1)} collective-permute-done((bf16[1024,512]{1,0:T(8,128)(2,1)}, bf16[1024,512]{1,0:T(8,128)(2,1)}, u32[]{:S(2)}, u32[]{:S(2)}) %collective-permute-start.18) | collective-permute-done | bytes 1048608 | tf_op jit(solution)/shard_map/ppermute | solution.py:610
  812.0 11.7 %dx.1 = (bf16[1024,1024]{1,0:T(8,128)(2,1)}, f32[1,1024]{1,0:T(1,128)}) custom-call(s32[1]{0:T(128)} %bitcast.sp_ref, bf16[1024,512]{1,0:T(8,128)(2,1)} %get-tuple-element.108.refs_0_, bf16[1024,512]{1,0:T(8,128)(2,1)} %collective-permute-done.16.refs_1_, bf16[1024,512]{1,0:T(8,128)(2,1)} %collective-permute-done.17.refs_2_, ...), custom_call_target="tpu_custom_call" | custom-call | flops 4294967296 | bytes 16777216 | tf_op jit(solution)/shard_map/dx/pallas_call | solution.py:578
  (130 shorter events, 113.7 us)
Async XLA Ops:
  7.2 305.0 %all-gather.6.cloned.1.call-start = ((), (), s32[]{:S(2)}) async-start(), calls=%async_computation.7 | async-start | bytes 4718592 | tf_op jit(solution)/shard_map/all_gather | solution.py:594
  7.9 313.8 %all-gather.12.cloned.1.call-start = ((), (), s32[]{:S(2)}) async-start(), calls=%async_computation.10 | async-start | bytes 3932160 | tf_op jit(solution)/shard_map/all_gather | solution.py:598
  8.7 313.1 %all-gather.10.cloned.1.call-start = ((), (), s32[]{:S(2)}) async-start(), calls=%async_computation.9 | async-start | bytes 3932160 | tf_op jit(solution)/shard_map/all_gather | solution.py:598
  19.1 73.8 %collective-permute-start = (bf16[1024,1024]{1,0:T(8,128)(2,1)}, bf16[1024,1024]{1,0:T(8,128)(2,1)S(1)}, u32[]{:S(2)}, u32[]{:S(2)}) collective-permute-start(bf16[1024,1024]{1,0:T(8,128)(2,1)} %bitcast.53), channel_id=1, source_target_pairs={{0,2},{1,3},{2,0},{3,1},{4,6},{5,7},{6,4},{7,5}} | collective-permute-start | bytes 6291464 | tf_op jit(solution)/shard_map/ppermute | solution.py:610
  21.9 96.3 %all-to-all-start = ((bf16[4,144,1024]{2,1,0:T(8,128)(2,1)}), bf16[4,144,1024]{2,1,0:T(8,128)(2,1)S(1)}, u32[]{:S(2)}, u32[]{:S(2)}) async-start(bf16[4,144,1024]{2,1,0:T(8,128)(2,1)} %bitcast.58), calls=%async_computation | async-start | bytes 2359296 | tf_op jit(solution)/shard_map/all_to_all | solution.py:602
  25.4 296.3 %all-gather.8.cloned.1.call-start = ((), (), s32[]{:S(2)}) async-start(), calls=%async_computation.8 | async-start | bytes 3932160 | tf_op jit(solution)/shard_map/all_gather | solution.py:598
  25.5 138.0 %collective-permute-start.6 = (bf16[1024,1024]{1,0:T(8,128)(2,1)}, bf16[1024,1024]{1,0:T(8,128)(2,1)}, u32[]{:S(2)}, u32[]{:S(2)}) collective-permute-start(bf16[1024,1024]{1,0:T(8,128)(2,1)} %bitcast.54), channel_id=1, source_target_pairs={{0,1},{1,0},{2,3},{3,2},{4,5},{5,4},{6,7},{7,6}} | collective-permute-start | bytes 6291464 | tf_op jit(solution)/shard_map/ppermute | solution.py:610
  92.8 81.0 %collective-permute-start.1 = (bf16[1024,1024]{1,0:T(8,128)(2,1)S(1)}, bf16[1024,1024]{1,0:T(8,128)(2,1)}, u32[]{:S(2)}, u32[]{:S(2)}) collective-permute-start(bf16[1024,1024]{1,0:T(8,128)(2,1)S(1)} %collective-permute-done.xa_ref), channel_id=1, source_target_pairs={{0,1},{1,0},{2,3},{3,2},{4,5},{5,4},{6,7},{7,6}} | collective-permute-start | bytes 6291464 | tf_op jit(solution)/shard_map/ppermute | solution.py:610
  230.5 50.0 %all-to-all-start.2 = ((bf16[4,1024,256]{2,1,0:T(8,128)(2,1)}), bf16[4,1024,256]{2,1,0:T(8,128)(2,1)S(1)}, u32[]{:S(2)}, u32[]{:S(2)}) async-start(bf16[4,1024,256]{2,1,0:T(8,128)(2,1)} %get-tuple-element.92.o1_ref), calls=%async_computation.2 | async-start | bytes 4194304 | tf_op jit(solution)/shard_map/all_to_all | solution.py:602
  286.4 455.5 %reduce-scatter.2.cloned.1.call-start = ((), (), s32[]{:S(2)}) async-start(), calls=%async_computation.12 | async-start | bytes 15728640 | tf_op jit(solution)/shard_map/reduce_scatter | solution.py:623
  286.9 61.5 %collective-permute-start.10 = (bf16[1024,1024]{1,0:T(8,128)(2,1)S(1)}, bf16[1024,1024]{1,0:T(8,128)(2,1)}, u32[]{:S(2)}, u32[]{:S(2)}) collective-permute-start(bf16[1024,1024]{1,0:T(8,128)(2,1)S(1)} %bitcast.48), channel_id=1, source_target_pairs={{0,1},{1,0},{2,3},{3,2},{4,5},{5,4},{6,7},{7,6}} | collective-permute-start | bytes 6291464 | tf_op jit(solution)/shard_map/ppermute | solution.py:610
  396.1 355.8 %all-gather.14.cloned.1.call-start = ((), (), s32[]{:S(2)}) async-start(), calls=%async_computation.11 | async-start | bytes 9437184 | tf_op jit(solution)/shard_map/all_gather | solution.py:594
  417.2 93.7 %collective-permute-start.14 = (bf16[1024,1024]{1,0:T(8,128)(2,1)}, bf16[1024,1024]{1,0:T(8,128)(2,1)}, u32[]{:S(2)}, u32[]{:S(2)}) collective-permute-start(bf16[1024,1024]{1,0:T(8,128)(2,1)} %get-tuple-element.141.h0_ref), channel_id=1, source_target_pairs={{0,2},{1,3},{2,0},{3,1},{4,6},{5,7},{6,4},{7,5}} | collective-permute-start | bytes 6291464 | tf_op jit(solution)/shard_map/ppermute | solution.py:610
  430.8 123.4 %collective-permute-start.24 = (f32[2,384,1024]{2,1,0:T(8,128)}, f32[2,384,1024]{2,1,0:T(8,128)S(1)}, u32[]{:S(2)}, u32[]{:S(2)}) collective-permute-start(f32[2,384,1024]{2,1,0:T(8,128)} %get-tuple-element.138), channel_id=1, source_target_pairs={{0,4},{4,0},{1,5},{5,1},{2,6},{6,2},{3,7},{7,3}} | collective-permute-start | bytes 9437192 | tf_op jit(solution)/shard_map/ppermute | solution.py:614
  434.2 125.5 %collective-permute-start.13 = (bf16[1024,1024]{1,0:T(8,128)(2,1)}, bf16[1024,1024]{1,0:T(8,128)(2,1)}, u32[]{:S(2)}, u32[]{:S(2)}) collective-permute-start(bf16[1024,1024]{1,0:T(8,128)(2,1)} %get-tuple-element.141.h0_ref), channel_id=1, source_target_pairs={{0,1},{1,0},{2,3},{3,2},{4,5},{5,4},{6,7},{7,6}} | collective-permute-start | bytes 6291464 | tf_op jit(solution)/shard_map/ppermute | solution.py:610
  558.1 183.8 %collective-permute-start.25 = (f32[384,1024]{1,0:T(8,128)}, f32[384,1024]{1,0:T(8,128)}, u32[]{:S(2)}, u32[]{:S(2)}) collective-permute-start(f32[384,1024]{1,0:T(8,128)} %fusion.12), channel_id=1, source_target_pairs={{0,2},{1,3},{2,0},{3,1},{4,6},{5,7},{6,4},{7,5}} | collective-permute-start | bytes 4718600 | tf_op jit(solution)/shard_map/ppermute | solution.py:610
  644.9 99.0 %collective-permute-start.19 = (bf16[1024,512]{1,0:T(8,128)(2,1)}, bf16[1024,512]{1,0:T(8,128)(2,1)}, u32[]{:S(2)}, u32[]{:S(2)}) collective-permute-start(bf16[1024,512]{1,0:T(8,128)(2,1)} %get-tuple-element.116.refs_1_), channel_id=1, source_target_pairs={{0,1},{1,0},{2,3},{3,2},{4,5},{5,4},{6,7},{7,6}} | collective-permute-start | bytes 3145736 | tf_op jit(solution)/shard_map/ppermute | solution.py:610
  644.9 101.7 %collective-permute-start.20 = (bf16[1024,512]{1,0:T(8,128)(2,1)}, bf16[1024,512]{1,0:T(8,128)(2,1)}, u32[]{:S(2)}, u32[]{:S(2)}) collective-permute-start(bf16[1024,512]{1,0:T(8,128)(2,1)} %get-tuple-element.117.refs_2_), channel_id=1, source_target_pairs={{0,2},{1,3},{2,0},{3,1},{4,6},{5,7},{6,4},{7,5}} | collective-permute-start | bytes 3145736 | tf_op jit(solution)/shard_map/ppermute | solution.py:610
  644.9 103.2 %collective-permute-start.21 = (bf16[1024,512]{1,0:T(8,128)(2,1)}, bf16[1024,512]{1,0:T(8,128)(2,1)}, u32[]{:S(2)}, u32[]{:S(2)}) collective-permute-start(bf16[1024,512]{1,0:T(8,128)(2,1)} %get-tuple-element.118.refs_3_), channel_id=1, source_target_pairs={{0,3},{1,2},{2,1},{3,0},{4,7},{5,6},{6,5},{7,4}} | collective-permute-start | bytes 3145736 | tf_op jit(solution)/shard_map/ppermute | solution.py:610
  656.1 81.4 %all-to-all-start.3 = ((f32[8,128,512]{2,1,0:T(8,128)}), f32[8,128,512]{2,1,0:T(8,128)S(1)}, u32[]{:S(2)}, u32[]{:S(2)}) async-start(f32[8,128,512]{2,1,0:T(8,128)} %bitcast.52), calls=%async_computation.3 | async-start | bytes 4194304 | tf_op jit(solution)/shard_map/all_to_all | solution.py:606
  738.8 88.6 %all-to-all-start.4 = ((f32[8,128,512]{2,1,0:T(8,128)}), f32[8,128,512]{2,1,0:T(8,128)}, u32[]{:S(2)}, u32[]{:S(2)}) async-start(f32[8,128,512]{2,1,0:T(8,128)} %bitcast.51), calls=%async_computation.4 | async-start | bytes 4194304 | tf_op jit(solution)/shard_map/all_to_all | solution.py:606
  743.8 68.2 %collective-permute-start.18 = (bf16[1024,512]{1,0:T(8,128)(2,1)}, bf16[1024,512]{1,0:T(8,128)(2,1)}, u32[]{:S(2)}, u32[]{:S(2)}) collective-permute-start(bf16[1024,512]{1,0:T(8,128)(2,1)} %get-tuple-element.111.refs_3_), channel_id=1, source_target_pairs={{0,3},{1,2},{2,1},{3,0},{4,7},{5,6},{6,5},{7,4}} | collective-permute-start | bytes 3145736 | tf_op jit(solution)/shard_map/ppermute | solution.py:610
  746.5 78.5 %collective-permute-start.22 = (f32[256,1024]{1,0:T(8,128)}, f32[256,1024]{1,0:T(8,128)}, u32[]{:S(2)}, u32[]{:S(2)}) collective-permute-start(f32[256,1024]{1,0:T(8,128)} %dynamic-slice_bitcast_fusion), channel_id=1, source_target_pairs={{0,4},{4,0},{1,5},{5,1},{2,6},{6,2},{3,7},{7,3}} | collective-permute-start | bytes 3145736 | tf_op jit(solution)/shard_map/ppermute | solution.py:614
  748.1 86.5 %collective-permute-start.23 = (f32[128,3072]{1,0:T(8,128)}, f32[128,3072]{1,0:T(8,128)}, u32[]{:S(2)}, u32[]{:S(2)}) collective-permute-start(f32[128,3072]{1,0:T(8,128)} %constant_dynamic-slice_fusion), channel_id=1, source_target_pairs={{0,1},{1,0},{2,3},{3,2},{4,5},{5,4},{6,7},{7,6}} | collective-permute-start | bytes 4718600 | tf_op jit(solution)/shard_map/ppermute | solution.py:610
  (30 other events, 505.0 us)
Sparse Core Ops, SparseCore 0:
  9.8 46.9 all-gather.5
  58.6 61.4 all-gather.11
  121.9 50.1 all-gather.9
  173.7 38.4 all-gather.7
  396.2 177.2 reduce-scatter.1
  575.8 59.4 all-gather.13

commit v2 on v1

--- a/solution.py
+++ b/solution.py
@@ -399,7 +399,17 @@
     )(a0, a1, wo, x, gain)
 
 
-def mlp_kernel(u_ref, dy_ref, w1_ref, w3_ref, w2_ref, z_ref, da_ref, dc_ref, y_ref, d_ref):
+def mlp_kernel(chip_ref, u_ref, dy_ref, *refs):
+    z_ref, da_ref, dc_ref, y_ref, d_ref, w1_ref, w3_ref, w2_ref = refs[3 * SP:]
+
+    @pl.when(pl.program_id(0) == 0)
+    def _():
+        for w, ref in enumerate((w1_ref, w3_ref, w2_ref)):
+            for n in range(SP):
+                piece = refs[w * SP + n]
+                rows = piece.shape[0]
+                ref[pl.ds(pl.multiple_of((chip_ref[0] ^ n) * rows, HEAD_DIM), rows), :] = piece[...]
+
     u, dy = u_ref[...], dy_ref[...]
     for n in range(HALF // GRP):
         cols = slice(n * GRP, (n + 1) * GRP)
@@ -415,19 +425,24 @@
     y_ref[...] = dot_nn(z_ref[...], w2_ref[...])
 
 
-def mlp_call(u, dy, w1, w3, w2):
-    blk = PAIR
-    row = lambda width: pl.BlockSpec((blk, width), lambda i: (i, 0))
+def mlp_call(chip_arr, u, dy, w1, w3, w2):
+    row = lambda width: pl.BlockSpec((PAIR, width), lambda i, s: (i, 0))
+    pieces = [*w1, *w3, *w2]
+    bf16, f32 = jnp.bfloat16, jnp.float32
     return pl.pallas_call(
         mlp_kernel,
-        grid=(TOK // blk,),
-        in_specs=[row(DIM), row(DIM), fixed((DIM, HALF)), fixed((DIM, HALF)), fixed((HALF, DIM))],
-        out_specs=[row(HALF), row(HALF), row(HALF), row(DIM), row(DIM)],
-        out_shape=[jax.ShapeDtypeStruct((TOK, HALF), jnp.bfloat16)] * 3 + [jax.ShapeDtypeStruct((TOK, DIM), jnp.float32)] * 2,
+        grid_spec=pltpu.PrefetchScalarGridSpec(
+            num_scalar_prefetch=1,
+            grid=(TOK // PAIR,),
+            in_specs=[row(DIM), row(DIM)] + [fixed(t.shape) for t in pieces],
+            out_specs=[row(HALF), row(HALF), row(HALF), row(DIM), row(DIM)],
+            scratch_shapes=[pltpu.VMEM((DIM, HALF), bf16), pltpu.VMEM((DIM, HALF), bf16), pltpu.VMEM((HALF, DIM), bf16)],
+        ),
+        out_shape=[jax.ShapeDtypeStruct((TOK, HALF), bf16)] * 3 + [jax.ShapeDtypeStruct((TOK, DIM), f32)] * PAIRS,
         compiler_params=params(),
         cost_estimate=cost(12 * TOK * DIM * HALF, 30),
         name='mlp',
-    )(u, dy, w1, w3, w2)
+    )(chip_arr, u, dy, *pieces)
 
 
 def dw_kernel(la_ref, lb_ref, *refs):
@@ -594,10 +609,6 @@
     return lax.all_gather(shard, ALL_AXES, axis=0, tiled=True)
 
 
-def gather_core(shard):
-    return lax.all_gather(shard, ALL_AXES, axis=0, tiled=True, axis_index_groups=CORE_GROUPS)
-
-
 def swap_seq(parts):
     return lax.all_to_all(parts, 'sp', 0, 0, tiled=True)
 
@@ -617,6 +628,13 @@
 def gather_chip_then_core(value):
     far = from_sp(value, 2)
     return value, from_sp(value, 1), far, from_sp(far, 1)
+
+
+def gather_chips(value):
+    across = from_dp(value)
+    along = from_sp(value, 2)
+    far = from_dp(along)
+    return value, along, across, far
 
 
 def reduce_chips(part):
@@ -629,20 +647,22 @@
     dp = lax.axis_index('dp')
     sp = lax.axis_index('sp')
     core = sp % 2
+    chip = dp * PAIRS + sp // PAIRS
     f32, bf16 = jnp.float32, jnp.bfloat16
     sp_arr, dp_arr, core_arr = (t.astype(jnp.int32)[None] for t in (sp, dp, core))
+    chip_arr = chip.astype(jnp.int32)[None]
 
     xs = gather_chip_then_core(tokens)
     w_cols, w_send, a1, b1, a3, b3 = pack_call(core_arr, w_query, w_key, w_value, w_gate, w_up, gain_attn[None], gain_mlp[None])
     w_mine = swap_seq(w_send)
-    w_own, gain1, gain2 = join_qkv_call(dp_arr, w_mine, from_dp(w_mine))
+    w_got = from_dp(w_mine)
+    w_own, gain1, gain2 = join_qkv_call(dp_arr, w_mine, w_got)
     gain1, gain2 = gain1[0:1], gain2[0:1]
     pos = gather_chip_then_core(positions[0].reshape(8, HEAD_DIM))
     pos_all = jnp.concatenate(pos).reshape(SEQ)
     w1_rows, w3_rows = join_call(core_arr, (a1, from_sp(b1, 1)), (a3, from_sp(b3, 1)))
     wo_full = gather_full(w_out)
-    w2 = gather_core(w_down)
-    w1, w3 = gather_core(w1_rows), gather_core(w3_rows)
+    w2, w1, w3 = (gather_chips(t) for t in (w_down, w1_rows, w3_rows))
     w_all = gather_full(w_cols)
     dy_pair = from_sp(d_layer, 1)
 
@@ -662,8 +682,8 @@
     residual, u_mlp = oproj_call(got0, got1, wo_full, tokens, gain2)
 
     u_pair = from_sp(u_mlp, 1)
-    z_a, da_a, dc_a, y_a, d_a = mlp_call(u_mlp, d_layer, w1, w3, w2)
-    z_b, da_b, dc_b, y_b, d_b = mlp_call(u_pair, dy_pair, w1, w3, w2)
+    z_a, da_a, dc_a, y_a, d_a = mlp_call(chip_arr, u_mlp, d_layer, w1, w3, w2)
+    z_b, da_b, dc_b, y_b, d_b = mlp_call(chip_arr, u_pair, dy_pair, w1, w3, w2)
     d_umlp = d_a + from_sp(d_b, 1)
     h32 = residual.astype(f32)
     layer_out = (h32 + (y_a + from_sp(y_b, 1))).astype(bf16)
@@ -673,7 +693,6 @@
     d_gain2 = jnp.sum(d_umlp * normed2, axis=0)
     d_resid = d_layer.astype(f32) + inv_rms2 * (d_normed2 - normed2 * jnp.mean(d_normed2 * normed2, axis=-1, keepdims=True))
     dhs = gather_chip_then_core(d_resid.astype(bf16))
-    chip = dp * PAIRS + sp // PAIRS
     order = jnp.stack([chip ^ 3, chip ^ 2, chip ^ 1, chip]).astype(jnp.int32)
     down_send, down_keep = dw_split_call(order, z_a, z_b, d_layer, dy_pair)
     down_got = from_dp(down_send)

time: 855 us -> 886 us (1.036)
  waiting for transfers between devices: 326 us -> 344 us
  starting transfers between devices: 38.6 us -> 49.5 us
    all_to_all x3, waiting for transfers between devices: 23.4 us -> 0.01 us  [swap_seq(): return lax.all_to_all(parts, 'sp', 0, 0, tiled=True)]
    ppermute x23 -> x26, waiting for transfers between devices: 227 us -> 249 us  [from_sp(): return lax.ppermute(value, 'sp', [(s, s ^ bits) for s in range(SP)])]
    ppermute x3 -> x9, waiting for transfers between devices: 73.2 us -> 94.4 us  [from_dp(): return lax.ppermute(value, 'dp', [(0, 1), (1, 0)])]
    ppermute x23 -> x26, starting transfers between devices: 11.9 us -> 18.9 us  [from_sp(): return lax.ppermute(value, 'sp', [(s, s ^ bits) for s in range(SP)])]
  transfers between devices with their start and end apart: 38 -> 44, of which waited for: 13 -> 15; matrix products, arithmetic and copies ran while one was open for 5% -> 5% of each run, Pallas kernels for 43% -> 42%
where the time goes in v2:
time: 886 us; the launch traced here: 877 us
  Pallas kernels  421 us (48%)
  waiting for transfers between devices  344 us (39%)
  starting transfers between devices  49.5 us (6%)
  other arithmetic  35.2 us (4%)
  between operations  14.5 us (2%)
  local copies, waits for them, and re-layouts  12.3 us (1%)
    ppermute x26, waiting for transfers between devices, from_sp(): return lax.ppermute(value, 'sp', [(s, s ^ bits) for s in range(SP)])  249 us
    pallas_call x2, Pallas kernels, bwd_call(): pl.pallas_call(bwd_kernel, grid_spec=pltpu.PrefetchScalarGridSpec(num_sca...  134 us
    ppermute x9, waiting for transfers between devices, from_dp(): return lax.ppermute(value, 'dp', [(0, 1), (1, 0)])  94.4 us
    pallas_call x2, Pallas kernels, fwd_call(): pl.pallas_call(fwd_kernel, grid=(SEQ // BLK,), in_specs=[pl.BlockSpec((BL...  92.7 us
    pallas_call x2, Pallas kernels, mlp_call(): pl.pallas_call(mlp_kernel, grid_spec=pltpu.PrefetchScalarGridSpec(num_sca...  54.9 us
    pallas_call x1, Pallas kernels, dw_call(): pl.pallas_call(dw_kernel, grid=(4,), in_specs=[left, left] + [right] * le...  21 us
    pallas_call x2, Pallas kernels, dx_call(): pl.pallas_call(dx_kernel if last else du_kernel, grid_spec=pltpu.Prefetch...  20.8 us
    pallas_call x2, Pallas kernels, qkv_call(): pl.pallas_call(qkv_kernel, grid_spec=pltpu.PrefetchScalarGridSpec(num_sca...  20.6 us
  transfers between devices with their start and end apart: 44, of which 15 were waited for; matrix products, arithmetic and copies ran while one was open for 5% of the time, Pallas kernels for 42%

profile of v2, /device:TPU:0, one launch (start us, length us, event | category | flops | bytes accessed | tf_op | source)
XLA Modules:
  0.0 876.8 jit_solution(17789674955818749692)
XLA Ops:
  18.4 38.8 %collective-permute-done.xa_ref = bf16[1024,1024]{1,0:T(8,128)(2,1)S(1)} collective-permute-done((bf16[1024,1024]{1,0:T(8,128)(2,1)}, bf16[1024,1024]{1,0:T(8,128)(2,1)S(1)}, u32[]{:S(2)}, u32[]{:S(2)}) %collective-permute-start) | collective-permute-done | bytes 2097184 | tf_op jit(solution)/shard_map/ppermute | solution.py:621
  59.5 13.4 %collective-permute-done.4 = s32[8,128]{1,0:T(8,128)S(1)} collective-permute-done((s32[8,128]{1,0:T(8,128)S(1)}, s32[8,128]{1,0:T(8,128)S(1)}, u32[]{:S(2)}, u32[]{:S(2)}) %collective-permute-start.4) | collective-permute-done | bytes 4128 | tf_op jit(solution)/shard_map/ppermute | solution.py:621
  83.7 28.9 %collective-permute-done.2.got_ref = bf16[576,1024]{1,0:T(8,128)(2,1)} collective-permute-done((bf16[576,1024]{1,0:T(8,128)(2,1)S(1)}, bf16[576,1024]{1,0:T(8,128)(2,1)}, u32[]{:S(2)}, u32[]{:S(2)}) %collective-permute-start.2) | collective-permute-done | bytes 1179680 | tf_op jit(solution)/shard_map/ppermute | solution.py:625
  117.0 10.3 %qkv.2 = (bf16[4096,1024]{1,0:T(8,128)(2,1)}, bf16[4096,256]{1,0:T(8,128)(2,1)}, bf16[4096,128]{1,0:T(8,128)(2,1)}, bf16[4096,128]{1,0:T(8,128)(2,1)}, bf16[4096...) custom-call(s32[1]{0:T(128)} %bitcast.sp_ref, bf16[1024,1024]{1,0:T(8,128)(2,1)} %bitcast.55, ...), custom_call_target="tpu_custom_call" | custom-call | flops 4294967296 | bytes 20971520 | tf_op jit(solution)/shard_map/qkv/pallas_call | solution.py:201
  127.3 10.3 %qkv.3 = (bf16[4096,1024]{1,0:T(8,128)(2,1)}, bf16[4096,256]{1,0:T(8,128)(2,1)}, bf16[4096,128]{1,0:T(8,128)(2,1)}, bf16[4096,128]{1,0:T(8,128)(2,1)}, bf16[4096...) custom-call(s32[1]{0:T(128)} %bitcast.sp_ref, ...), custom_call_target="tpu_custom_call", output_to_operand_aliasing={{0}: (7, {}), {1}: (8, {}), {2}: (9, {}), {3}: (10, {}), {4... | custom-call | flops 4294967296 | bytes 20971520 | tf_op jit(solution)/shard_map/qkv/pallas_call | solution.py:201
  137.6 46.4 %attn_fwd.3 = (bf16[4,1024,256]{2,1,0:T(8,128)(2,1)}, f32[2,8,4096]{2,1,0:T(8,128)}) custom-call(bf16[4096,256]{1,0:T(8,128)(2,1)} %get-tuple-element.89.q_ref, bf16[4096,128]{1,0:T(8,128)(2,1)} %get-tuple-element.90.k_ref, bf16[4096,128]{1,0:T(8,128)(2,1)} %get-tuple-element.91.v_ref), custom_call_target="tpu_custom_call" | custom-call | flops 24000000000 | bytes 8388608 | tf_op jit(solution)/shard_map/attn_fwd/pallas_call | solution.py:269
  187.7 46.3 %attn_fwd.2 = (bf16[4,1024,256]{2,1,0:T(8,128)(2,1)}, f32[2,8,4096]{2,1,0:T(8,128)}) custom-call(bf16[4096,256]{1,0:T(8,128)(2,1)} %get-tuple-element.85.q_ref, bf16[4096,128]{1,0:T(8,128)(2,1)} %get-tuple-element.86.k_ref, bf16[4096,128]{1,0:T(8,128)(2,1)} %get-tuple-element.87.v_ref), custom_call_target="tpu_custom_call" | custom-call | flops 24000000000 | bytes 8388608 | tf_op jit(solution)/shard_map/attn_fwd/pallas_call | solution.py:269
  250.3 33.1 %collective-permute-done.15.refs_9_ = bf16[384,1024]{1,0:T(8,128)(2,1)} collective-permute-done((bf16[384,1024]{1,0:T(8,128)(2,1)S(1)}, bf16[384,1024]{1,0:T(8,128)(2,1)}, u32[]{:S(2)}, u32[]{:S(2)}) %collective-permute-start.15) | collective-permute-done | bytes 786464 | tf_op jit(solution)/shard_map/ppermute | solution.py:621
  285.4 14.8 %collective-permute-done.9.refs_1_ = bf16[256,1536]{1,0:T(8,128)(2,1)} collective-permute-done((bf16[256,1536]{1,0:T(8,128)(2,1)}, bf16[256,1536]{1,0:T(8,128)(2,1)}, u32[]{:S(2)}, u32[]{:S(2)}) %collective-permute-start.9) | collective-permute-done | bytes 786464 | tf_op jit(solution)/shard_map/ppermute | solution.py:621
  301.5 14.6 %collective-permute-done.12.refs_5_ = bf16[256,1536]{1,0:T(8,128)(2,1)} collective-permute-done((bf16[256,1536]{1,0:T(8,128)(2,1)}, bf16[256,1536]{1,0:T(8,128)(2,1)}, u32[]{:S(2)}, u32[]{:S(2)}) %collective-permute-start.12) | collective-permute-done | bytes 786464 | tf_op jit(solution)/shard_map/ppermute | solution.py:621
  318.8 9.8 %oproj.1 = (bf16[1024,1024]{1,0:T(8,128)(2,1)}, bf16[1024,1024]{1,0:T(8,128)(2,1)}) custom-call(bf16[4,1024,256]{2,1,0:T(8,128)(2,1)} %all-to-all-done.1.a0_ref, bf16[4,1024,256]{2,1,0:T(8,128)(2,1)} %copy-done.11, bf16[2048,1024]{1,0:T(8,128)(2,1)} %all-gather.3.cloned.1.call-done.w_ref.wa_ref.wb_ref, bf16[1024,1024]{1,0:T(8,128)(2,1)} %bitcast.56, ...), custom_call_target="tpu_custom_call" | custom-call | flops 4294967296 | bytes 14680064 | tf_op jit(solution)/shard_map/oproj/pallas_call | solution.py:390
  337.8 14.2 %collective-permute-done.14.refs_7_ = bf16[256,1536]{1,0:T(8,128)(2,1)} collective-permute-done((bf16[256,1536]{1,0:T(8,128)(2,1)}, bf16[256,1536]{1,0:T(8,128)(2,1)}, u32[]{:S(2)}, u32[]{:S(2)}) %collective-permute-start.14) | collective-permute-done | bytes 786464 | tf_op jit(solution)/shard_map/ppermute | solution.py:625
  352.0 27.4 %mlp.2 = (bf16[1024,1536]{1,0:T(8,128)(2,1)}, bf16[1024,1536]{1,0:T(8,128)(2,1)}, bf16[1024,1536]{1,0:T(8,128)(2,1)}, f32[1024,1024]{1,0:T(8,128)}, f32[1024,1024]{1,0:T(8,128)}) custom-call(s32[1]{0:T(128)} %bitcast.10.chip_ref, bf16[1024,1024]{1,0:T(8,128)(2,1)} %get-tuple-element.95.u_ref.la_ref, bf16[1024,1024]{1,0:T(8,128)(2,1)} %bitcast.46, ...), custom_call_target="tpu_custom_call" | custom-call | flops 19327352832 | bytes 31457280 | tf_op jit(solution)/shard_map/mlp/pallas_call | solution.py:432
  379.4 27.5 %mlp.3 = (bf16[1024,1536]{1,0:T(8,128)(2,1)}, bf16[1024,1536]{1,0:T(8,128)(2,1)}, bf16[1024,1536]{1,0:T(8,128)(2,1)}, f32[1024,1024]{1,0:T(8,128)}, f32[1024,1024]{1,0:T(8,128)}) custom-call(s32[1]{0:T(128)} %bitcast.10.chip_ref, bf16[1024,1024]{1,0:T(8,128)(2,1)} %collective-permute-done.18.u_ref.lb_ref, ...), custom_call_target="tpu_custom_call" | custom-call | flops 19327352832 | bytes 31457280 | tf_op jit(solution)/shard_map/mlp/pallas_call | solution.py:432
  406.9 21.0 %dw.1 = f32[1024,3072]{1,0:T(8,128)} custom-call(bf16[1024,1024]{1,0:T(8,128)(2,1)} %get-tuple-element.95.u_ref.la_ref, bf16[1024,1024]{1,0:T(8,128)(2,1)} %collective-permute-done.18.u_ref.lb_ref, bf16[1024,1536]{1,0:T(8,128)(2,1)} %get-tuple-element.128.refs_0_, bf16[1024,1536]{1,0:T(8,128)(2,1)} %get-tuple-element.129.refs_1_, ...), custom_call_target="tpu_custom_call" | custom-call | flops 12884901888 | bytes 20971520 | tf_op jit(solution)/shard_map/dw/pallas_call | solution.py:461
  450.8 13.3 %dw_split.1 = (f32[2,384,1024]{2,1,0:T(8,128)}, f32[2,384,1024]{2,1,0:T(8,128)}) custom-call(s32[4]{0:T(128)} %pad_add_fusion.idx_ref, bf16[1024,1536]{1,0:T(8,128)(2,1)} %get-tuple-element.135.la_ref, bf16[1024,1536]{1,0:T(8,128)(2,1)} %get-tuple-element.136.lb_ref, bf16[1024,1024]{1,0:T(8,128)(2,1)} %bitcast.47, ...), custom_call_target="tpu_custom_call" | custom-call | flops 6442450944 | bytes 20971520 | tf_op jit(solution)/shard_map/dw_split/pallas_call | solution.py:487
  465.5 77.2 %collective-permute-done.23.h2_ref = bf16[1024,1024]{1,0:T(8,128)(2,1)} collective-permute-done((bf16[1024,1024]{1,0:T(8,128)(2,1)}, bf16[1024,1024]{1,0:T(8,128)(2,1)}, u32[]{:S(2)}, u32[]{:S(2)}) %collective-permute-start.23) | collective-permute-done | bytes 2097184 | tf_op jit(solution)/shard_map/ppermute | solution.py:621
  542.7 42.7 %collective-permute-done.33 = f32[2,384,1024]{2,1,0:T(8,128)S(1)} collective-permute-done((f32[2,384,1024]{2,1,0:T(8,128)}, f32[2,384,1024]{2,1,0:T(8,128)S(1)}, u32[]{:S(2)}, u32[]{:S(2)}) %collective-permute-start.33) | collective-permute-done | bytes 3145760 | tf_op jit(solution)/shard_map/ppermute | solution.py:625
  590.8 17.9 %dout.1 = (bf16[4096,256]{1,0:T(8,128)(2,1)}, bf16[4096,256]{1,0:T(8,128)(2,1)}, f32[2,256,1024]{2,1,0:T(8,128)}) custom-call(s32[1]{0:T(128)} %bitcast.sp_ref, bf16[1024,1024]{1,0:T(8,128)(2,1)} %get-tuple-element.141.h0_ref, bf16[1024,1024]{1,0:T(8,128)(2,1)} %collective-permute-done.22.h1_ref, bf16[1024,1024]{1,0:T(8,128)(2,1)} %collective-permute-done.23.h2_ref, ...), custom_call_target="tpu_custom_call" | custom-call | flops 8589934592 | bytes 20971520 | tf_op jit(solution)/shard_map/dout/pallas_call | solution.py:542
  608.7 67.3 %attn_bwd.3 = (bf16[1024,512]{1,0:T(8,128)(2,1)}, bf16[1024,512]{1,0:T(8,128)(2,1)}, bf16[1024,512]{1,0:T(8,128)(2,1)}, bf16[1024,512]{1,0:T(8,128)(2,1)}) custom-call(s32[1]{0:T(128)} %bitcast.sp_ref, bf16[4096,256]{1,0:T(8,128)(2,1)} %get-tuple-element.85.q_ref, bf16[4096,128]{1,0:T(8,128)(2,1)} %get-tuple-element.86.k_ref, ...), custom_call_target="tpu_custom_call" | custom-call | flops 60000002048 | bytes 16777216 | tf_op jit(solution)/shard_map/attn_bwd/pallas_call | solution.py:353
  689.8 66.7 %attn_bwd.2 = (bf16[1024,512]{1,0:T(8,128)(2,1)}, bf16[1024,512]{1,0:T(8,128)(2,1)}, bf16[1024,512]{1,0:T(8,128)(2,1)}, bf16[1024,512]{1,0:T(8,128)(2,1)}) custom-call(s32[1]{0:T(128)} %bitcast.sp_ref, bf16[4096,256]{1,0:T(8,128)(2,1)} %get-tuple-element.89.q_ref, bf16[4096,128]{1,0:T(8,128)(2,1)} %get-tuple-element.90.k_ref, ...), custom_call_target="tpu_custom_call" | custom-call | flops 60000002048 | bytes 16777216 | tf_op jit(solution)/shard_map/attn_bwd/pallas_call | solution.py:353
  792.2 29.6 %collective-permute-done.26.refs_2_ = bf16[1024,512]{1,0:T(8,128)(2,1)} collective-permute-done((bf16[1024,512]{1,0:T(8,128)(2,1)}, bf16[1024,512]{1,0:T(8,128)(2,1)}, u32[]{:S(2)}, u32[]{:S(2)}) %collective-permute-start.26) | collective-permute-done | bytes 1048608 | tf_op jit(solution)/shard_map/ppermute | solution.py:621
  821.8 21.3 %collective-permute-done.27.refs_3_ = bf16[1024,512]{1,0:T(8,128)(2,1)} collective-permute-done((bf16[1024,512]{1,0:T(8,128)(2,1)}, bf16[1024,512]{1,0:T(8,128)(2,1)}, u32[]{:S(2)}, u32[]{:S(2)}) %collective-permute-start.27) | collective-permute-done | bytes 1048608 | tf_op jit(solution)/shard_map/ppermute | solution.py:621
  843.2 11.7 %dx.1 = (bf16[1024,1024]{1,0:T(8,128)(2,1)}, f32[1,1024]{1,0:T(1,128)}) custom-call(s32[1]{0:T(128)} %bitcast.sp_ref, bf16[1024,512]{1,0:T(8,128)(2,1)} %get-tuple-element.108.refs_0_, bf16[1024,512]{1,0:T(8,128)(2,1)} %collective-permute-done.25.refs_1_, bf16[1024,512]{1,0:T(8,128)(2,1)} %collective-permute-done.26.refs_2_, ...), custom_call_target="tpu_custom_call" | custom-call | flops 4294967296 | bytes 16777216 | tf_op jit(solution)/shard_map/dx/pallas_call | solution.py:593
  (147 shorter events, 157.9 us)
Async XLA Ops:
  14.4 58.5 %all-to-all-start = ((bf16[4,144,1024]{2,1,0:T(8,128)(2,1)}), bf16[4,144,1024]{2,1,0:T(8,128)(2,1)S(1)}, u32[]{:S(2)}, u32[]{:S(2)}) async-start(bf16[4,144,1024]{2,1,0:T(8,128)(2,1)} %bitcast.58), calls=%async_computation | async-start | bytes 2359296 | tf_op jit(solution)/shard_map/all_to_all | solution.py:613
  17.9 300.9 %all-gather.3.cloned.1.call-start = ((), (), s32[]{:S(2)}) async-start(), calls=%async_computation.7 | async-start | bytes 4718592 | tf_op jit(solution)/shard_map/all_gather | solution.py:609
  18.0 99.0 %collective-permute-start.6 = (bf16[1024,1024]{1,0:T(8,128)(2,1)}, bf16[1024,1024]{1,0:T(8,128)(2,1)}, u32[]{:S(2)}, u32[]{:S(2)}) collective-permute-start(bf16[1024,1024]{1,0:T(8,128)(2,1)} %bitcast.54), channel_id=1, source_target_pairs={{0,1},{1,0},{2,3},{3,2},{4,5},{5,4},{6,7},{7,6}} | collective-permute-start | bytes 6291464 | tf_op jit(solution)/shard_map/ppermute | solution.py:621
  57.2 70.1 %collective-permute-start.1 = (bf16[1024,1024]{1,0:T(8,128)(2,1)S(1)}, bf16[1024,1024]{1,0:T(8,128)(2,1)}, u32[]{:S(2)}, u32[]{:S(2)}) collective-permute-start(bf16[1024,1024]{1,0:T(8,128)(2,1)S(1)} %collective-permute-done.xa_ref), channel_id=1, source_target_pairs={{0,1},{1,0},{2,3},{3,2},{4,5},{5,4},{6,7},{7,6}} | collective-permute-start | bytes 6291464 | tf_op jit(solution)/shard_map/ppermute | solution.py:621
  235.4 83.4 %all-to-all-start.1 = ((bf16[4,1024,256]{2,1,0:T(8,128)(2,1)}), bf16[4,1024,256]{2,1,0:T(8,128)(2,1)}, u32[]{:S(2)}, u32[]{:S(2)}) async-start(bf16[4,1024,256]{2,1,0:T(8,128)(2,1)} %get-tuple-element.88.o0_ref), calls=%async_computation.1 | async-start | bytes 4194304 | tf_op jit(solution)/shard_map/all_to_all | solution.py:613
  239.9 533.2 %reduce-scatter.2.cloned.1.call-start = ((), (), s32[]{:S(2)}) async-start(), calls=%async_computation.9 | async-start | bytes 15728640 | tf_op jit(solution)/shard_map/reduce_scatter | solution.py:641
  247.6 52.6 %collective-permute-start.9 = (bf16[256,1536]{1,0:T(8,128)(2,1)}, bf16[256,1536]{1,0:T(8,128)(2,1)}, u32[]{:S(2)}, u32[]{:S(2)}) collective-permute-start(bf16[256,1536]{1,0:T(8,128)(2,1)} %get-tuple-element.100.refs_0_), channel_id=1, source_target_pairs={{0,2},{1,3},{2,0},{3,1},{4,6},{5,7},{6,4},{7,5}} | collective-permute-start | bytes 2359304 | tf_op jit(solution)/shard_map/ppermute | solution.py:621
  248.4 67.8 %collective-permute-start.12 = (bf16[256,1536]{1,0:T(8,128)(2,1)}, bf16[256,1536]{1,0:T(8,128)(2,1)}, u32[]{:S(2)}, u32[]{:S(2)}) collective-permute-start(bf16[256,1536]{1,0:T(8,128)(2,1)} %get-tuple-element.101.refs_4_), channel_id=1, source_target_pairs={{0,2},{1,3},{2,0},{3,1},{4,6},{5,7},{6,4},{7,5}} | collective-permute-start | bytes 2359304 | tf_op jit(solution)/shard_map/ppermute | solution.py:621
  249.6 79.0 %collective-permute-start.10 = (bf16[256,1536]{1,0:T(8,128)(2,1)}, bf16[256,1536]{1,0:T(8,128)(2,1)}, u32[]{:S(2)}, u32[]{:S(2)}) collective-permute-start(bf16[256,1536]{1,0:T(8,128)(2,1)} %get-tuple-element.100.refs_0_), channel_id=1, source_target_pairs={{0,4},{4,0},{1,5},{5,1},{2,6},{6,2},{3,7},{7,3}} | collective-permute-start | bytes 2359304 | tf_op jit(solution)/shard_map/ppermute | solution.py:625
  328.6 50.7 %collective-permute-start.19 = (bf16[1024,1024]{1,0:T(8,128)(2,1)S(1)}, bf16[1024,1024]{1,0:T(8,128)(2,1)}, u32[]{:S(2)}, u32[]{:S(2)}) collective-permute-start(bf16[1024,1024]{1,0:T(8,128)(2,1)S(1)} %bitcast.48), channel_id=1, source_target_pairs={{0,1},{1,0},{2,3},{3,2},{4,5},{5,4},{6,7},{7,6}} | collective-permute-start | bytes 6291464 | tf_op jit(solution)/shard_map/ppermute | solution.py:621
  328.7 50.7 %collective-permute-start.18 = (bf16[1024,1024]{1,0:T(8,128)(2,1)}, bf16[1024,1024]{1,0:T(8,128)(2,1)}, u32[]{:S(2)}, u32[]{:S(2)}) collective-permute-start(bf16[1024,1024]{1,0:T(8,128)(2,1)} %get-tuple-element.95.u_ref.la_ref), channel_id=1, source_target_pairs={{0,1},{1,0},{2,3},{3,2},{4,5},{5,4},{6,7},{7,6}} | collective-permute-start | bytes 6291464 | tf_op jit(solution)/shard_map/ppermute | solution.py:621
  427.9 355.2 %all-gather.5.cloned.1.call-start = ((), (), s32[]{:S(2)}) async-start(), calls=%async_computation.8 | async-start | bytes 9437184 | tf_op jit(solution)/shard_map/all_gather | solution.py:609
  449.1 93.6 %collective-permute-start.23 = (bf16[1024,1024]{1,0:T(8,128)(2,1)}, bf16[1024,1024]{1,0:T(8,128)(2,1)}, u32[]{:S(2)}, u32[]{:S(2)}) collective-permute-start(bf16[1024,1024]{1,0:T(8,128)(2,1)} %get-tuple-element.141.h0_ref), channel_id=1, source_target_pairs={{0,2},{1,3},{2,0},{3,1},{4,6},{5,7},{6,4},{7,5}} | collective-permute-start | bytes 6291464 | tf_op jit(solution)/shard_map/ppermute | solution.py:621
  464.1 121.3 %collective-permute-start.33 = (f32[2,384,1024]{2,1,0:T(8,128)}, f32[2,384,1024]{2,1,0:T(8,128)S(1)}, u32[]{:S(2)}, u32[]{:S(2)}) collective-permute-start(f32[2,384,1024]{2,1,0:T(8,128)} %get-tuple-element.138), channel_id=1, source_target_pairs={{0,4},{4,0},{1,5},{5,1},{2,6},{6,2},{3,7},{7,3}} | collective-permute-start | bytes 9437192 | tf_op jit(solution)/shard_map/ppermute | solution.py:625
  465.5 125.4 %collective-permute-start.22 = (bf16[1024,1024]{1,0:T(8,128)(2,1)}, bf16[1024,1024]{1,0:T(8,128)(2,1)}, u32[]{:S(2)}, u32[]{:S(2)}) collective-permute-start(bf16[1024,1024]{1,0:T(8,128)(2,1)} %get-tuple-element.141.h0_ref), channel_id=1, source_target_pairs={{0,1},{1,0},{2,3},{3,2},{4,5},{5,4},{6,7},{7,6}} | collective-permute-start | bytes 6291464 | tf_op jit(solution)/shard_map/ppermute | solution.py:621
  589.4 183.7 %collective-permute-start.34 = (f32[384,1024]{1,0:T(8,128)}, f32[384,1024]{1,0:T(8,128)}, u32[]{:S(2)}, u32[]{:S(2)}) collective-permute-start(f32[384,1024]{1,0:T(8,128)} %fusion.12), channel_id=1, source_target_pairs={{0,2},{1,3},{2,0},{3,1},{4,6},{5,7},{6,4},{7,5}} | collective-permute-start | bytes 4718600 | tf_op jit(solution)/shard_map/ppermute | solution.py:621
  676.0 99.0 %collective-permute-start.28 = (bf16[1024,512]{1,0:T(8,128)(2,1)}, bf16[1024,512]{1,0:T(8,128)(2,1)}, u32[]{:S(2)}, u32[]{:S(2)}) collective-permute-start(bf16[1024,512]{1,0:T(8,128)(2,1)} %get-tuple-element.116.refs_1_), channel_id=1, source_target_pairs={{0,1},{1,0},{2,3},{3,2},{4,5},{5,4},{6,7},{7,6}} | collective-permute-start | bytes 3145736 | tf_op jit(solution)/shard_map/ppermute | solution.py:621
  676.0 101.7 %collective-permute-start.29 = (bf16[1024,512]{1,0:T(8,128)(2,1)}, bf16[1024,512]{1,0:T(8,128)(2,1)}, u32[]{:S(2)}, u32[]{:S(2)}) collective-permute-start(bf16[1024,512]{1,0:T(8,128)(2,1)} %get-tuple-element.117.refs_2_), channel_id=1, source_target_pairs={{0,2},{1,3},{2,0},{3,1},{4,6},{5,7},{6,4},{7,5}} | collective-permute-start | bytes 3145736 | tf_op jit(solution)/shard_map/ppermute | solution.py:621
  676.2 103.0 %collective-permute-start.30 = (bf16[1024,512]{1,0:T(8,128)(2,1)}, bf16[1024,512]{1,0:T(8,128)(2,1)}, u32[]{:S(2)}, u32[]{:S(2)}) collective-permute-start(bf16[1024,512]{1,0:T(8,128)(2,1)} %get-tuple-element.118.refs_3_), channel_id=1, source_target_pairs={{0,3},{1,2},{2,1},{3,0},{4,7},{5,6},{6,5},{7,4}} | collective-permute-start | bytes 3145736 | tf_op jit(solution)/shard_map/ppermute | solution.py:621
  687.2 81.4 %all-to-all-start.3 = ((f32[8,128,512]{2,1,0:T(8,128)}), f32[8,128,512]{2,1,0:T(8,128)S(1)}, u32[]{:S(2)}, u32[]{:S(2)}) async-start(f32[8,128,512]{2,1,0:T(8,128)} %bitcast.52), calls=%async_computation.3 | async-start | bytes 4194304 | tf_op jit(solution)/shard_map/all_to_all | solution.py:617
  770.0 88.6 %all-to-all-start.4 = ((f32[8,128,512]{2,1,0:T(8,128)}), f32[8,128,512]{2,1,0:T(8,128)}, u32[]{:S(2)}, u32[]{:S(2)}) async-start(f32[8,128,512]{2,1,0:T(8,128)} %bitcast.51), calls=%async_computation.4 | async-start | bytes 4194304 | tf_op jit(solution)/shard_map/all_to_all | solution.py:617
  775.0 68.2 %collective-permute-start.27 = (bf16[1024,512]{1,0:T(8,128)(2,1)}, bf16[1024,512]{1,0:T(8,128)(2,1)}, u32[]{:S(2)}, u32[]{:S(2)}) collective-permute-start(bf16[1024,512]{1,0:T(8,128)(2,1)} %get-tuple-element.111.refs_3_), channel_id=1, source_target_pairs={{0,3},{1,2},{2,1},{3,0},{4,7},{5,6},{6,5},{7,4}} | collective-permute-start | bytes 3145736 | tf_op jit(solution)/shard_map/ppermute | solution.py:621
  777.7 78.5 %collective-permute-start.31 = (f32[256,1024]{1,0:T(8,128)}, f32[256,1024]{1,0:T(8,128)}, u32[]{:S(2)}, u32[]{:S(2)}) collective-permute-start(f32[256,1024]{1,0:T(8,128)} %dynamic-slice_bitcast_fusion), channel_id=1, source_target_pairs={{0,4},{4,0},{1,5},{5,1},{2,6},{6,2},{3,7},{7,3}} | collective-permute-start | bytes 3145736 | tf_op jit(solution)/shard_map/ppermute | solution.py:625
  779.2 86.4 %collective-permute-start.32 = (f32[128,3072]{1,0:T(8,128)}, f32[128,3072]{1,0:T(8,128)}, u32[]{:S(2)}, u32[]{:S(2)}) collective-permute-start(f32[128,3072]{1,0:T(8,128)} %constant_dynamic-slice_fusion), channel_id=1, source_target_pairs={{0,1},{1,0},{2,3},{3,2},{4,5},{5,4},{6,7},{7,6}} | collective-permute-start | bytes 4718600 | tf_op jit(solution)/shard_map/ppermute | solution.py:621
  (40 other events, 811.7 us)
Sparse Core Ops, SparseCore 0:
  59.6 45.3 all-gather.2
  428.0 176.4 reduce-scatter.1
  607.0 59.3 all-gather.4

commit v3 on v2

--- a/solution.py
+++ b/solution.py
@@ -49,6 +49,39 @@
     return pl.BlockSpec(shape, lambda *_: tuple(0 for _ in shape))
 
 
+def row_block(width):
+    return pl.BlockSpec((PAIR, width), lambda i, *_: (i, 0))
+
+
+def pick(values, index):
+    return lax.dynamic_index_in_dim(values, index, 0, keepdims=False)
+
+
+def row_mean(values):
+    return jnp.mean(values, axis=-1, keepdims=True)
+
+
+def normalize(values):
+    inv_rms = lax.rsqrt(row_mean(values * values) + NORM_EPS)
+    return values * inv_rms, inv_rms
+
+
+def normalize_grad(d_normed, normed, inv_rms):
+    return inv_rms * (d_normed - normed * row_mean(d_normed * normed))
+
+
+def accumulate(ref, value):
+    @pl.when(pl.program_id(0) == 0)
+    def _():
+        ref[...] = jnp.zeros_like(ref)
+
+    ref[...] += value
+
+
+def col_sum(values):
+    return jnp.sum(values, axis=0, keepdims=True)
+
+
 def params(**kw):
     return pltpu.CompilerParams(vmem_limit_bytes=VMEM_LIMIT, dimension_semantics=('arbitrary',), **kw)
 
@@ -174,9 +207,7 @@
     def _():
         x_scr[...] = xb_ref[...]
 
-    x32 = x_scr[...].astype(jnp.float32)
-    inv_rms = lax.rsqrt(jnp.mean(x32 * x32, axis=-1, keepdims=True) + NORM_EPS)
-    u = (x32 * inv_rms * g_ref[...].astype(jnp.float32)).astype(jnp.bfloat16)
+    u = (normalize(x_scr[...].astype(jnp.float32))[0] * g_ref[...].astype(jnp.float32)).astype(jnp.bfloat16)
     u_ref[...] = u
     cos, sin = cos_ref[...], sin_ref[...]
 
@@ -192,8 +223,8 @@
 
 
 def qkv_call(sp_arr, xa, xb, first, gain, w_own, cos, sin, prev):
-    place = lambda width: pl.BlockSpec((BLK, width), lambda i, s: ((s[0] ^ (first + i // 2)) * 2 + i % 2, 0))
-    local = lambda width: pl.BlockSpec((BLK, width), lambda i, s: (first * 2 + i, 0))
+    place = lambda width: pl.BlockSpec((BLK, width), lambda i, s: ((s[0] ^ (first + i // PAIRS)) * PAIRS + i % PAIRS, 0))
+    local = lambda width: pl.BlockSpec((BLK, width), lambda i, s: (first * PAIRS + i, 0))
     out = lambda width: jax.ShapeDtypeStruct((SEQ, width), jnp.bfloat16)
     xa_spec = pl.BlockSpec((BLK, DIM), lambda i, s: (jnp.minimum(i, 1), 0))
     xb_spec = pl.BlockSpec((BLK, DIM), lambda i, s: (jnp.maximum(i - 2, 0), 0))
@@ -378,14 +409,12 @@
         total += dot_nn(a, w_ref[g * DIM:(g + 1) * DIM, :])
     h = total.astype(jnp.bfloat16)
     h_ref[...] = h
-    h32 = h.astype(jnp.float32)
-    inv_rms = lax.rsqrt(jnp.mean(h32 * h32, axis=-1, keepdims=True) + NORM_EPS)
-    u_ref[...] = (h32 * inv_rms * g_ref[...].astype(jnp.float32)).astype(jnp.bfloat16)
+    u_ref[...] = (normalize(h.astype(jnp.float32))[0] * g_ref[...].astype(jnp.float32)).astype(jnp.bfloat16)
 
 
 def oproj_call(a0, a1, wo, x, gain):
     blk = PAIR
-    row = pl.BlockSpec((blk, DIM), lambda i: (i, 0))
+    row = row_block(DIM)
     part = pl.BlockSpec((4, blk, PAIR), lambda i: (0, i, 0))
     return pl.pallas_call(
         oproj_kernel,
@@ -426,7 +455,7 @@
 
 
 def mlp_call(chip_arr, u, dy, w1, w3, w2):
-    row = lambda width: pl.BlockSpec((PAIR, width), lambda i, s: (i, 0))
+    row = row_block
     pieces = [*w1, *w3, *w2]
     bf16, f32 = jnp.bfloat16, jnp.float32
     return pl.pallas_call(
@@ -571,22 +600,38 @@
 def dx_kernel(sp_ref, *refs):
     w_ref, du_ref, x_ref, dr_ref, g_ref, dx_ref, dg_ref = refs[SP:]
     d_u = du_ref[...] + du_sum(sp_ref, refs[:SP], w_ref)
-    x32 = x_ref[...].astype(jnp.float32)
-    inv_rms = lax.rsqrt(jnp.mean(x32 * x32, axis=-1, keepdims=True) + NORM_EPS)
-    normed = x32 * inv_rms
-    d_normed = d_u * g_ref[...].astype(jnp.float32)
-    grad_in = inv_rms * (d_normed - normed * jnp.mean(d_normed * normed, axis=-1, keepdims=True))
+    normed, inv_rms = normalize(x_ref[...].astype(jnp.float32))
+    grad_in = normalize_grad(d_u * g_ref[...].astype(jnp.float32), normed, inv_rms)
     dx_ref[...] = (dr_ref[...] + grad_in).astype(jnp.bfloat16)
-
-    @pl.when(pl.program_id(0) == 0)
-    def _():
-        dg_ref[...] = jnp.zeros_like(dg_ref)
-
-    dg_ref[...] += jnp.sum(d_u * normed, axis=0, keepdims=True)
+    accumulate(dg_ref, col_sum(d_u * normed))
+
+
+def dh_kernel(da_ref, db_ref, h_ref, dy_ref, g_ref, dr_ref, dh_ref, dg_ref):
+    d_u = da_ref[...] + db_ref[...]
+    normed, inv_rms = normalize(h_ref[...].astype(jnp.float32))
+    d_resid = dy_ref[...].astype(jnp.float32) + normalize_grad(d_u * g_ref[...].astype(jnp.float32), normed, inv_rms)
+    dr_ref[...] = d_resid
+    dh_ref[...] = d_resid.astype(jnp.bfloat16)
+    accumulate(dg_ref, col_sum(d_u * normed))
+
+
+def dh_call(d_a, d_b, h, dy, gain):
+    row = row_block(DIM)
+    out = lambda rows, dtype: jax.ShapeDtypeStruct((rows, DIM), dtype)
+    return pl.pallas_call(
+        dh_kernel,
+        grid=(TOK // PAIR,),
+        in_specs=[row] * SP + [fixed(gain.shape)],
+        out_specs=[row, row, fixed(gain.shape)],
+        out_shape=[out(TOK, jnp.float32), out(TOK, jnp.bfloat16), out(gain.shape[0], jnp.float32)],
+        compiler_params=params(),
+        cost_estimate=cost(TINY, 18),
+        name='dh',
+    )(d_a, d_b, h, dy, gain)
 
 
 def dx_call(sp_arr, group, pieces, w_all, *rest):
-    row = lambda width: pl.BlockSpec((PAIR, width), lambda i, s: (i, 0))
+    row = row_block
     one = fixed((1, DIM))
     du_shape = jax.ShapeDtypeStruct((TOK, DIM), jnp.float32)
     last = len(rest) > 0
@@ -627,14 +672,16 @@
 
 def gather_chip_then_core(value):
     far = from_sp(value, 2)
-    return value, from_sp(value, 1), far, from_sp(far, 1)
-
-
-def gather_chips(value):
+    near = from_sp(value, 1)
+    return value, near, far, from_sp(far, 1)
+
+
+def gather_chips(value, by_x):
     across = from_dp(value)
     along = from_sp(value, 2)
-    far = from_dp(along)
-    return value, along, across, far
+    if by_x:
+        return value, along, across, from_dp(along)
+    return value, along, across, from_sp(across, 2)
 
 
 def reduce_chips(part):
@@ -662,7 +709,7 @@
     pos_all = jnp.concatenate(pos).reshape(SEQ)
     w1_rows, w3_rows = join_call(core_arr, (a1, from_sp(b1, 1)), (a3, from_sp(b3, 1)))
     wo_full = gather_full(w_out)
-    w2, w1, w3 = (gather_chips(t) for t in (w_down, w1_rows, w3_rows))
+    w1, w3, w2 = gather_chips(w1_rows, True), gather_chips(w3_rows, True), gather_chips(w_down, False)
     w_all = gather_full(w_cols)
     dy_pair = from_sp(d_layer, 1)
 
@@ -684,15 +731,11 @@
     u_pair = from_sp(u_mlp, 1)
     z_a, da_a, dc_a, y_a, d_a = mlp_call(chip_arr, u_mlp, d_layer, w1, w3, w2)
     z_b, da_b, dc_b, y_b, d_b = mlp_call(chip_arr, u_pair, dy_pair, w1, w3, w2)
-    d_umlp = d_a + from_sp(d_b, 1)
-    h32 = residual.astype(f32)
-    layer_out = (h32 + (y_a + from_sp(y_b, 1))).astype(bf16)
-    inv_rms2 = lax.rsqrt(jnp.mean(h32 * h32, axis=-1, keepdims=True) + NORM_EPS)
-    normed2 = h32 * inv_rms2
-    d_normed2 = d_umlp * gain2.astype(f32)
-    d_gain2 = jnp.sum(d_umlp * normed2, axis=0)
-    d_resid = d_layer.astype(f32) + inv_rms2 * (d_normed2 - normed2 * jnp.mean(d_normed2 * normed2, axis=-1, keepdims=True))
-    dhs = gather_chip_then_core(d_resid.astype(bf16))
+    d_got = from_sp(d_b, 1)
+    layout_parts = y_a + from_sp(y_b, 1)
+    layer_out = (residual.astype(f32) + layout_parts).astype(bf16)
+    d_resid, dh, d_gain2 = dh_call(d_a, d_got, residual, d_layer, gain2)
+    dhs = gather_chip_then_core(dh)
     order = jnp.stack([chip ^ 3, chip ^ 2, chip ^ 1, chip]).astype(jnp.int32)
     down_send, down_keep = dw_split_call(order, z_a, z_b, d_layer, dy_pair)
     down_got = from_dp(down_send)
@@ -712,7 +755,7 @@
     part1 = dw_qkv_call(u_all, d1).reshape(8, HEAD_DIM, GRP)
     part1, _ = lax.optimization_barrier((part1, dw0))
     dw1 = swap_all(part1)
-    grad_w_out = lax.dynamic_index_in_dim(dwo, dp, 0, keepdims=False) + from_dp(lax.dynamic_index_in_dim(dwo, 1 - dp, 0, keepdims=False))
+    grad_w_out = pick(dwo, dp) + from_dp(pick(dwo, 1 - dp))
     part, _ = lax.optimization_barrier((part, part1))
     send = lax.dynamic_slice(part, ((1 - core) * HEAD_DIM, 0), (HEAD_DIM, 2 * HALF))
     grad_w_gate, grad_w_up = unpack_cols_call(core_arr, part, from_sp(send, 1))

time: 886 us -> 874 us (0.986)
  waiting for transfers between devices: 344 us -> 334 us
    pallas_call x0 -> x1, Pallas kernels: none -> 9 us  [dh_call(): pl.pallas_call(dh_kernel, grid=(TOK // PAIR,), in_specs=[row] * SP + [fix...]
    ppermute x26 -> x27, waiting for transfers between devices: 249 us -> 244 us  [from_sp(): return lax.ppermute(value, 'sp', [(s, s ^ bits) for s in range(SP)])]
    ppermute x9 -> x8, waiting for transfers between devices: 94.4 us -> 89.3 us  [from_dp(): return lax.ppermute(value, 'dp', [(0, 1), (1, 0)])]
    ppermute x26 -> x27, starting transfers between devices: 18.9 us -> 19.2 us  [from_sp(): return lax.ppermute(value, 'sp', [(s, s ^ bits) for s in range(SP)])]
  transfers between devices with their start and end apart: 44 -> 44, of which waited for: 15 -> 15; matrix products, arithmetic and copies ran while one was open for 5% -> 4% of each run, Pallas kernels for 42% -> 44%
where the time goes in v3:
time: 874 us; the launch traced here: 865 us
  Pallas kernels  429 us (49%)
  waiting for transfers between devices  334 us (38%)
  starting transfers between devices  48.6 us (6%)
  other arithmetic  27.4 us (3%)
  between operations  14.2 us (2%)
  local copies, waits for them, and re-layouts  11.7 us (1%)
    ppermute x27, waiting for transfers between devices, from_sp(): return lax.ppermute(value, 'sp', [(s, s ^ bits) for s in range(SP)])  244 us
    pallas_call x2, Pallas kernels, bwd_call(): pl.pallas_call(bwd_kernel, grid_spec=pltpu.PrefetchScalarGridSpec(num_sca...  133 us
    pallas_call x2, Pallas kernels, fwd_call(): pl.pallas_call(fwd_kernel, grid=(SEQ // BLK,), in_specs=[pl.BlockSpec((BL...  92.7 us
    ppermute x8, waiting for transfers between devices, from_dp(): return lax.ppermute(value, 'dp', [(0, 1), (1, 0)])  89.3 us
    pallas_call x2, Pallas kernels, mlp_call(): pl.pallas_call(mlp_kernel, grid_spec=pltpu.PrefetchScalarGridSpec(num_sca...  55.1 us
    pallas_call x2, Pallas kernels, dx_call(): pl.pallas_call(dx_kernel if last else du_kernel, grid_spec=pltpu.Prefetch...  20.8 us
    pallas_call x1, Pallas kernels, dw_call(): pl.pallas_call(dw_kernel, grid=(4,), in_specs=[left, left] + [right] * le...  20.6 us
    pallas_call x2, Pallas kernels, qkv_call(): pl.pallas_call(qkv_kernel, grid_spec=pltpu.PrefetchScalarGridSpec(num_sca...  20.6 us
  transfers between devices with their start and end apart: 44, of which 15 were waited for; matrix products, arithmetic and copies ran while one was open for 4% of the time, Pallas kernels for 44%

profile of v3, /device:TPU:0, one launch (start us, length us, event | category | flops | bytes accessed | tf_op | source)
XLA Modules:
  0.0 865.3 jit_solution(8839028356534847379)
XLA Ops:
  18.4 38.8 %collective-permute-done.xa_ref = bf16[1024,1024]{1,0:T(8,128)(2,1)S(1)} collective-permute-done((bf16[1024,1024]{1,0:T(8,128)(2,1)}, bf16[1024,1024]{1,0:T(8,128)(2,1)S(1)}, u32[]{:S(2)}, u32[]{:S(2)}) %collective-permute-start) | collective-permute-done | bytes 2097184 | tf_op jit(solution)/shard_map/ppermute | solution.py:666
  59.5 13.4 %collective-permute-done.4 = s32[8,128]{1,0:T(8,128)S(1)} collective-permute-done((s32[8,128]{1,0:T(8,128)S(1)}, s32[8,128]{1,0:T(8,128)S(1)}, u32[]{:S(2)}, u32[]{:S(2)}) %collective-permute-start.4) | collective-permute-done | bytes 4128 | tf_op jit(solution)/shard_map/ppermute | solution.py:666
  83.7 28.9 %collective-permute-done.2.got_ref = bf16[576,1024]{1,0:T(8,128)(2,1)} collective-permute-done((bf16[576,1024]{1,0:T(8,128)(2,1)S(1)}, bf16[576,1024]{1,0:T(8,128)(2,1)}, u32[]{:S(2)}, u32[]{:S(2)}) %collective-permute-start.2) | collective-permute-done | bytes 1179680 | tf_op jit(solution)/shard_map/ppermute | solution.py:670
  117.0 10.3 %qkv.2 = (bf16[4096,1024]{1,0:T(8,128)(2,1)}, bf16[4096,256]{1,0:T(8,128)(2,1)}, bf16[4096,128]{1,0:T(8,128)(2,1)}, bf16[4096,128]{1,0:T(8,128)(2,1)}, bf16[4096...) custom-call(s32[1]{0:T(128)} %bitcast.sp_ref, bf16[1024,1024]{1,0:T(8,128)(2,1)} %bitcast.55, ...), custom_call_target="tpu_custom_call" | custom-call | flops 4294967296 | bytes 20971520 | tf_op jit(solution)/shard_map/qkv/pallas_call | solution.py:232
  127.3 10.3 %qkv.3 = (bf16[4096,1024]{1,0:T(8,128)(2,1)}, bf16[4096,256]{1,0:T(8,128)(2,1)}, bf16[4096,128]{1,0:T(8,128)(2,1)}, bf16[4096,128]{1,0:T(8,128)(2,1)}, bf16[4096...) custom-call(s32[1]{0:T(128)} %bitcast.sp_ref, ...), custom_call_target="tpu_custom_call", output_to_operand_aliasing={{0}: (7, {}), {1}: (8, {}), {2}: (9, {}), {3}: (10, {}), {4... | custom-call | flops 4294967296 | bytes 20971520 | tf_op jit(solution)/shard_map/qkv/pallas_call | solution.py:232
  137.6 46.4 %attn_fwd.3 = (bf16[4,1024,256]{2,1,0:T(8,128)(2,1)}, f32[2,8,4096]{2,1,0:T(8,128)}) custom-call(bf16[4096,256]{1,0:T(8,128)(2,1)} %get-tuple-element.92.q_ref, bf16[4096,128]{1,0:T(8,128)(2,1)} %get-tuple-element.93.k_ref, bf16[4096,128]{1,0:T(8,128)(2,1)} %get-tuple-element.94.v_ref), custom_call_target="tpu_custom_call" | custom-call | flops 24000000000 | bytes 8388608 | tf_op jit(solution)/shard_map/attn_fwd/pallas_call | solution.py:300
  187.7 46.3 %attn_fwd.2 = (bf16[4,1024,256]{2,1,0:T(8,128)(2,1)}, f32[2,8,4096]{2,1,0:T(8,128)}) custom-call(bf16[4096,256]{1,0:T(8,128)(2,1)} %get-tuple-element.88.q_ref, bf16[4096,128]{1,0:T(8,128)(2,1)} %get-tuple-element.89.k_ref, bf16[4096,128]{1,0:T(8,128)(2,1)} %get-tuple-element.90.v_ref), custom_call_target="tpu_custom_call" | custom-call | flops 24000000000 | bytes 8388608 | tf_op jit(solution)/shard_map/attn_fwd/pallas_call | solution.py:300
  250.3 10.7 %collective-permute-done.16.refs_10_ = bf16[384,1024]{1,0:T(8,128)(2,1)} collective-permute-done((bf16[384,1024]{1,0:T(8,128)(2,1)S(1)}, bf16[384,1024]{1,0:T(8,128)(2,1)}, u32[]{:S(2)}, u32[]{:S(2)}) %collective-permute-start.16) | collective-permute-done | bytes 786464 | tf_op jit(solution)/shard_map/ppermute | solution.py:670
  262.3 20.9 %collective-permute-done.15.refs_9_ = bf16[384,1024]{1,0:T(8,128)(2,1)S(1)} collective-permute-done((bf16[384,1024]{1,0:T(8,128)(2,1)S(1)}, bf16[384,1024]{1,0:T(8,128)(2,1)S(1)}, u32[]{:S(2)}, u32[]{:S(2)}) %collective-permute-start.15) | collective-permute-done | bytes 786464 | tf_op jit(solution)/shard_map/ppermute | solution.py:666
  283.3 17.0 %collective-permute-done.9.refs_1_ = bf16[256,1536]{1,0:T(8,128)(2,1)} collective-permute-done((bf16[256,1536]{1,0:T(8,128)(2,1)}, bf16[256,1536]{1,0:T(8,128)(2,1)}, u32[]{:S(2)}, u32[]{:S(2)}) %collective-permute-start.9) | collective-permute-done | bytes 786464 | tf_op jit(solution)/shard_map/ppermute | solution.py:666
  301.5 15.5 %collective-permute-done.12.refs_5_ = bf16[256,1536]{1,0:T(8,128)(2,1)} collective-permute-done((bf16[256,1536]{1,0:T(8,128)(2,1)}, bf16[256,1536]{1,0:T(8,128)(2,1)}, u32[]{:S(2)}, u32[]{:S(2)}) %collective-permute-start.12) | collective-permute-done | bytes 786464 | tf_op jit(solution)/shard_map/ppermute | solution.py:666
  319.7 10.1 %oproj.1 = (bf16[1024,1024]{1,0:T(8,128)(2,1)}, bf16[1024,1024]{1,0:T(8,128)(2,1)}) custom-call(bf16[4,1024,256]{2,1,0:T(8,128)(2,1)} %all-to-all-done.1.a0_ref, bf16[4,1024,256]{2,1,0:T(8,128)(2,1)} %copy-done.7, bf16[2048,1024]{1,0:T(8,128)(2,1)} %all-gather.3.cloned.1.call-done.w_ref.wa_ref.wb_ref, bf16[1024,1024]{1,0:T(8,128)(2,1)} %bitcast.56, ...), custom_call_target="tpu_custom_call" | custom-call | flops 4294967296 | bytes 14680064 | tf_op jit(solution)/shard_map/oproj/pallas_call | solution.py:419
  335.1 27.6 %mlp.2 = (bf16[1024,1536]{1,0:T(8,128)(2,1)}, bf16[1024,1536]{1,0:T(8,128)(2,1)}, bf16[1024,1536]{1,0:T(8,128)(2,1)}, f32[1024,1024]{1,0:T(8,128)}, f32[1024,1024]{1,0:T(8,128)}) custom-call(s32[1]{0:T(128)} %bitcast.10.chip_ref, bf16[1024,1024]{1,0:T(8,128)(2,1)} %get-tuple-element.98.u_ref.la_ref, bf16[1024,1024]{1,0:T(8,128)(2,1)} %bitcast.49, ...), custom_call_target="tpu_custom_call" | custom-call | flops 19327352832 | bytes 31457280 | tf_op jit(solution)/shard_map/mlp/pallas_call | solution.py:461
  362.8 27.4 %mlp.3 = (bf16[1024,1536]{1,0:T(8,128)(2,1)}, bf16[1024,1536]{1,0:T(8,128)(2,1)}, bf16[1024,1536]{1,0:T(8,128)(2,1)}, f32[1024,1024]{1,0:T(8,128)}, f32[1024,1024]{1,0:T(8,128)}) custom-call(s32[1]{0:T(128)} %bitcast.10.chip_ref, bf16[1024,1024]{1,0:T(8,128)(2,1)} %collective-permute-done.18.u_ref.lb_ref, ...), custom_call_target="tpu_custom_call" | custom-call | flops 19327352832 | bytes 31457280 | tf_op jit(solution)/shard_map/mlp/pallas_call | solution.py:461
  390.2 20.6 %dw.1 = f32[1024,3072]{1,0:T(8,128)} custom-call(bf16[1024,1024]{1,0:T(8,128)(2,1)} %get-tuple-element.98.u_ref.la_ref, bf16[1024,1024]{1,0:T(8,128)(2,1)} %collective-permute-done.18.u_ref.lb_ref, bf16[1024,1536]{1,0:T(8,128)(2,1)} %get-tuple-element.134.refs_0_, bf16[1024,1536]{1,0:T(8,128)(2,1)} %get-tuple-element.135.refs_1_, ...), custom_call_target="tpu_custom_call" | custom-call | flops 12884901888 | bytes 20971520 | tf_op jit(solution)/shard_map/dw/pallas_call | solution.py:490
  428.7 13.1 %dw_split.1 = (f32[2,384,1024]{2,1,0:T(8,128)}, f32[2,384,1024]{2,1,0:T(8,128)}) custom-call(s32[4]{0:T(128)} %pad_add_fusion.idx_ref, bf16[1024,1536]{1,0:T(8,128)(2,1)} %get-tuple-element.141.la_ref, bf16[1024,1536]{1,0:T(8,128)(2,1)} %get-tuple-element.142.lb_ref, bf16[1024,1024]{1,0:T(8,128)(2,1)} %bitcast.51, ...), custom_call_target="tpu_custom_call" | custom-call | flops 6442450944 | bytes 20971520 | tf_op jit(solution)/shard_map/dw_split/pallas_call | solution.py:516
  442.7 78.2 %collective-permute-done.23.h2_ref = bf16[1024,1024]{1,0:T(8,128)(2,1)} collective-permute-done((bf16[1024,1024]{1,0:T(8,128)(2,1)}, bf16[1024,1024]{1,0:T(8,128)(2,1)}, u32[]{:S(2)}, u32[]{:S(2)}) %collective-permute-start.23) | collective-permute-done | bytes 2097184 | tf_op jit(solution)/shard_map/ppermute | solution.py:666
  520.9 47.5 %collective-permute-done.33 = f32[2,384,1024]{2,1,0:T(8,128)S(1)} collective-permute-done((f32[2,384,1024]{2,1,0:T(8,128)}, f32[2,384,1024]{2,1,0:T(8,128)S(1)}, u32[]{:S(2)}, u32[]{:S(2)}) %collective-permute-start.33) | collective-permute-done | bytes 3145760 | tf_op jit(solution)/shard_map/ppermute | solution.py:670
  580.2 17.7 %dout.1 = (bf16[4096,256]{1,0:T(8,128)(2,1)}, bf16[4096,256]{1,0:T(8,128)(2,1)}, f32[2,256,1024]{2,1,0:T(8,128)}) custom-call(s32[1]{0:T(128)} %bitcast.sp_ref, bf16[1024,1024]{1,0:T(8,128)(2,1)} %get-tuple-element.109.h0_ref, bf16[1024,1024]{1,0:T(8,128)(2,1)} %collective-permute-done.22.h1_ref, bf16[1024,1024]{1,0:T(8,128)(2,1)} %collective-permute-done.23.h2_ref, ...), custom_call_target="tpu_custom_call" | custom-call | flops 8589934592 | bytes 20971520 | tf_op jit(solution)/shard_map/dout/pallas_call | solution.py:571
  597.9 66.7 %attn_bwd.3 = (bf16[1024,512]{1,0:T(8,128)(2,1)}, bf16[1024,512]{1,0:T(8,128)(2,1)}, bf16[1024,512]{1,0:T(8,128)(2,1)}, bf16[1024,512]{1,0:T(8,128)(2,1)}) custom-call(s32[1]{0:T(128)} %bitcast.sp_ref, bf16[4096,256]{1,0:T(8,128)(2,1)} %get-tuple-element.88.q_ref, bf16[4096,128]{1,0:T(8,128)(2,1)} %get-tuple-element.89.k_ref, ...), custom_call_target="tpu_custom_call" | custom-call | flops 60000002048 | bytes 16777216 | tf_op jit(solution)/shard_map/attn_bwd/pallas_call | solution.py:384
  678.4 66.7 %attn_bwd.2 = (bf16[1024,512]{1,0:T(8,128)(2,1)}, bf16[1024,512]{1,0:T(8,128)(2,1)}, bf16[1024,512]{1,0:T(8,128)(2,1)}, bf16[1024,512]{1,0:T(8,128)(2,1)}) custom-call(s32[1]{0:T(128)} %bitcast.sp_ref, bf16[4096,256]{1,0:T(8,128)(2,1)} %get-tuple-element.92.q_ref, bf16[4096,128]{1,0:T(8,128)(2,1)} %get-tuple-element.93.k_ref, ...), custom_call_target="tpu_custom_call" | custom-call | flops 60000002048 | bytes 16777216 | tf_op jit(solution)/shard_map/attn_bwd/pallas_call | solution.py:384
  780.7 29.6 %collective-permute-done.26.refs_2_ = bf16[1024,512]{1,0:T(8,128)(2,1)} collective-permute-done((bf16[1024,512]{1,0:T(8,128)(2,1)}, bf16[1024,512]{1,0:T(8,128)(2,1)}, u32[]{:S(2)}, u32[]{:S(2)}) %collective-permute-start.26) | collective-permute-done | bytes 1048608 | tf_op jit(solution)/shard_map/ppermute | solution.py:666
  810.4 21.3 %collective-permute-done.27.refs_3_ = bf16[1024,512]{1,0:T(8,128)(2,1)} collective-permute-done((bf16[1024,512]{1,0:T(8,128)(2,1)}, bf16[1024,512]{1,0:T(8,128)(2,1)}, u32[]{:S(2)}, u32[]{:S(2)}) %collective-permute-start.27) | collective-permute-done | bytes 1048608 | tf_op jit(solution)/shard_map/ppermute | solution.py:666
  831.7 11.7 %dx.1 = (bf16[1024,1024]{1,0:T(8,128)(2,1)}, f32[1,1024]{1,0:T(1,128)}) custom-call(s32[1]{0:T(128)} %bitcast.sp_ref, bf16[1024,512]{1,0:T(8,128)(2,1)} %get-tuple-element.112.refs_0_, bf16[1024,512]{1,0:T(8,128)(2,1)} %collective-permute-done.25.refs_1_, bf16[1024,512]{1,0:T(8,128)(2,1)} %collective-permute-done.26.refs_2_, ...), custom_call_target="tpu_custom_call" | custom-call | flops 4294967296 | bytes 16777216 | tf_op jit(solution)/shard_map/dx/pallas_call | solution.py:638
  (138 shorter events, 154.4 us)
Async XLA Ops:
  14.4 58.5 %all-to-all-start = ((bf16[4,144,1024]{2,1,0:T(8,128)(2,1)}), bf16[4,144,1024]{2,1,0:T(8,128)(2,1)S(1)}, u32[]{:S(2)}, u32[]{:S(2)}) async-start(bf16[4,144,1024]{2,1,0:T(8,128)(2,1)} %bitcast.58), calls=%async_computation | async-start | bytes 2359296 | tf_op jit(solution)/shard_map/all_to_all | solution.py:658
  17.9 301.8 %all-gather.3.cloned.1.call-start = ((), (), s32[]{:S(2)}) async-start(), calls=%async_computation.7 | async-start | bytes 4718592 | tf_op jit(solution)/shard_map/all_gather | solution.py:654
  18.0 99.0 %collective-permute-start.6 = (bf16[1024,1024]{1,0:T(8,128)(2,1)}, bf16[1024,1024]{1,0:T(8,128)(2,1)}, u32[]{:S(2)}, u32[]{:S(2)}) collective-permute-start(bf16[1024,1024]{1,0:T(8,128)(2,1)} %bitcast.54), channel_id=1, source_target_pairs={{0,1},{1,0},{2,3},{3,2},{4,5},{5,4},{6,7},{7,6}} | collective-permute-start | bytes 6291464 | tf_op jit(solution)/shard_map/ppermute | solution.py:666
  57.2 70.1 %collective-permute-start.1 = (bf16[1024,1024]{1,0:T(8,128)(2,1)S(1)}, bf16[1024,1024]{1,0:T(8,128)(2,1)}, u32[]{:S(2)}, u32[]{:S(2)}) collective-permute-start(bf16[1024,1024]{1,0:T(8,128)(2,1)S(1)} %collective-permute-done.xa_ref), channel_id=1, source_target_pairs={{0,1},{1,0},{2,3},{3,2},{4,5},{5,4},{6,7},{7,6}} | collective-permute-start | bytes 6291464 | tf_op jit(solution)/shard_map/ppermute | solution.py:666
  235.4 84.3 %all-to-all-start.1 = ((bf16[4,1024,256]{2,1,0:T(8,128)(2,1)}), bf16[4,1024,256]{2,1,0:T(8,128)(2,1)}, u32[]{:S(2)}, u32[]{:S(2)}) async-start(bf16[4,1024,256]{2,1,0:T(8,128)(2,1)} %get-tuple-element.91.o0_ref), calls=%async_computation.1 | async-start | bytes 4194304 | tf_op jit(solution)/shard_map/all_to_all | solution.py:658
  239.9 521.8 %reduce-scatter.2.cloned.1.call-start = ((), (), s32[]{:S(2)}) async-start(), calls=%async_computation.9 | async-start | bytes 15728640 | tf_op jit(solution)/shard_map/reduce_scatter | solution.py:688
  248.4 68.7 %collective-permute-start.12 = (bf16[256,1536]{1,0:T(8,128)(2,1)}, bf16[256,1536]{1,0:T(8,128)(2,1)}, u32[]{:S(2)}, u32[]{:S(2)}) collective-permute-start(bf16[256,1536]{1,0:T(8,128)(2,1)} %get-tuple-element.104.refs_4_), channel_id=1, source_target_pairs={{0,2},{1,3},{2,0},{3,1},{4,6},{5,7},{6,4},{7,5}} | collective-permute-start | bytes 2359304 | tf_op jit(solution)/shard_map/ppermute | solution.py:666
  249.6 80.2 %collective-permute-start.10 = (bf16[256,1536]{1,0:T(8,128)(2,1)}, bf16[256,1536]{1,0:T(8,128)(2,1)}, u32[]{:S(2)}, u32[]{:S(2)}) collective-permute-start(bf16[256,1536]{1,0:T(8,128)(2,1)} %get-tuple-element.103.refs_0_), channel_id=1, source_target_pairs={{0,4},{4,0},{1,5},{5,1},{2,6},{6,2},{3,7},{7,3}} | collective-permute-start | bytes 2359304 | tf_op jit(solution)/shard_map/ppermute | solution.py:670
  261.0 68.8 %collective-permute-start.13 = (bf16[256,1536]{1,0:T(8,128)(2,1)}, bf16[256,1536]{1,0:T(8,128)(2,1)}, u32[]{:S(2)}, u32[]{:S(2)}) collective-permute-start(bf16[256,1536]{1,0:T(8,128)(2,1)} %get-tuple-element.104.refs_4_), channel_id=1, source_target_pairs={{0,4},{4,0},{1,5},{5,1},{2,6},{6,2},{3,7},{7,3}} | collective-permute-start | bytes 2359304 | tf_op jit(solution)/shard_map/ppermute | solution.py:670
  410.9 360.7 %all-gather.5.cloned.1.call-start = ((), (), s32[]{:S(2)}) async-start(), calls=%async_computation.8 | async-start | bytes 9437184 | tf_op jit(solution)/shard_map/all_gather | solution.py:654
  410.9 163.1 %collective-permute-start.20 = (f32[1024,1024]{1,0:T(8,128)}, f32[1024,1024]{1,0:T(8,128)}, u32[]{:S(2)}, u32[]{:S(2)}) collective-permute-start(f32[1024,1024]{1,0:T(8,128)} %get-tuple-element.106), channel_id=1, source_target_pairs={{0,1},{1,0},{2,3},{3,2},{4,5},{5,4},{6,7},{7,6}} | collective-permute-start | bytes 12582920 | tf_op jit(solution)/shard_map/ppermute | solution.py:666
  427.4 93.5 %collective-permute-start.23 = (bf16[1024,1024]{1,0:T(8,128)(2,1)}, bf16[1024,1024]{1,0:T(8,128)(2,1)}, u32[]{:S(2)}, u32[]{:S(2)}) collective-permute-start(bf16[1024,1024]{1,0:T(8,128)(2,1)} %get-tuple-element.109.h0_ref), channel_id=1, source_target_pairs={{0,2},{1,3},{2,0},{3,1},{4,6},{5,7},{6,4},{7,5}} | collective-permute-start | bytes 6291464 | tf_op jit(solution)/shard_map/ppermute | solution.py:666
  441.7 126.7 %collective-permute-start.33 = (f32[2,384,1024]{2,1,0:T(8,128)}, f32[2,384,1024]{2,1,0:T(8,128)S(1)}, u32[]{:S(2)}, u32[]{:S(2)}) collective-permute-start(f32[2,384,1024]{2,1,0:T(8,128)} %get-tuple-element.144), channel_id=1, source_target_pairs={{0,4},{4,0},{1,5},{5,1},{2,6},{6,2},{3,7},{7,3}} | collective-permute-start | bytes 9437192 | tf_op jit(solution)/shard_map/ppermute | solution.py:670
  442.7 137.5 %collective-permute-start.22 = (bf16[1024,1024]{1,0:T(8,128)(2,1)}, bf16[1024,1024]{1,0:T(8,128)(2,1)}, u32[]{:S(2)}, u32[]{:S(2)}) collective-permute-start(bf16[1024,1024]{1,0:T(8,128)(2,1)} %get-tuple-element.109.h0_ref), channel_id=1, source_target_pairs={{0,1},{1,0},{2,3},{3,2},{4,5},{5,4},{6,7},{7,6}} | collective-permute-start | bytes 6291464 | tf_op jit(solution)/shard_map/ppermute | solution.py:666
  520.9 59.3 %collective-permute-start.24 = (bf16[1024,1024]{1,0:T(8,128)(2,1)}, bf16[1024,1024]{1,0:T(8,128)(2,1)}, u32[]{:S(2)}, u32[]{:S(2)}) collective-permute-start(bf16[1024,1024]{1,0:T(8,128)(2,1)} %collective-permute-done.23.h2_ref), channel_id=1, source_target_pairs={{0,1},{1,0},{2,3},{3,2},{4,5},{5,4},{6,7},{7,6}} | collective-permute-start | bytes 6291464 | tf_op jit(solution)/shard_map/ppermute | solution.py:666
  572.5 189.1 %collective-permute-start.34 = (f32[384,1024]{1,0:T(8,128)}, f32[384,1024]{1,0:T(8,128)}, u32[]{:S(2)}, u32[]{:S(2)}) collective-permute-start(f32[384,1024]{1,0:T(8,128)} %fusion.2), channel_id=1, source_target_pairs={{0,2},{1,3},{2,0},{3,1},{4,6},{5,7},{6,4},{7,5}} | collective-permute-start | bytes 4718600 | tf_op jit(solution)/shard_map/ppermute | solution.py:666
  664.6 99.0 %collective-permute-start.28 = (bf16[1024,512]{1,0:T(8,128)(2,1)}, bf16[1024,512]{1,0:T(8,128)(2,1)}, u32[]{:S(2)}, u32[]{:S(2)}) collective-permute-start(bf16[1024,512]{1,0:T(8,128)(2,1)} %get-tuple-element.120.refs_1_), channel_id=1, source_target_pairs={{0,1},{1,0},{2,3},{3,2},{4,5},{5,4},{6,7},{7,6}} | collective-permute-start | bytes 3145736 | tf_op jit(solution)/shard_map/ppermute | solution.py:666
  664.6 101.7 %collective-permute-start.29 = (bf16[1024,512]{1,0:T(8,128)(2,1)}, bf16[1024,512]{1,0:T(8,128)(2,1)}, u32[]{:S(2)}, u32[]{:S(2)}) collective-permute-start(bf16[1024,512]{1,0:T(8,128)(2,1)} %get-tuple-element.121.refs_2_), channel_id=1, source_target_pairs={{0,2},{1,3},{2,0},{3,1},{4,6},{5,7},{6,4},{7,5}} | collective-permute-start | bytes 3145736 | tf_op jit(solution)/shard_map/ppermute | solution.py:666
  665.2 102.6 %collective-permute-start.30 = (bf16[1024,512]{1,0:T(8,128)(2,1)}, bf16[1024,512]{1,0:T(8,128)(2,1)}, u32[]{:S(2)}, u32[]{:S(2)}) collective-permute-start(bf16[1024,512]{1,0:T(8,128)(2,1)} %get-tuple-element.122.refs_3_), channel_id=1, source_target_pairs={{0,3},{1,2},{2,1},{3,0},{4,7},{5,6},{6,5},{7,4}} | collective-permute-start | bytes 3145736 | tf_op jit(solution)/shard_map/ppermute | solution.py:666
  675.8 81.3 %all-to-all-start.3 = ((f32[8,128,512]{2,1,0:T(8,128)}), f32[8,128,512]{2,1,0:T(8,128)S(1)}, u32[]{:S(2)}, u32[]{:S(2)}) async-start(f32[8,128,512]{2,1,0:T(8,128)} %bitcast.48), calls=%async_computation.3 | async-start | bytes 4194304 | tf_op jit(solution)/shard_map/all_to_all | solution.py:662
  758.5 88.6 %all-to-all-start.4 = ((f32[8,128,512]{2,1,0:T(8,128)}), f32[8,128,512]{2,1,0:T(8,128)}, u32[]{:S(2)}, u32[]{:S(2)}) async-start(f32[8,128,512]{2,1,0:T(8,128)} %bitcast.47), calls=%async_computation.4 | async-start | bytes 4194304 | tf_op jit(solution)/shard_map/all_to_all | solution.py:662
  763.5 68.2 %collective-permute-start.27 = (bf16[1024,512]{1,0:T(8,128)(2,1)}, bf16[1024,512]{1,0:T(8,128)(2,1)}, u32[]{:S(2)}, u32[]{:S(2)}) collective-permute-start(bf16[1024,512]{1,0:T(8,128)(2,1)} %get-tuple-element.115.refs_3_), channel_id=1, source_target_pairs={{0,3},{1,2},{2,1},{3,0},{4,7},{5,6},{6,5},{7,4}} | collective-permute-start | bytes 3145736 | tf_op jit(solution)/shard_map/ppermute | solution.py:666
  766.2 78.5 %collective-permute-start.31 = (f32[256,1024]{1,0:T(8,128)}, f32[256,1024]{1,0:T(8,128)}, u32[]{:S(2)}, u32[]{:S(2)}) collective-permute-start(f32[256,1024]{1,0:T(8,128)} %dynamic-slice_bitcast_fusion), channel_id=1, source_target_pairs={{0,4},{4,0},{1,5},{5,1},{2,6},{6,2},{3,7},{7,3}} | collective-permute-start | bytes 3145736 | tf_op jit(solution)/shard_map/ppermute | solution.py:670
  767.7 86.6 %collective-permute-start.32 = (f32[128,3072]{1,0:T(8,128)}, f32[128,3072]{1,0:T(8,128)}, u32[]{:S(2)}, u32[]{:S(2)}) collective-permute-start(f32[128,3072]{1,0:T(8,128)} %constant_dynamic-slice_fusion), channel_id=1, source_target_pairs={{0,1},{1,0},{2,3},{3,2},{4,5},{5,4},{6,7},{7,6}} | collective-permute-start | bytes 4718600 | tf_op jit(solution)/shard_map/ppermute | solution.py:666
  (37 other events, 748.6 us)
Sparse Core Ops, SparseCore 0:
  59.6 45.3 all-gather.2
  411.0 176.5 reduce-scatter.1
  589.9 59.3 all-gather.4

commit v4 on v3

--- a/solution.py
+++ b/solution.py
@@ -606,30 +606,6 @@
     accumulate(dg_ref, col_sum(d_u * normed))
 
 
-def dh_kernel(da_ref, db_ref, h_ref, dy_ref, g_ref, dr_ref, dh_ref, dg_ref):
-    d_u = da_ref[...] + db_ref[...]
-    normed, inv_rms = normalize(h_ref[...].astype(jnp.float32))
-    d_resid = dy_ref[...].astype(jnp.float32) + normalize_grad(d_u * g_ref[...].astype(jnp.float32), normed, inv_rms)
-    dr_ref[...] = d_resid
-    dh_ref[...] = d_resid.astype(jnp.bfloat16)
-    accumulate(dg_ref, col_sum(d_u * normed))
-
-
-def dh_call(d_a, d_b, h, dy, gain):
-    row = row_block(DIM)
-    out = lambda rows, dtype: jax.ShapeDtypeStruct((rows, DIM), dtype)
-    return pl.pallas_call(
-        dh_kernel,
-        grid=(TOK // PAIR,),
-        in_specs=[row] * SP + [fixed(gain.shape)],
-        out_specs=[row, row, fixed(gain.shape)],
-        out_shape=[out(TOK, jnp.float32), out(TOK, jnp.bfloat16), out(gain.shape[0], jnp.float32)],
-        compiler_params=params(),
-        cost_estimate=cost(TINY, 18),
-        name='dh',
-    )(d_a, d_b, h, dy, gain)
-
-
 def dx_call(sp_arr, group, pieces, w_all, *rest):
     row = row_block
     one = fixed((1, DIM))
@@ -731,11 +707,13 @@
     u_pair = from_sp(u_mlp, 1)
     z_a, da_a, dc_a, y_a, d_a = mlp_call(chip_arr, u_mlp, d_layer, w1, w3, w2)
     z_b, da_b, dc_b, y_b, d_b = mlp_call(chip_arr, u_pair, dy_pair, w1, w3, w2)
-    d_got = from_sp(d_b, 1)
-    layout_parts = y_a + from_sp(y_b, 1)
-    layer_out = (residual.astype(f32) + layout_parts).astype(bf16)
-    d_resid, dh, d_gain2 = dh_call(d_a, d_got, residual, d_layer, gain2)
-    dhs = gather_chip_then_core(dh)
+    d_umlp = d_a + from_sp(d_b, 1)
+    h32 = residual.astype(f32)
+    layer_out = (h32 + (y_a + from_sp(y_b, 1))).astype(bf16)
+    normed2, inv_rms2 = normalize(h32)
+    d_gain2 = col_sum(d_umlp * normed2)
+    d_resid = d_layer.astype(f32) + normalize_grad(d_umlp * gain2.astype(f32), normed2, inv_rms2)
+    dhs = gather_chip_then_core(d_resid.astype(bf16))
     order = jnp.stack([chip ^ 3, chip ^ 2, chip ^ 1, chip]).astype(jnp.int32)
     down_send, down_keep = dw_split_call(order, z_a, z_b, d_layer, dy_pair)
     down_got = from_dp(down_send)
@@ -758,7 +736,8 @@
     grad_w_out = pick(dwo, dp) + from_dp(pick(dwo, 1 - dp))
     part, _ = lax.optimization_barrier((part, part1))
     send = lax.dynamic_slice(part, ((1 - core) * HEAD_DIM, 0), (HEAD_DIM, 2 * HALF))
-    grad_w_gate, grad_w_up = unpack_cols_call(core_arr, part, from_sp(send, 1))
+    cols_got = from_sp(send, 1)
+    grad_w_gate, grad_w_up = unpack_cols_call(core_arr, part, cols_got)
     grad_w_down = down_near + down_last
     du0 = dx_call(sp_arr, 0, back0, w_all)
     grad_hidden, d_gain1 = dx_call(sp_arr, 1, back1, w_all, du0, tokens, d_resid, gain1)

time: 874 us -> 869 us (level)
    pallas_call x1 -> x0, Pallas kernels: 9 us -> none  [dh_call(): pl.pallas_call(dh_kernel, grid=(TOK // PAIR,), in_specs=[row] * SP + [fix...]
  transfers between devices with their start and end apart: 44 -> 44, of which waited for: 15 -> 16; matrix products, arithmetic and copies ran while one was open for 4% -> 5% of each run, Pallas kernels for 44% -> 43%
where the time goes in v4:
time: 869 us; the launch traced here: 860 us
  Pallas kernels  421 us (48%)
  waiting for transfers between devices  328 us (38%)
  starting transfers between devices  48.8 us (6%)
  other arithmetic  35.2 us (4%)
  between operations  14.5 us (2%)
  local copies, waits for them, and re-layouts  12.3 us (1%)
    ppermute x27, waiting for transfers between devices, from_sp(): return lax.ppermute(value, 'sp', [(s, s ^ bits) for s in range(SP)])  243 us
    pallas_call x2, Pallas kernels, bwd_call(): pl.pallas_call(bwd_kernel, grid_spec=pltpu.PrefetchScalarGridSpec(num_sca...  134 us
    pallas_call x2, Pallas kernels, fwd_call(): pl.pallas_call(fwd_kernel, grid=(SEQ // BLK,), in_specs=[pl.BlockSpec((BL...  92.7 us
    ppermute x8, waiting for transfers between devices, from_dp(): return lax.ppermute(value, 'dp', [(0, 1), (1, 0)])  84.5 us
    pallas_call x2, Pallas kernels, mlp_call(): pl.pallas_call(mlp_kernel, grid_spec=pltpu.PrefetchScalarGridSpec(num_sca...  54.9 us
    pallas_call x1, Pallas kernels, dw_call(): pl.pallas_call(dw_kernel, grid=(4,), in_specs=[left, left] + [right] * le...  21 us
    pallas_call x2, Pallas kernels, dx_call(): pl.pallas_call(dx_kernel if last else du_kernel, grid_spec=pltpu.Prefetch...  20.8 us
    pallas_call x2, Pallas kernels, qkv_call(): pl.pallas_call(qkv_kernel, grid_spec=pltpu.PrefetchScalarGridSpec(num_sca...  20.6 us
  transfers between devices with their start and end apart: 44, of which 16 were waited for; matrix products, arithmetic and copies ran while one was open for 5% of the time, Pallas kernels for 43%

profile of v4, /device:TPU:0, one launch (start us, length us, event | category | flops | bytes accessed | tf_op | source)
XLA Modules:
  0.0 859.9 jit_solution(4808937810348700300)
XLA Ops:
  18.4 38.8 %collective-permute-done.xa_ref = bf16[1024,1024]{1,0:T(8,128)(2,1)S(1)} collective-permute-done((bf16[1024,1024]{1,0:T(8,128)(2,1)}, bf16[1024,1024]{1,0:T(8,128)(2,1)S(1)}, u32[]{:S(2)}, u32[]{:S(2)}) %collective-permute-start) | collective-permute-done | bytes 2097184 | tf_op jit(solution)/shard_map/ppermute | solution.py:642
  59.5 13.4 %collective-permute-done.4 = s32[8,128]{1,0:T(8,128)S(1)} collective-permute-done((s32[8,128]{1,0:T(8,128)S(1)}, s32[8,128]{1,0:T(8,128)S(1)}, u32[]{:S(2)}, u32[]{:S(2)}) %collective-permute-start.4) | collective-permute-done | bytes 4128 | tf_op jit(solution)/shard_map/ppermute | solution.py:642
  83.7 28.9 %collective-permute-done.2.got_ref = bf16[576,1024]{1,0:T(8,128)(2,1)} collective-permute-done((bf16[576,1024]{1,0:T(8,128)(2,1)S(1)}, bf16[576,1024]{1,0:T(8,128)(2,1)}, u32[]{:S(2)}, u32[]{:S(2)}) %collective-permute-start.2) | collective-permute-done | bytes 1179680 | tf_op jit(solution)/shard_map/ppermute | solution.py:646
  117.0 10.3 %qkv.2 = (bf16[4096,1024]{1,0:T(8,128)(2,1)}, bf16[4096,256]{1,0:T(8,128)(2,1)}, bf16[4096,128]{1,0:T(8,128)(2,1)}, bf16[4096,128]{1,0:T(8,128)(2,1)}, bf16[4096...) custom-call(s32[1]{0:T(128)} %bitcast.sp_ref, bf16[1024,1024]{1,0:T(8,128)(2,1)} %bitcast.55, ...), custom_call_target="tpu_custom_call" | custom-call | flops 4294967296 | bytes 20971520 | tf_op jit(solution)/shard_map/qkv/pallas_call | solution.py:232
  127.3 10.3 %qkv.3 = (bf16[4096,1024]{1,0:T(8,128)(2,1)}, bf16[4096,256]{1,0:T(8,128)(2,1)}, bf16[4096,128]{1,0:T(8,128)(2,1)}, bf16[4096,128]{1,0:T(8,128)(2,1)}, bf16[4096...) custom-call(s32[1]{0:T(128)} %bitcast.sp_ref, ...), custom_call_target="tpu_custom_call", output_to_operand_aliasing={{0}: (7, {}), {1}: (8, {}), {2}: (9, {}), {3}: (10, {}), {4... | custom-call | flops 4294967296 | bytes 20971520 | tf_op jit(solution)/shard_map/qkv/pallas_call | solution.py:232
  137.6 46.4 %attn_fwd.3 = (bf16[4,1024,256]{2,1,0:T(8,128)(2,1)}, f32[2,8,4096]{2,1,0:T(8,128)}) custom-call(bf16[4096,256]{1,0:T(8,128)(2,1)} %get-tuple-element.89.q_ref, bf16[4096,128]{1,0:T(8,128)(2,1)} %get-tuple-element.90.k_ref, bf16[4096,128]{1,0:T(8,128)(2,1)} %get-tuple-element.91.v_ref), custom_call_target="tpu_custom_call" | custom-call | flops 24000000000 | bytes 8388608 | tf_op jit(solution)/shard_map/attn_fwd/pallas_call | solution.py:300
  187.7 46.3 %attn_fwd.2 = (bf16[4,1024,256]{2,1,0:T(8,128)(2,1)}, f32[2,8,4096]{2,1,0:T(8,128)}) custom-call(bf16[4096,256]{1,0:T(8,128)(2,1)} %get-tuple-element.85.q_ref, bf16[4096,128]{1,0:T(8,128)(2,1)} %get-tuple-element.86.k_ref, bf16[4096,128]{1,0:T(8,128)(2,1)} %get-tuple-element.87.v_ref), custom_call_target="tpu_custom_call" | custom-call | flops 24000000000 | bytes 8388608 | tf_op jit(solution)/shard_map/attn_fwd/pallas_call | solution.py:300
  250.3 10.7 %collective-permute-done.16.refs_10_ = bf16[384,1024]{1,0:T(8,128)(2,1)} collective-permute-done((bf16[384,1024]{1,0:T(8,128)(2,1)S(1)}, bf16[384,1024]{1,0:T(8,128)(2,1)}, u32[]{:S(2)}, u32[]{:S(2)}) %collective-permute-start.16) | collective-permute-done | bytes 786464 | tf_op jit(solution)/shard_map/ppermute | solution.py:646
  262.3 21.0 %collective-permute-done.15.refs_9_ = bf16[384,1024]{1,0:T(8,128)(2,1)S(1)} collective-permute-done((bf16[384,1024]{1,0:T(8,128)(2,1)S(1)}, bf16[384,1024]{1,0:T(8,128)(2,1)S(1)}, u32[]{:S(2)}, u32[]{:S(2)}) %collective-permute-start.15) | collective-permute-done | bytes 786464 | tf_op jit(solution)/shard_map/ppermute | solution.py:642
  283.3 17.0 %collective-permute-done.9.refs_1_ = bf16[256,1536]{1,0:T(8,128)(2,1)} collective-permute-done((bf16[256,1536]{1,0:T(8,128)(2,1)}, bf16[256,1536]{1,0:T(8,128)(2,1)}, u32[]{:S(2)}, u32[]{:S(2)}) %collective-permute-start.9) | collective-permute-done | bytes 786464 | tf_op jit(solution)/shard_map/ppermute | solution.py:642
  301.5 15.5 %collective-permute-done.12.refs_5_ = bf16[256,1536]{1,0:T(8,128)(2,1)} collective-permute-done((bf16[256,1536]{1,0:T(8,128)(2,1)}, bf16[256,1536]{1,0:T(8,128)(2,1)}, u32[]{:S(2)}, u32[]{:S(2)}) %collective-permute-start.12) | collective-permute-done | bytes 786464 | tf_op jit(solution)/shard_map/ppermute | solution.py:642
  319.7 9.8 %oproj.1 = (bf16[1024,1024]{1,0:T(8,128)(2,1)}, bf16[1024,1024]{1,0:T(8,128)(2,1)}) custom-call(bf16[4,1024,256]{2,1,0:T(8,128)(2,1)} %all-to-all-done.1.a0_ref, bf16[4,1024,256]{2,1,0:T(8,128)(2,1)} %copy-done.11, bf16[2048,1024]{1,0:T(8,128)(2,1)} %all-gather.3.cloned.1.call-done.w_ref.wa_ref.wb_ref, bf16[1024,1024]{1,0:T(8,128)(2,1)} %bitcast.56, ...), custom_call_target="tpu_custom_call" | custom-call | flops 4294967296 | bytes 14680064 | tf_op jit(solution)/shard_map/oproj/pallas_call | solution.py:419
  335.1 27.4 %mlp.2 = (bf16[1024,1536]{1,0:T(8,128)(2,1)}, bf16[1024,1536]{1,0:T(8,128)(2,1)}, bf16[1024,1536]{1,0:T(8,128)(2,1)}, f32[1024,1024]{1,0:T(8,128)}, f32[1024,1024]{1,0:T(8,128)}) custom-call(s32[1]{0:T(128)} %bitcast.10.chip_ref, bf16[1024,1024]{1,0:T(8,128)(2,1)} %get-tuple-element.95.u_ref.la_ref, bf16[1024,1024]{1,0:T(8,128)(2,1)} %bitcast.46, ...), custom_call_target="tpu_custom_call" | custom-call | flops 19327352832 | bytes 31457280 | tf_op jit(solution)/shard_map/mlp/pallas_call | solution.py:461
  362.5 27.5 %mlp.3 = (bf16[1024,1536]{1,0:T(8,128)(2,1)}, bf16[1024,1536]{1,0:T(8,128)(2,1)}, bf16[1024,1536]{1,0:T(8,128)(2,1)}, f32[1024,1024]{1,0:T(8,128)}, f32[1024,1024]{1,0:T(8,128)}) custom-call(s32[1]{0:T(128)} %bitcast.10.chip_ref, bf16[1024,1024]{1,0:T(8,128)(2,1)} %collective-permute-done.18.u_ref.lb_ref, ...), custom_call_target="tpu_custom_call" | custom-call | flops 19327352832 | bytes 31457280 | tf_op jit(solution)/shard_map/mlp/pallas_call | solution.py:461
  390.0 21.0 %dw.1 = f32[1024,3072]{1,0:T(8,128)} custom-call(bf16[1024,1024]{1,0:T(8,128)(2,1)} %get-tuple-element.95.u_ref.la_ref, bf16[1024,1024]{1,0:T(8,128)(2,1)} %collective-permute-done.18.u_ref.lb_ref, bf16[1024,1536]{1,0:T(8,128)(2,1)} %get-tuple-element.128.refs_0_, bf16[1024,1536]{1,0:T(8,128)(2,1)} %get-tuple-element.129.refs_1_, ...), custom_call_target="tpu_custom_call" | custom-call | flops 12884901888 | bytes 20971520 | tf_op jit(solution)/shard_map/dw/pallas_call | solution.py:490
  434.0 13.3 %dw_split.1 = (f32[2,384,1024]{2,1,0:T(8,128)}, f32[2,384,1024]{2,1,0:T(8,128)}) custom-call(s32[4]{0:T(128)} %pad_add_fusion.idx_ref, bf16[1024,1536]{1,0:T(8,128)(2,1)} %get-tuple-element.135.la_ref, bf16[1024,1536]{1,0:T(8,128)(2,1)} %get-tuple-element.136.lb_ref, bf16[1024,1024]{1,0:T(8,128)(2,1)} %bitcast.47, ...), custom_call_target="tpu_custom_call" | custom-call | flops 6442450944 | bytes 20971520 | tf_op jit(solution)/shard_map/dw_split/pallas_call | solution.py:516
  448.6 77.2 %collective-permute-done.23.h2_ref = bf16[1024,1024]{1,0:T(8,128)(2,1)} collective-permute-done((bf16[1024,1024]{1,0:T(8,128)(2,1)}, bf16[1024,1024]{1,0:T(8,128)(2,1)}, u32[]{:S(2)}, u32[]{:S(2)}) %collective-permute-start.23) | collective-permute-done | bytes 2097184 | tf_op jit(solution)/shard_map/ppermute | solution.py:642
  525.9 42.7 %collective-permute-done.33 = f32[2,384,1024]{2,1,0:T(8,128)S(1)} collective-permute-done((f32[2,384,1024]{2,1,0:T(8,128)}, f32[2,384,1024]{2,1,0:T(8,128)S(1)}, u32[]{:S(2)}, u32[]{:S(2)}) %collective-permute-start.33) | collective-permute-done | bytes 3145760 | tf_op jit(solution)/shard_map/ppermute | solution.py:646
  574.0 17.9 %dout.1 = (bf16[4096,256]{1,0:T(8,128)(2,1)}, bf16[4096,256]{1,0:T(8,128)(2,1)}, f32[2,256,1024]{2,1,0:T(8,128)}) custom-call(s32[1]{0:T(128)} %bitcast.sp_ref, bf16[1024,1024]{1,0:T(8,128)(2,1)} %get-tuple-element.141.h0_ref, bf16[1024,1024]{1,0:T(8,128)(2,1)} %collective-permute-done.22.h1_ref, bf16[1024,1024]{1,0:T(8,128)(2,1)} %collective-permute-done.23.h2_ref, ...), custom_call_target="tpu_custom_call" | custom-call | flops 8589934592 | bytes 20971520 | tf_op jit(solution)/shard_map/dout/pallas_call | solution.py:571
  591.9 67.3 %attn_bwd.3 = (bf16[1024,512]{1,0:T(8,128)(2,1)}, bf16[1024,512]{1,0:T(8,128)(2,1)}, bf16[1024,512]{1,0:T(8,128)(2,1)}, bf16[1024,512]{1,0:T(8,128)(2,1)}) custom-call(s32[1]{0:T(128)} %bitcast.sp_ref, bf16[4096,256]{1,0:T(8,128)(2,1)} %get-tuple-element.85.q_ref, bf16[4096,128]{1,0:T(8,128)(2,1)} %get-tuple-element.86.k_ref, ...), custom_call_target="tpu_custom_call" | custom-call | flops 60000002048 | bytes 16777216 | tf_op jit(solution)/shard_map/attn_bwd/pallas_call | solution.py:384
  673.0 66.7 %attn_bwd.2 = (bf16[1024,512]{1,0:T(8,128)(2,1)}, bf16[1024,512]{1,0:T(8,128)(2,1)}, bf16[1024,512]{1,0:T(8,128)(2,1)}, bf16[1024,512]{1,0:T(8,128)(2,1)}) custom-call(s32[1]{0:T(128)} %bitcast.sp_ref, bf16[4096,256]{1,0:T(8,128)(2,1)} %get-tuple-element.89.q_ref, bf16[4096,128]{1,0:T(8,128)(2,1)} %get-tuple-element.90.k_ref, ...), custom_call_target="tpu_custom_call" | custom-call | flops 60000002048 | bytes 16777216 | tf_op jit(solution)/shard_map/attn_bwd/pallas_call | solution.py:384
  775.3 29.6 %collective-permute-done.26.refs_2_ = bf16[1024,512]{1,0:T(8,128)(2,1)} collective-permute-done((bf16[1024,512]{1,0:T(8,128)(2,1)}, bf16[1024,512]{1,0:T(8,128)(2,1)}, u32[]{:S(2)}, u32[]{:S(2)}) %collective-permute-start.26) | collective-permute-done | bytes 1048608 | tf_op jit(solution)/shard_map/ppermute | solution.py:642
  804.9 21.3 %collective-permute-done.27.refs_3_ = bf16[1024,512]{1,0:T(8,128)(2,1)} collective-permute-done((bf16[1024,512]{1,0:T(8,128)(2,1)}, bf16[1024,512]{1,0:T(8,128)(2,1)}, u32[]{:S(2)}, u32[]{:S(2)}) %collective-permute-start.27) | collective-permute-done | bytes 1048608 | tf_op jit(solution)/shard_map/ppermute | solution.py:642
  826.3 11.7 %dx.1 = (bf16[1024,1024]{1,0:T(8,128)(2,1)}, f32[1,1024]{1,0:T(1,128)}) custom-call(s32[1]{0:T(128)} %bitcast.sp_ref, bf16[1024,512]{1,0:T(8,128)(2,1)} %get-tuple-element.108.refs_0_, bf16[1024,512]{1,0:T(8,128)(2,1)} %collective-permute-done.25.refs_1_, bf16[1024,512]{1,0:T(8,128)(2,1)} %collective-permute-done.26.refs_2_, ...), custom_call_target="tpu_custom_call" | custom-call | flops 4294967296 | bytes 16777216 | tf_op jit(solution)/shard_map/dx/pallas_call | solution.py:614
  (147 shorter events, 153.6 us)
Async XLA Ops:
  14.4 58.5 %all-to-all-start = ((bf16[4,144,1024]{2,1,0:T(8,128)(2,1)}), bf16[4,144,1024]{2,1,0:T(8,128)(2,1)S(1)}, u32[]{:S(2)}, u32[]{:S(2)}) async-start(bf16[4,144,1024]{2,1,0:T(8,128)(2,1)} %bitcast.58), calls=%async_computation | async-start | bytes 2359296 | tf_op jit(solution)/shard_map/all_to_all | solution.py:634
  17.9 301.8 %all-gather.3.cloned.1.call-start = ((), (), s32[]{:S(2)}) async-start(), calls=%async_computation.7 | async-start | bytes 4718592 | tf_op jit(solution)/shard_map/all_gather | solution.py:630
  18.0 99.0 %collective-permute-start.6 = (bf16[1024,1024]{1,0:T(8,128)(2,1)}, bf16[1024,1024]{1,0:T(8,128)(2,1)}, u32[]{:S(2)}, u32[]{:S(2)}) collective-permute-start(bf16[1024,1024]{1,0:T(8,128)(2,1)} %bitcast.54), channel_id=1, source_target_pairs={{0,1},{1,0},{2,3},{3,2},{4,5},{5,4},{6,7},{7,6}} | collective-permute-start | bytes 6291464 | tf_op jit(solution)/shard_map/ppermute | solution.py:642
  57.2 70.1 %collective-permute-start.1 = (bf16[1024,1024]{1,0:T(8,128)(2,1)S(1)}, bf16[1024,1024]{1,0:T(8,128)(2,1)}, u32[]{:S(2)}, u32[]{:S(2)}) collective-permute-start(bf16[1024,1024]{1,0:T(8,128)(2,1)S(1)} %collective-permute-done.xa_ref), channel_id=1, source_target_pairs={{0,1},{1,0},{2,3},{3,2},{4,5},{5,4},{6,7},{7,6}} | collective-permute-start | bytes 6291464 | tf_op jit(solution)/shard_map/ppermute | solution.py:642
  184.0 50.1 %all-to-all-start.2 = ((bf16[4,1024,256]{2,1,0:T(8,128)(2,1)}), bf16[4,1024,256]{2,1,0:T(8,128)(2,1)S(1)}, u32[]{:S(2)}, u32[]{:S(2)}) async-start(bf16[4,1024,256]{2,1,0:T(8,128)(2,1)} %get-tuple-element.92.o1_ref), calls=%async_computation.2 | async-start | bytes 4194304 | tf_op jit(solution)/shard_map/all_to_all | solution.py:634
  235.4 84.3 %all-to-all-start.1 = ((bf16[4,1024,256]{2,1,0:T(8,128)(2,1)}), bf16[4,1024,256]{2,1,0:T(8,128)(2,1)}, u32[]{:S(2)}, u32[]{:S(2)}) async-start(bf16[4,1024,256]{2,1,0:T(8,128)(2,1)} %get-tuple-element.88.o0_ref), calls=%async_computation.1 | async-start | bytes 4194304 | tf_op jit(solution)/shard_map/all_to_all | solution.py:634
  239.9 516.3 %reduce-scatter.2.cloned.1.call-start = ((), (), s32[]{:S(2)}) async-start(), calls=%async_computation.9 | async-start | bytes 15728640 | tf_op jit(solution)/shard_map/reduce_scatter | solution.py:664
  247.6 52.6 %collective-permute-start.9 = (bf16[256,1536]{1,0:T(8,128)(2,1)}, bf16[256,1536]{1,0:T(8,128)(2,1)}, u32[]{:S(2)}, u32[]{:S(2)}) collective-permute-start(bf16[256,1536]{1,0:T(8,128)(2,1)} %get-tuple-element.100.refs_0_), channel_id=1, source_target_pairs={{0,2},{1,3},{2,0},{3,1},{4,6},{5,7},{6,4},{7,5}} | collective-permute-start | bytes 2359304 | tf_op jit(solution)/shard_map/ppermute | solution.py:642
  248.4 68.7 %collective-permute-start.12 = (bf16[256,1536]{1,0:T(8,128)(2,1)}, bf16[256,1536]{1,0:T(8,128)(2,1)}, u32[]{:S(2)}, u32[]{:S(2)}) collective-permute-start(bf16[256,1536]{1,0:T(8,128)(2,1)} %get-tuple-element.101.refs_4_), channel_id=1, source_target_pairs={{0,2},{1,3},{2,0},{3,1},{4,6},{5,7},{6,4},{7,5}} | collective-permute-start | bytes 2359304 | tf_op jit(solution)/shard_map/ppermute | solution.py:642
  249.6 79.9 %collective-permute-start.10 = (bf16[256,1536]{1,0:T(8,128)(2,1)}, bf16[256,1536]{1,0:T(8,128)(2,1)}, u32[]{:S(2)}, u32[]{:S(2)}) collective-permute-start(bf16[256,1536]{1,0:T(8,128)(2,1)} %get-tuple-element.100.refs_0_), channel_id=1, source_target_pairs={{0,4},{4,0},{1,5},{5,1},{2,6},{6,2},{3,7},{7,3}} | collective-permute-start | bytes 2359304 | tf_op jit(solution)/shard_map/ppermute | solution.py:646
  261.0 68.6 %collective-permute-start.13 = (bf16[256,1536]{1,0:T(8,128)(2,1)}, bf16[256,1536]{1,0:T(8,128)(2,1)}, u32[]{:S(2)}, u32[]{:S(2)}) collective-permute-start(bf16[256,1536]{1,0:T(8,128)(2,1)} %get-tuple-element.101.refs_4_), channel_id=1, source_target_pairs={{0,4},{4,0},{1,5},{5,1},{2,6},{6,2},{3,7},{7,3}} | collective-permute-start | bytes 2359304 | tf_op jit(solution)/shard_map/ppermute | solution.py:646
  411.0 355.1 %all-gather.5.cloned.1.call-start = ((), (), s32[]{:S(2)}) async-start(), calls=%async_computation.8 | async-start | bytes 9437184 | tf_op jit(solution)/shard_map/all_gather | solution.py:630
  432.3 93.6 %collective-permute-start.23 = (bf16[1024,1024]{1,0:T(8,128)(2,1)}, bf16[1024,1024]{1,0:T(8,128)(2,1)}, u32[]{:S(2)}, u32[]{:S(2)}) collective-permute-start(bf16[1024,1024]{1,0:T(8,128)(2,1)} %get-tuple-element.141.h0_ref), channel_id=1, source_target_pairs={{0,2},{1,3},{2,0},{3,1},{4,6},{5,7},{6,4},{7,5}} | collective-permute-start | bytes 6291464 | tf_op jit(solution)/shard_map/ppermute | solution.py:642
  447.3 121.3 %collective-permute-start.33 = (f32[2,384,1024]{2,1,0:T(8,128)}, f32[2,384,1024]{2,1,0:T(8,128)S(1)}, u32[]{:S(2)}, u32[]{:S(2)}) collective-permute-start(f32[2,384,1024]{2,1,0:T(8,128)} %get-tuple-element.138), channel_id=1, source_target_pairs={{0,4},{4,0},{1,5},{5,1},{2,6},{6,2},{3,7},{7,3}} | collective-permute-start | bytes 9437192 | tf_op jit(solution)/shard_map/ppermute | solution.py:646
  448.6 125.4 %collective-permute-start.22 = (bf16[1024,1024]{1,0:T(8,128)(2,1)}, bf16[1024,1024]{1,0:T(8,128)(2,1)}, u32[]{:S(2)}, u32[]{:S(2)}) collective-permute-start(bf16[1024,1024]{1,0:T(8,128)(2,1)} %get-tuple-element.141.h0_ref), channel_id=1, source_target_pairs={{0,1},{1,0},{2,3},{3,2},{4,5},{5,4},{6,7},{7,6}} | collective-permute-start | bytes 6291464 | tf_op jit(solution)/shard_map/ppermute | solution.py:642
  572.6 183.6 %collective-permute-start.34 = (f32[384,1024]{1,0:T(8,128)}, f32[384,1024]{1,0:T(8,128)}, u32[]{:S(2)}, u32[]{:S(2)}) collective-permute-start(f32[384,1024]{1,0:T(8,128)} %fusion.12), channel_id=1, source_target_pairs={{0,2},{1,3},{2,0},{3,1},{4,6},{5,7},{6,4},{7,5}} | collective-permute-start | bytes 4718600 | tf_op jit(solution)/shard_map/ppermute | solution.py:642
  659.1 99.0 %collective-permute-start.28 = (bf16[1024,512]{1,0:T(8,128)(2,1)}, bf16[1024,512]{1,0:T(8,128)(2,1)}, u32[]{:S(2)}, u32[]{:S(2)}) collective-permute-start(bf16[1024,512]{1,0:T(8,128)(2,1)} %get-tuple-element.116.refs_1_), channel_id=1, source_target_pairs={{0,1},{1,0},{2,3},{3,2},{4,5},{5,4},{6,7},{7,6}} | collective-permute-start | bytes 3145736 | tf_op jit(solution)/shard_map/ppermute | solution.py:642
  659.1 101.7 %collective-permute-start.29 = (bf16[1024,512]{1,0:T(8,128)(2,1)}, bf16[1024,512]{1,0:T(8,128)(2,1)}, u32[]{:S(2)}, u32[]{:S(2)}) collective-permute-start(bf16[1024,512]{1,0:T(8,128)(2,1)} %get-tuple-element.117.refs_2_), channel_id=1, source_target_pairs={{0,2},{1,3},{2,0},{3,1},{4,6},{5,7},{6,4},{7,5}} | collective-permute-start | bytes 3145736 | tf_op jit(solution)/shard_map/ppermute | solution.py:642
  659.3 103.0 %collective-permute-start.30 = (bf16[1024,512]{1,0:T(8,128)(2,1)}, bf16[1024,512]{1,0:T(8,128)(2,1)}, u32[]{:S(2)}, u32[]{:S(2)}) collective-permute-start(bf16[1024,512]{1,0:T(8,128)(2,1)} %get-tuple-element.118.refs_3_), channel_id=1, source_target_pairs={{0,3},{1,2},{2,1},{3,0},{4,7},{5,6},{6,5},{7,4}} | collective-permute-start | bytes 3145736 | tf_op jit(solution)/shard_map/ppermute | solution.py:642
  670.4 81.4 %all-to-all-start.3 = ((f32[8,128,512]{2,1,0:T(8,128)}), f32[8,128,512]{2,1,0:T(8,128)S(1)}, u32[]{:S(2)}, u32[]{:S(2)}) async-start(f32[8,128,512]{2,1,0:T(8,128)} %bitcast.52), calls=%async_computation.3 | async-start | bytes 4194304 | tf_op jit(solution)/shard_map/all_to_all | solution.py:638
  753.1 88.6 %all-to-all-start.4 = ((f32[8,128,512]{2,1,0:T(8,128)}), f32[8,128,512]{2,1,0:T(8,128)}, u32[]{:S(2)}, u32[]{:S(2)}) async-start(f32[8,128,512]{2,1,0:T(8,128)} %bitcast.51), calls=%async_computation.4 | async-start | bytes 4194304 | tf_op jit(solution)/shard_map/all_to_all | solution.py:638
  758.1 68.2 %collective-permute-start.27 = (bf16[1024,512]{1,0:T(8,128)(2,1)}, bf16[1024,512]{1,0:T(8,128)(2,1)}, u32[]{:S(2)}, u32[]{:S(2)}) collective-permute-start(bf16[1024,512]{1,0:T(8,128)(2,1)} %get-tuple-element.111.refs_3_), channel_id=1, source_target_pairs={{0,3},{1,2},{2,1},{3,0},{4,7},{5,6},{6,5},{7,4}} | collective-permute-start | bytes 3145736 | tf_op jit(solution)/shard_map/ppermute | solution.py:642
  760.8 78.5 %collective-permute-start.31 = (f32[256,1024]{1,0:T(8,128)}, f32[256,1024]{1,0:T(8,128)}, u32[]{:S(2)}, u32[]{:S(2)}) collective-permute-start(f32[256,1024]{1,0:T(8,128)} %dynamic-slice_bitcast_fusion), channel_id=1, source_target_pairs={{0,4},{4,0},{1,5},{5,1},{2,6},{6,2},{3,7},{7,3}} | collective-permute-start | bytes 3145736 | tf_op jit(solution)/shard_map/ppermute | solution.py:646
  762.3 86.4 %collective-permute-start.32 = (f32[128,3072]{1,0:T(8,128)}, f32[128,3072]{1,0:T(8,128)}, u32[]{:S(2)}, u32[]{:S(2)}) collective-permute-start(f32[128,3072]{1,0:T(8,128)} %constant_dynamic-slice_fusion), channel_id=1, source_target_pairs={{0,1},{1,0},{2,3},{3,2},{4,5},{5,4},{6,7},{7,6}} | collective-permute-start | bytes 4718600 | tf_op jit(solution)/shard_map/ppermute | solution.py:642
  (40 other events, 723.6 us)
Sparse Core Ops, SparseCore 0:
  59.6 45.3 all-gather.2
  411.2 176.4 reduce-scatter.1
  590.1 59.3 all-gather.4

commit v5 on v4

--- a/solution.py
+++ b/solution.py
@@ -160,19 +160,19 @@
     )(dp_arr, own, got)
 
 
-def unpack_qkv_kernel(p0_ref, p1_ref, wq_ref, wk_ref, wv_ref):
-    for g, ref in enumerate((p0_ref, p1_ref)):
+def unpack_qkv_kernel(p_ref, wq_ref, wk_ref, wv_ref):
+    for g in range(PAIRS):
         for n in range(SP):
-            m = g * 4 + n
-            total = ref[n] + ref[4 + n]
-            wq_ref[:, m * PAIR:(m + 1) * PAIR] = total[:, 0:PAIR]
+            m = g * SP + n
+            total = p_ref[n, :, g * GRP:(g + 1) * GRP]
+            wq_ref[:, m * PAIR:(m + 1) * PAIR] = total[:, :PAIR]
             wk_ref[:, m * HEAD_DIM:(m + 1) * HEAD_DIM] = total[:, PAIR:OWN]
-            wv_ref[:, m * HEAD_DIM:(m + 1) * HEAD_DIM] = total[:, OWN:GRP]
-
-
-def unpack_qkv_call(p0, p1):
+            wv_ref[:, m * HEAD_DIM:(m + 1) * HEAD_DIM] = total[:, OWN:]
+
+
+def unpack_qkv_call(parts):
     out = lambda cols: jax.ShapeDtypeStruct((HEAD_DIM, cols), jnp.float32)
-    return pl.pallas_call(unpack_qkv_kernel, out_shape=[out(2048), out(DIM), out(DIM)], cost_estimate=cost(TINY, 6), name='unpack_qkv')(p0, p1)
+    return pl.pallas_call(unpack_qkv_kernel, out_shape=[out(PAIRS * DIM), out(DIM), out(DIM)], cost_estimate=cost(TINY, 6), name='unpack_qkv')(parts)
 
 
 def unpack_cols_kernel(core_ref, own_ref, got_ref, gate_ref, up_ref):
@@ -707,7 +707,8 @@
     u_pair = from_sp(u_mlp, 1)
     z_a, da_a, dc_a, y_a, d_a = mlp_call(chip_arr, u_mlp, d_layer, w1, w3, w2)
     z_b, da_b, dc_b, y_b, d_b = mlp_call(chip_arr, u_pair, dy_pair, w1, w3, w2)
-    d_umlp = d_a + from_sp(d_b, 1)
+    d_got = from_sp(d_b, 1)
+    d_umlp = d_a + d_got
     h32 = residual.astype(f32)
     layer_out = (h32 + (y_a + from_sp(y_b, 1))).astype(bf16)
     normed2, inv_rms2 = normalize(h32)
@@ -726,13 +727,15 @@
     o_seq = (o0.reshape(SEQ, PAIR), o1.reshape(SEQ, PAIR))
     d0 = bwd_call(sp_arr, q0, k0, v0, o_seq[0], do0, lse0, cos, sin)
     back0 = [d0[0]] + [from_sp(d0[n], n) for n in (1, 2, 3)]
-    part0 = dw_qkv_call(u_all, d0).reshape(8, HEAD_DIM, GRP)
-    dw0 = swap_all(part0)
+    part0 = dw_qkv_call(u_all, d0).reshape(PAIRS, GRP, GRP)
+    dw_got0 = from_dp(pick(part0, 1 - dp))
     d1 = bwd_call(sp_arr, q1, k1, v1, o_seq[1], do1, lse1, cos, sin)
     back1 = [d1[0]] + [from_sp(d1[n], n) for n in (1, 2, 3)]
-    part1 = dw_qkv_call(u_all, d1).reshape(8, HEAD_DIM, GRP)
-    part1, _ = lax.optimization_barrier((part1, dw0))
-    dw1 = swap_all(part1)
+    part1 = dw_qkv_call(u_all, d1).reshape(PAIRS, GRP, GRP)
+    dw_got1 = from_dp(pick(part1, 1 - dp))
+    dw_rows = jnp.concatenate([pick(part0, dp) + dw_got0, pick(part1, dp) + dw_got1], axis=1)
+    dw_cols = swap_seq(dw_rows.reshape(SP, HEAD_DIM, DIM))
+
     grad_w_out = pick(dwo, dp) + from_dp(pick(dwo, 1 - dp))
     part, _ = lax.optimization_barrier((part, part1))
     send = lax.dynamic_slice(part, ((1 - core) * HEAD_DIM, 0), (HEAD_DIM, 2 * HALF))
@@ -741,9 +744,9 @@
     grad_w_down = down_near + down_last
     du0 = dx_call(sp_arr, 0, back0, w_all)
     grad_hidden, d_gain1 = dx_call(sp_arr, 1, back1, w_all, du0, tokens, d_resid, gain1)
-    grad_w_query, grad_w_key, grad_w_value = unpack_qkv_call(dw0, dw1)
+    grad_w_query, grad_w_key, grad_w_value = unpack_qkv_call(dw_cols)
     gain_parts = jnp.stack([d_gain1.reshape(8, HEAD_DIM), d_gain2.reshape(8, HEAD_DIM)], axis=1)
-    gain_parts, _ = lax.optimization_barrier((gain_parts, dw1))
+    gain_parts, _ = lax.optimization_barrier((gain_parts, dw_cols))
     gain_sums = jnp.sum(swap_all(gain_parts), axis=0)
     return (layer_out[None], grad_hidden[None], gain_sums[0], gain_sums[1], grad_w_query, grad_w_key, grad_w_value,
             grad_w_out, grad_w_gate, grad_w_up, grad_w_down)

time: 869 us -> 910 us (1.047)
  waiting for transfers between devices: 328 us -> 362 us
    ppermute x8 -> x10, waiting for transfers between devices: 84.5 us -> 102 us  [from_dp(): return lax.ppermute(value, 'dp', [(0, 1), (1, 0)])]
    ppermute x27, waiting for transfers between devices: 243 us -> 258 us  [from_sp(): return lax.ppermute(value, 'sp', [(s, s ^ bits) for s in range(SP)])]
  transfers between devices with their start and end apart: 44 -> 45, of which waited for: 16 -> 18; matrix products, arithmetic and copies ran while one was open for 5% -> 6% of each run, Pallas kernels for 43% -> 41%
where the time goes in v5:
time: 910 us; the launch traced here: 901 us
  Pallas kernels  421 us (46%)
  waiting for transfers between devices  362 us (40%)
  starting transfers between devices  49.4 us (5%)
  other arithmetic  39.9 us (4%)
  local copies, waits for them, and re-layouts  14.8 us (2%)
  between operations  14.5 us (2%)
    ppermute x27, waiting for transfers between devices, from_sp(): return lax.ppermute(value, 'sp', [(s, s ^ bits) for s in range(SP)])  258 us
    pallas_call x2, Pallas kernels, bwd_call(): pl.pallas_call(bwd_kernel, grid_spec=pltpu.PrefetchScalarGridSpec(num_sca...  134 us
    ppermute x10, waiting for transfers between devices, from_dp(): return lax.ppermute(value, 'dp', [(0, 1), (1, 0)])  102 us
    pallas_call x2, Pallas kernels, fwd_call(): pl.pallas_call(fwd_kernel, grid=(SEQ // BLK,), in_specs=[pl.BlockSpec((BL...  92.7 us
    pallas_call x2, Pallas kernels, mlp_call(): pl.pallas_call(mlp_kernel, grid_spec=pltpu.PrefetchScalarGridSpec(num_sca...  54.9 us
    pallas_call x1, Pallas kernels, dw_call(): pl.pallas_call(dw_kernel, grid=(4,), in_specs=[left, left] + [right] * le...  21 us
    pallas_call x2, Pallas kernels, dx_call(): pl.pallas_call(dx_kernel if last else du_kernel, grid_spec=pltpu.Prefetch...  20.7 us
    pallas_call x2, Pallas kernels, qkv_call(): pl.pallas_call(qkv_kernel, grid_spec=pltpu.PrefetchScalarGridSpec(num_sca...  20.6 us
  transfers between devices with their start and end apart: 45, of which 18 were waited for; matrix products, arithmetic and copies ran while one was open for 6% of the time, Pallas kernels for 41%

profile of v5, /device:TPU:0, one launch (start us, length us, event | category | flops | bytes accessed | tf_op | source)
XLA Modules:
  0.0 901.0 jit_solution(16103960344713891071)
XLA Ops:
  18.4 38.8 %collective-permute-done.xa_ref = bf16[1024,1024]{1,0:T(8,128)(2,1)S(1)} collective-permute-done((bf16[1024,1024]{1,0:T(8,128)(2,1)}, bf16[1024,1024]{1,0:T(8,128)(2,1)S(1)}, u32[]{:S(2)}, u32[]{:S(2)}) %collective-permute-start) | collective-permute-done | bytes 2097184 | tf_op jit(solution)/shard_map/ppermute | solution.py:642
  59.5 13.4 %collective-permute-done.4 = s32[8,128]{1,0:T(8,128)S(1)} collective-permute-done((s32[8,128]{1,0:T(8,128)S(1)}, s32[8,128]{1,0:T(8,128)S(1)}, u32[]{:S(2)}, u32[]{:S(2)}) %collective-permute-start.4) | collective-permute-done | bytes 4128 | tf_op jit(solution)/shard_map/ppermute | solution.py:642
  83.7 28.9 %collective-permute-done.2.got_ref = bf16[576,1024]{1,0:T(8,128)(2,1)} collective-permute-done((bf16[576,1024]{1,0:T(8,128)(2,1)S(1)}, bf16[576,1024]{1,0:T(8,128)(2,1)}, u32[]{:S(2)}, u32[]{:S(2)}) %collective-permute-start.2) | collective-permute-done | bytes 1179680 | tf_op jit(solution)/shard_map/ppermute | solution.py:646
  127.3 10.3 %qkv.3 = (bf16[4096,1024]{1,0:T(8,128)(2,1)}, bf16[4096,256]{1,0:T(8,128)(2,1)}, bf16[4096,128]{1,0:T(8,128)(2,1)}, bf16[4096,128]{1,0:T(8,128)(2,1)}, bf16[4096...) custom-call(s32[1]{0:T(128)} %bitcast.sp_ref, ...), custom_call_target="tpu_custom_call", output_to_operand_aliasing={{0}: (7, {}), {1}: (8, {}), {2}: (9, {}), {3}: (10, {}), {4... | custom-call | flops 4294967296 | bytes 20971520 | tf_op jit(solution)/shard_map/qkv/pallas_call | solution.py:232
  137.6 46.4 %attn_fwd.3 = (bf16[4,1024,256]{2,1,0:T(8,128)(2,1)}, f32[2,8,4096]{2,1,0:T(8,128)}) custom-call(bf16[4096,256]{1,0:T(8,128)(2,1)} %get-tuple-element.88.q_ref, bf16[4096,128]{1,0:T(8,128)(2,1)} %get-tuple-element.89.k_ref, bf16[4096,128]{1,0:T(8,128)(2,1)} %get-tuple-element.90.v_ref), custom_call_target="tpu_custom_call" | custom-call | flops 24000000000 | bytes 8388608 | tf_op jit(solution)/shard_map/attn_fwd/pallas_call | solution.py:300
  187.7 46.3 %attn_fwd.2 = (bf16[4,1024,256]{2,1,0:T(8,128)(2,1)}, f32[2,8,4096]{2,1,0:T(8,128)}) custom-call(bf16[4096,256]{1,0:T(8,128)(2,1)} %get-tuple-element.84.q_ref, bf16[4096,128]{1,0:T(8,128)(2,1)} %get-tuple-element.85.k_ref, bf16[4096,128]{1,0:T(8,128)(2,1)} %get-tuple-element.86.v_ref), custom_call_target="tpu_custom_call" | custom-call | flops 24000000000 | bytes 8388608 | tf_op jit(solution)/shard_map/attn_fwd/pallas_call | solution.py:300
  250.3 10.7 %collective-permute-done.16.refs_10_ = bf16[384,1024]{1,0:T(8,128)(2,1)} collective-permute-done((bf16[384,1024]{1,0:T(8,128)(2,1)S(1)}, bf16[384,1024]{1,0:T(8,128)(2,1)}, u32[]{:S(2)}, u32[]{:S(2)}) %collective-permute-start.16) | collective-permute-done | bytes 786464 | tf_op jit(solution)/shard_map/ppermute | solution.py:646
  262.3 21.0 %collective-permute-done.15.refs_9_ = bf16[384,1024]{1,0:T(8,128)(2,1)S(1)} collective-permute-done((bf16[384,1024]{1,0:T(8,128)(2,1)S(1)}, bf16[384,1024]{1,0:T(8,128)(2,1)S(1)}, u32[]{:S(2)}, u32[]{:S(2)}) %collective-permute-start.15) | collective-permute-done | bytes 786464 | tf_op jit(solution)/shard_map/ppermute | solution.py:642
  283.3 17.0 %collective-permute-done.9.refs_1_ = bf16[256,1536]{1,0:T(8,128)(2,1)} collective-permute-done((bf16[256,1536]{1,0:T(8,128)(2,1)}, bf16[256,1536]{1,0:T(8,128)(2,1)}, u32[]{:S(2)}, u32[]{:S(2)}) %collective-permute-start.9) | collective-permute-done | bytes 786464 | tf_op jit(solution)/shard_map/ppermute | solution.py:642
  301.6 15.5 %collective-permute-done.12.refs_5_ = bf16[256,1536]{1,0:T(8,128)(2,1)} collective-permute-done((bf16[256,1536]{1,0:T(8,128)(2,1)}, bf16[256,1536]{1,0:T(8,128)(2,1)}, u32[]{:S(2)}, u32[]{:S(2)}) %collective-permute-start.12) | collective-permute-done | bytes 786464 | tf_op jit(solution)/shard_map/ppermute | solution.py:642
  335.1 27.4 %mlp.2 = (bf16[1024,1536]{1,0:T(8,128)(2,1)}, bf16[1024,1536]{1,0:T(8,128)(2,1)}, bf16[1024,1536]{1,0:T(8,128)(2,1)}, f32[1024,1024]{1,0:T(8,128)}, f32[1024,1024]{1,0:T(8,128)}) custom-call(s32[1]{0:T(128)} %bitcast.10.chip_ref, bf16[1024,1024]{1,0:T(8,128)(2,1)} %get-tuple-element.94.u_ref.la_ref, bf16[1024,1024]{1,0:T(8,128)(2,1)} %bitcast.56, ...), custom_call_target="tpu_custom_call" | custom-call | flops 19327352832 | bytes 31457280 | tf_op jit(solution)/shard_map/mlp/pallas_call | solution.py:461
  362.5 27.5 %mlp.3 = (bf16[1024,1536]{1,0:T(8,128)(2,1)}, bf16[1024,1536]{1,0:T(8,128)(2,1)}, bf16[1024,1536]{1,0:T(8,128)(2,1)}, f32[1024,1024]{1,0:T(8,128)}, f32[1024,1024]{1,0:T(8,128)}) custom-call(s32[1]{0:T(128)} %bitcast.10.chip_ref, bf16[1024,1024]{1,0:T(8,128)(2,1)} %collective-permute-done.18.u_ref.lb_ref, ...), custom_call_target="tpu_custom_call" | custom-call | flops 19327352832 | bytes 31457280 | tf_op jit(solution)/shard_map/mlp/pallas_call | solution.py:461
  390.0 21.0 %dw.1 = f32[1024,3072]{1,0:T(8,128)} custom-call(bf16[1024,1024]{1,0:T(8,128)(2,1)} %get-tuple-element.94.u_ref.la_ref, bf16[1024,1024]{1,0:T(8,128)(2,1)} %collective-permute-done.18.u_ref.lb_ref, bf16[1024,1536]{1,0:T(8,128)(2,1)} %get-tuple-element.126.refs_0_, bf16[1024,1536]{1,0:T(8,128)(2,1)} %get-tuple-element.127.refs_1_, ...), custom_call_target="tpu_custom_call" | custom-call | flops 12884901888 | bytes 20971520 | tf_op jit(solution)/shard_map/dw/pallas_call | solution.py:490
  434.0 13.3 %dw_split.1 = (f32[2,384,1024]{2,1,0:T(8,128)}, f32[2,384,1024]{2,1,0:T(8,128)}) custom-call(s32[4]{0:T(128)} %pad_add_fusion.idx_ref, bf16[1024,1536]{1,0:T(8,128)(2,1)} %get-tuple-element.133.la_ref, bf16[1024,1536]{1,0:T(8,128)(2,1)} %get-tuple-element.134.lb_ref, bf16[1024,1024]{1,0:T(8,128)(2,1)} %bitcast.57, ...), custom_call_target="tpu_custom_call" | custom-call | flops 6442450944 | bytes 20971520 | tf_op jit(solution)/shard_map/dw_split/pallas_call | solution.py:516
  448.7 77.1 %collective-permute-done.23.h2_ref = bf16[1024,1024]{1,0:T(8,128)(2,1)} collective-permute-done((bf16[1024,1024]{1,0:T(8,128)(2,1)}, bf16[1024,1024]{1,0:T(8,128)(2,1)}, u32[]{:S(2)}, u32[]{:S(2)}) %collective-permute-start.23) | collective-permute-done | bytes 2097184 | tf_op jit(solution)/shard_map/ppermute | solution.py:642
  525.9 42.8 %collective-permute-done.35 = f32[2,384,1024]{2,1,0:T(8,128)S(1)} collective-permute-done((f32[2,384,1024]{2,1,0:T(8,128)}, f32[2,384,1024]{2,1,0:T(8,128)S(1)}, u32[]{:S(2)}, u32[]{:S(2)}) %collective-permute-start.35) | collective-permute-done | bytes 3145760 | tf_op jit(solution)/shard_map/ppermute | solution.py:646
  574.0 17.9 %dout.1 = (bf16[4096,256]{1,0:T(8,128)(2,1)}, bf16[4096,256]{1,0:T(8,128)(2,1)}, f32[2,256,1024]{2,1,0:T(8,128)}) custom-call(s32[1]{0:T(128)} %bitcast.sp_ref, bf16[1024,1024]{1,0:T(8,128)(2,1)} %get-tuple-element.139.h0_ref, bf16[1024,1024]{1,0:T(8,128)(2,1)} %collective-permute-done.22.h1_ref, bf16[1024,1024]{1,0:T(8,128)(2,1)} %collective-permute-done.23.h2_ref, ...), custom_call_target="tpu_custom_call" | custom-call | flops 8589934592 | bytes 20971520 | tf_op jit(solution)/shard_map/dout/pallas_call | solution.py:571
  591.9 67.2 %attn_bwd.3 = (bf16[1024,512]{1,0:T(8,128)(2,1)}, bf16[1024,512]{1,0:T(8,128)(2,1)}, bf16[1024,512]{1,0:T(8,128)(2,1)}, bf16[1024,512]{1,0:T(8,128)(2,1)}) custom-call(s32[1]{0:T(128)} %bitcast.sp_ref, bf16[4096,256]{1,0:T(8,128)(2,1)} %get-tuple-element.84.q_ref, bf16[4096,128]{1,0:T(8,128)(2,1)} %get-tuple-element.85.k_ref, ...), custom_call_target="tpu_custom_call" | custom-call | flops 60000002048 | bytes 16777216 | tf_op jit(solution)/shard_map/attn_bwd/pallas_call | solution.py:384
  670.9 66.9 %attn_bwd.2 = (bf16[1024,512]{1,0:T(8,128)(2,1)}, bf16[1024,512]{1,0:T(8,128)(2,1)}, bf16[1024,512]{1,0:T(8,128)(2,1)}, bf16[1024,512]{1,0:T(8,128)(2,1)}) custom-call(s32[1]{0:T(128)} %bitcast.sp_ref, bf16[4096,256]{1,0:T(8,128)(2,1)} %get-tuple-element.88.q_ref, bf16[4096,128]{1,0:T(8,128)(2,1)} %get-tuple-element.89.k_ref, ...), custom_call_target="tpu_custom_call" | custom-call | flops 60000002048 | bytes 16777216 | tf_op jit(solution)/shard_map/attn_bwd/pallas_call | solution.py:384
  756.0 17.6 %collective-permute-done.32 = f32[512,512]{1,0:T(8,128)} collective-permute-done((f32[512,512]{1,0:T(8,128)}, f32[512,512]{1,0:T(8,128)}, u32[]{:S(2)}, u32[]{:S(2)}) %collective-permute-start.32) | collective-permute-done | bytes 1048608 | tf_op jit(solution)/shard_map/ppermute | solution.py:646
  786.9 12.6 %collective-permute-done.30.refs_3_ = bf16[1024,512]{1,0:T(8,128)(2,1)} collective-permute-done((bf16[1024,512]{1,0:T(8,128)(2,1)}, bf16[1024,512]{1,0:T(8,128)(2,1)}, u32[]{:S(2)}, u32[]{:S(2)}) %collective-permute-start.30) | collective-permute-done | bytes 1048608 | tf_op jit(solution)/shard_map/ppermute | solution.py:642
  813.2 32.2 %collective-permute-done.26.refs_2_ = bf16[1024,512]{1,0:T(8,128)(2,1)} collective-permute-done((bf16[1024,512]{1,0:T(8,128)(2,1)}, bf16[1024,512]{1,0:T(8,128)(2,1)}, u32[]{:S(2)}, u32[]{:S(2)}) %collective-permute-start.26) | collective-permute-done | bytes 1048608 | tf_op jit(solution)/shard_map/ppermute | solution.py:642
  845.4 21.5 %collective-permute-done.27.refs_3_ = bf16[1024,512]{1,0:T(8,128)(2,1)} collective-permute-done((bf16[1024,512]{1,0:T(8,128)(2,1)}, bf16[1024,512]{1,0:T(8,128)(2,1)}, u32[]{:S(2)}, u32[]{:S(2)}) %collective-permute-start.27) | collective-permute-done | bytes 1048608 | tf_op jit(solution)/shard_map/ppermute | solution.py:642
  866.9 11.6 %dx.1 = (bf16[1024,1024]{1,0:T(8,128)(2,1)}, f32[1,1024]{1,0:T(1,128)}) custom-call(s32[1]{0:T(128)} %bitcast.sp_ref, bf16[1024,512]{1,0:T(8,128)(2,1)} %get-tuple-element.107.refs_0_, bf16[1024,512]{1,0:T(8,128)(2,1)} %collective-permute-done.25.refs_1_, bf16[1024,512]{1,0:T(8,128)(2,1)} %collective-permute-done.26.refs_2_, ...), custom_call_target="tpu_custom_call" | custom-call | flops 4294967296 | bytes 16777216 | tf_op jit(solution)/shard_map/dx/pallas_call | solution.py:614
  (160 shorter events, 181.6 us)
Async XLA Ops:
  7.2 50.0 %collective-permute-start = (bf16[1024,1024]{1,0:T(8,128)(2,1)}, bf16[1024,1024]{1,0:T(8,128)(2,1)S(1)}, u32[]{:S(2)}, u32[]{:S(2)}) collective-permute-start(bf16[1024,1024]{1,0:T(8,128)(2,1)} %bitcast.65), channel_id=1, source_target_pairs={{0,2},{1,3},{2,0},{3,1},{4,6},{5,7},{6,4},{7,5}} | collective-permute-start | bytes 6291464 | tf_op jit(solution)/shard_map/ppermute | solution.py:642
  14.4 58.5 %all-to-all-start = ((bf16[4,144,1024]{2,1,0:T(8,128)(2,1)}), bf16[4,144,1024]{2,1,0:T(8,128)(2,1)S(1)}, u32[]{:S(2)}, u32[]{:S(2)}) async-start(bf16[4,144,1024]{2,1,0:T(8,128)(2,1)} %bitcast.70), calls=%async_computation | async-start | bytes 2359296 | tf_op jit(solution)/shard_map/all_to_all | solution.py:634
  17.9 301.8 %all-gather.3.cloned.1.call-start = ((), (), s32[]{:S(2)}) async-start(), calls=%async_computation.6 | async-start | bytes 4718592 | tf_op jit(solution)/shard_map/all_gather | solution.py:630
  18.0 99.0 %collective-permute-start.6 = (bf16[1024,1024]{1,0:T(8,128)(2,1)}, bf16[1024,1024]{1,0:T(8,128)(2,1)}, u32[]{:S(2)}, u32[]{:S(2)}) collective-permute-start(bf16[1024,1024]{1,0:T(8,128)(2,1)} %bitcast.66), channel_id=1, source_target_pairs={{0,1},{1,0},{2,3},{3,2},{4,5},{5,4},{6,7},{7,6}} | collective-permute-start | bytes 6291464 | tf_op jit(solution)/shard_map/ppermute | solution.py:642
  57.2 70.1 %collective-permute-start.1 = (bf16[1024,1024]{1,0:T(8,128)(2,1)S(1)}, bf16[1024,1024]{1,0:T(8,128)(2,1)}, u32[]{:S(2)}, u32[]{:S(2)}) collective-permute-start(bf16[1024,1024]{1,0:T(8,128)(2,1)S(1)} %collective-permute-done.xa_ref), channel_id=1, source_target_pairs={{0,1},{1,0},{2,3},{3,2},{4,5},{5,4},{6,7},{7,6}} | collective-permute-start | bytes 6291464 | tf_op jit(solution)/shard_map/ppermute | solution.py:642
  184.0 50.1 %all-to-all-start.2 = ((bf16[4,1024,256]{2,1,0:T(8,128)(2,1)}), bf16[4,1024,256]{2,1,0:T(8,128)(2,1)S(1)}, u32[]{:S(2)}, u32[]{:S(2)}) async-start(bf16[4,1024,256]{2,1,0:T(8,128)(2,1)} %get-tuple-element.91.o1_ref), calls=%async_computation.2 | async-start | bytes 4194304 | tf_op jit(solution)/shard_map/all_to_all | solution.py:634
  235.4 84.3 %all-to-all-start.1 = ((bf16[4,1024,256]{2,1,0:T(8,128)(2,1)}), bf16[4,1024,256]{2,1,0:T(8,128)(2,1)}, u32[]{:S(2)}, u32[]{:S(2)}) async-start(bf16[4,1024,256]{2,1,0:T(8,128)(2,1)} %get-tuple-element.87.o0_ref), calls=%async_computation.1 | async-start | bytes 4194304 | tf_op jit(solution)/shard_map/all_to_all | solution.py:634
  239.9 540.2 %reduce-scatter.2.cloned.1.call-start = ((), (), s32[]{:S(2)}) async-start(), calls=%async_computation.8 | async-start | bytes 15728640 | tf_op jit(solution)/shard_map/reduce_scatter | solution.py:664
  247.6 52.7 %collective-permute-start.9 = (bf16[256,1536]{1,0:T(8,128)(2,1)}, bf16[256,1536]{1,0:T(8,128)(2,1)}, u32[]{:S(2)}, u32[]{:S(2)}) collective-permute-start(bf16[256,1536]{1,0:T(8,128)(2,1)} %get-tuple-element.99.refs_0_), channel_id=1, source_target_pairs={{0,2},{1,3},{2,0},{3,1},{4,6},{5,7},{6,4},{7,5}} | collective-permute-start | bytes 2359304 | tf_op jit(solution)/shard_map/ppermute | solution.py:642
  248.4 68.7 %collective-permute-start.12 = (bf16[256,1536]{1,0:T(8,128)(2,1)}, bf16[256,1536]{1,0:T(8,128)(2,1)}, u32[]{:S(2)}, u32[]{:S(2)}) collective-permute-start(bf16[256,1536]{1,0:T(8,128)(2,1)} %get-tuple-element.100.refs_4_), channel_id=1, source_target_pairs={{0,2},{1,3},{2,0},{3,1},{4,6},{5,7},{6,4},{7,5}} | collective-permute-start | bytes 2359304 | tf_op jit(solution)/shard_map/ppermute | solution.py:642
  249.6 80.0 %collective-permute-start.10 = (bf16[256,1536]{1,0:T(8,128)(2,1)}, bf16[256,1536]{1,0:T(8,128)(2,1)}, u32[]{:S(2)}, u32[]{:S(2)}) collective-permute-start(bf16[256,1536]{1,0:T(8,128)(2,1)} %get-tuple-element.99.refs_0_), channel_id=1, source_target_pairs={{0,4},{4,0},{1,5},{5,1},{2,6},{6,2},{3,7},{7,3}} | collective-permute-start | bytes 2359304 | tf_op jit(solution)/shard_map/ppermute | solution.py:646
  261.0 68.6 %collective-permute-start.13 = (bf16[256,1536]{1,0:T(8,128)(2,1)}, bf16[256,1536]{1,0:T(8,128)(2,1)}, u32[]{:S(2)}, u32[]{:S(2)}) collective-permute-start(bf16[256,1536]{1,0:T(8,128)(2,1)} %get-tuple-element.100.refs_4_), channel_id=1, source_target_pairs={{0,4},{4,0},{1,5},{5,1},{2,6},{6,2},{3,7},{7,3}} | collective-permute-start | bytes 2359304 | tf_op jit(solution)/shard_map/ppermute | solution.py:646
  283.3 49.6 %collective-permute-start.17 = (bf16[384,1024]{1,0:T(8,128)(2,1)}, bf16[384,1024]{1,0:T(8,128)(2,1)S(1)}, u32[]{:S(2)}, u32[]{:S(2)}) collective-permute-start(bf16[384,1024]{1,0:T(8,128)(2,1)} %collective-permute-done.16.refs_10_), channel_id=1, source_target_pairs={{0,2},{1,3},{2,0},{3,1},{4,6},{5,7},{6,4},{7,5}} | collective-permute-start | bytes 2359304 | tf_op jit(solution)/shard_map/ppermute | solution.py:642
  411.0 393.0 %all-gather.5.cloned.1.call-start = ((), (), s32[]{:S(2)}) async-start(), calls=%async_computation.7 | async-start | bytes 9437184 | tf_op jit(solution)/shard_map/all_gather | solution.py:630
  432.3 93.6 %collective-permute-start.23 = (bf16[1024,1024]{1,0:T(8,128)(2,1)}, bf16[1024,1024]{1,0:T(8,128)(2,1)}, u32[]{:S(2)}, u32[]{:S(2)}) collective-permute-start(bf16[1024,1024]{1,0:T(8,128)(2,1)} %get-tuple-element.139.h0_ref), channel_id=1, source_target_pairs={{0,2},{1,3},{2,0},{3,1},{4,6},{5,7},{6,4},{7,5}} | collective-permute-start | bytes 6291464 | tf_op jit(solution)/shard_map/ppermute | solution.py:642
  447.4 121.3 %collective-permute-start.35 = (f32[2,384,1024]{2,1,0:T(8,128)}, f32[2,384,1024]{2,1,0:T(8,128)S(1)}, u32[]{:S(2)}, u32[]{:S(2)}) collective-permute-start(f32[2,384,1024]{2,1,0:T(8,128)} %get-tuple-element.136), channel_id=1, source_target_pairs={{0,4},{4,0},{1,5},{5,1},{2,6},{6,2},{3,7},{7,3}} | collective-permute-start | bytes 9437192 | tf_op jit(solution)/shard_map/ppermute | solution.py:646
  448.7 125.3 %collective-permute-start.22 = (bf16[1024,1024]{1,0:T(8,128)(2,1)}, bf16[1024,1024]{1,0:T(8,128)(2,1)}, u32[]{:S(2)}, u32[]{:S(2)}) collective-permute-start(bf16[1024,1024]{1,0:T(8,128)(2,1)} %get-tuple-element.139.h0_ref), channel_id=1, source_target_pairs={{0,1},{1,0},{2,3},{3,2},{4,5},{5,4},{6,7},{7,6}} | collective-permute-start | bytes 6291464 | tf_op jit(solution)/shard_map/ppermute | solution.py:642
  572.6 207.5 %collective-permute-start.36 = (f32[384,1024]{1,0:T(8,128)}, f32[384,1024]{1,0:T(8,128)}, u32[]{:S(2)}, u32[]{:S(2)}) collective-permute-start(f32[384,1024]{1,0:T(8,128)} %fusion.12), channel_id=1, source_target_pairs={{0,2},{1,3},{2,0},{3,1},{4,6},{5,7},{6,4},{7,5}} | collective-permute-start | bytes 4718600 | tf_op jit(solution)/shard_map/ppermute | solution.py:642
  670.8 82.0 %collective-permute-start.31 = (f32[512,512]{1,0:T(8,128)}, f32[512,512]{1,0:T(8,128)}, u32[]{:S(2)}, u32[]{:S(2)}) collective-permute-start(f32[512,512]{1,0:T(8,128)} %dynamic-slice_bitcast_fusion.2), channel_id=1, source_target_pairs={{0,4},{4,0},{1,5},{5,1},{2,6},{6,2},{3,7},{7,3}} | collective-permute-start | bytes 3145736 | tf_op jit(solution)/shard_map/ppermute | solution.py:646
  776.5 106.0 %all-to-all-start.3 = ((f32[4,128,1024]{2,1,0:T(8,128)}), f32[4,128,1024]{2,1,0:T(8,128)S(1)}, u32[]{:S(2)}, u32[]{:S(2)}) async-start(f32[4,128,1024]{2,1,0:T(8,128)} %bitcast.53), calls=%async_computation.3 | async-start | bytes 4194304 | tf_op jit(solution)/shard_map/all_to_all | solution.py:634
  780.1 65.2 %collective-permute-start.26 = (bf16[1024,512]{1,0:T(8,128)(2,1)}, bf16[1024,512]{1,0:T(8,128)(2,1)}, u32[]{:S(2)}, u32[]{:S(2)}) collective-permute-start(bf16[1024,512]{1,0:T(8,128)(2,1)} %get-tuple-element.109.refs_2_), channel_id=1, source_target_pairs={{0,2},{1,3},{2,0},{3,1},{4,6},{5,7},{6,4},{7,5}} | collective-permute-start | bytes 3145736 | tf_op jit(solution)/shard_map/ppermute | solution.py:642
  782.1 84.8 %collective-permute-start.27 = (bf16[1024,512]{1,0:T(8,128)(2,1)}, bf16[1024,512]{1,0:T(8,128)(2,1)}, u32[]{:S(2)}, u32[]{:S(2)}) collective-permute-start(bf16[1024,512]{1,0:T(8,128)(2,1)} %get-tuple-element.110.refs_3_), channel_id=1, source_target_pairs={{0,3},{1,2},{2,1},{3,0},{4,7},{5,6},{6,5},{7,4}} | collective-permute-start | bytes 3145736 | tf_op jit(solution)/shard_map/ppermute | solution.py:642
  785.2 94.6 %collective-permute-start.33 = (f32[256,1024]{1,0:T(8,128)}, f32[256,1024]{1,0:T(8,128)}, u32[]{:S(2)}, u32[]{:S(2)}) collective-permute-start(f32[256,1024]{1,0:T(8,128)} %dynamic-slice_bitcast_fusion), channel_id=1, source_target_pairs={{0,4},{4,0},{1,5},{5,1},{2,6},{6,2},{3,7},{7,3}} | collective-permute-start | bytes 3145736 | tf_op jit(solution)/shard_map/ppermute | solution.py:646
  799.5 90.3 %collective-permute-start.34 = (f32[128,3072]{1,0:T(8,128)}, f32[128,3072]{1,0:T(8,128)}, u32[]{:S(2)}, u32[]{:S(2)}) collective-permute-start(f32[128,3072]{1,0:T(8,128)} %constant_dynamic-slice_fusion), channel_id=1, source_target_pairs={{0,1},{1,0},{2,3},{3,2},{4,5},{5,4},{6,7},{7,6}} | collective-permute-start | bytes 4718600 | tf_op jit(solution)/shard_map/ppermute | solution.py:642
  (44 other events, 765.8 us)
Sparse Core Ops, SparseCore 0:
  59.6 45.3 all-gather.2
  411.2 176.5 reduce-scatter.1
  590.1 59.3 all-gather.4
